TPU v7x, 32 devices: a whole 2x2x4 slice. The times are simulated.
32 devices in a mesh: section: 4 (over y, x), tp: 8 (over z, core).
Axes of the slice: x: 2, y: 2, z: 4, core: 2. Of those that a mesh axis runs over, the one named last changes fastest.
Arguments:
- awaiting_arrivals: bfloat16 [4, 8, 25, 1920], P('section', 'tp'), may hold values from -6 to 6
- label_numbers: int32 [5, 8], replicated, may hold values from 0 to 1000
- drawn_coarse_codes: int32 [1, 8, 30], replicated, may hold values from 0 to 4095
- discrete_prototypes: float32 [4096, 32], replicated, may hold values from -6 to 6
- code_raising_operator: bfloat16 [32, 1920], replicated, may hold values from -1 to 1
- placement_tier_features: bfloat16 [25, 1920], replicated, may hold values from -3 to 3
- label_feature_rows: bfloat16 [1001, 1920], P(None, 'tp'), may hold values from -6 to 6
- conditioned_gain_mapping: bfloat16 [4, 1920, 3, 1920], P('section', None, None, 'tp'), may hold values from -0.125 to 0.125
- conditioned_shift_addend: float32 [4, 3, 1920], P('section', None, 'tp'), may hold values from -3 to 3
- question_answer_operator: bfloat16 [4, 1920, 3, 1920], P('section', None, None, 'tp'), may hold values from -0.125 to 0.125
- mixing_return_operator: bfloat16 [4, 1920, 1920], P('section', None, 'tp'), may hold values from -0.125 to 0.125
- focus_sharpness_exponents: float32 [4, 30], P('section'), may hold values from 1 to 5.5
- prior_resolution_probes: bfloat16 [4, 2, 8, 30, 1920], P('section', None, 'tp'), may hold values from -0.75 to 0.75
- prior_resolution_answers: bfloat16 [4, 2, 8, 30, 1920], P('section', None, 'tp'), may hold values from -6 to 6
Outputs:
- section_out: bfloat16 [4, 2, 8, 25, 1920], P('section', None, 'tp')
Inputs may be any that keep to these rules, and one draw needn't show every extreme that they name: `drawn_coarse_codes`: codebook indices of the maps of sides 1 to 4 of each image, one map after another, each row by row. `label_numbers`: class of each image; row r belongs to the micro-batch r - 4.
All inputs are finite; a program needn't handle non-finite values.
Results may differ from a plain program's by a relative error of at most 0.0151.
Values may be sent and summed in bfloat16 or wider, within the bound.
No kernel may reach another device: no remote copies, remote signals or barrier semaphores. Data moves between devices by JAX's collectives and lax.ppermute only.
A program may use at most 128 MiB of HBM per device.

v0:
```python
import jax
import jax.numpy as jnp
from jax import lax
from jax.sharding import PartitionSpec as P

FOCUS_GROUPS = 30
HEAD_DIM = 64
SIDE = 5


LOG_CAP = 4.605170185988092


def shifted(value, axis, steps):
    count = lax.axis_size(axis)
    first, last = (max(0, -steps), min(count, count - steps))
    return lax.ppermute(value, axis, [(source, source + steps) for source in range(first, last)])


def crossing_matrix(target, coarse):
    fine_index = jnp.arange(target, dtype=jnp.float32)
    coarse_index = jnp.arange(coarse, dtype=jnp.float32)
    begins = jnp.maximum(fine_index[:, None] / target, coarse_index[None, :] / coarse)
    finish = jnp.minimum(
        (fine_index[:, None] + 1.0) / target, (coarse_index[None, :] + 1.0) / coarse
    )
    return jnp.maximum(finish - begins, 0.0) * target


def resampler():
    blocks = []
    for coarse in range(1, SIDE):
        crossing = crossing_matrix(SIDE, coarse)
        blocks.append(
            (crossing[:, None, :, None] * crossing[None, :, None, :]).reshape(
                SIDE * SIDE, coarse * coarse
            )
        )
    return jnp.concatenate(blocks, axis=1)


def embed(
    drawn_coarse_codes,
    discrete_prototypes,
    code_raising_operator,
    placement_tier_features,
    resample_table,
):
    looked_up = discrete_prototypes[drawn_coarse_codes]
    mapped = jnp.einsum(
        "tc,nicv->nitv", resample_table, looked_up, precision=lax.Precision.HIGHEST
    ).astype(jnp.bfloat16)
    leading = mapped.shape[:3]
    projected_rows = jnp.dot(
        mapped.reshape(-1, mapped.shape[3]),
        code_raising_operator,
        preferred_element_type=jnp.float32,
    )
    projected_rows = projected_rows.reshape(leading + (code_raising_operator.shape[1],))
    return (projected_rows + placement_tier_features.astype(jnp.float32)).astype(jnp.bfloat16)


def norm_mod(latent_stream, scale_term, offset_term):
    widened = latent_stream.astype(jnp.float32)
    average = jnp.mean(widened, axis=-1, keepdims=True)
    centred = widened - average
    spread = jnp.mean(centred * centred, axis=-1, keepdims=True)
    normed = (
        centred * lax.rsqrt(spread + 1e-06) * (1.0 + scale_term[:, None, :])
        + offset_term[:, None, :]
    )
    return normed.astype(jnp.bfloat16)


def attention(qkv_cols, log_scale, cached_keys, cached_values):
    qkv = lax.all_to_all(qkv_cols, "tp", split_axis=0, concat_axis=3, tiled=True)
    images = qkv.shape[0]
    count = qkv.shape[1]
    widened = qkv.astype(jnp.float32)
    query = widened[:, :, 0].reshape(images, count, FOCUS_GROUPS, HEAD_DIM)
    new_keys = widened[:, :, 1].reshape(images, count, FOCUS_GROUPS, HEAD_DIM)
    new_values = qkv[:, :, 2].reshape(images, count, FOCUS_GROUPS, HEAD_DIM)
    head_mult = jnp.exp(jnp.minimum(log_scale, LOG_CAP))
    query = (
        query
        * lax.rsqrt(jnp.sum(query * query, axis=-1, keepdims=True) + 1e-06)
        * head_mult[:, None]
    )
    new_keys = new_keys * lax.rsqrt(jnp.sum(new_keys * new_keys, axis=-1, keepdims=True) + 1e-06)
    all_keys = jnp.concatenate(
        [cached_keys.astype(jnp.float32).reshape(images, -1, FOCUS_GROUPS, HEAD_DIM), new_keys],
        axis=1,
    )
    all_values = jnp.concatenate(
        [cached_values.reshape(images, -1, FOCUS_GROUPS, HEAD_DIM), new_values], axis=1
    )
    scores = jnp.einsum("iqhd,ikhd->ihqk", query, all_keys, precision=lax.Precision.HIGHEST)
    maximum = jnp.max(scores, axis=-1, keepdims=True)
    weights = jnp.exp(scores - maximum)
    probabilities = (weights / jnp.sum(weights, axis=-1, keepdims=True)).astype(jnp.bfloat16)
    mixed = jnp.einsum(
        "ihqk,ikhd->iqhd", probabilities, all_values, preferred_element_type=jnp.float32
    )
    return mixed.reshape(images, count, FOCUS_GROUPS * HEAD_DIM).astype(jnp.bfloat16)


def project_out(attended, out_matrix):
    return jnp.dot(
        lax.all_gather(attended, "tp", axis=0, tiled=True),
        out_matrix,
        preferred_element_type=jnp.float32,
    )


def pass_on(latent_stream):
    return shifted(latent_stream, "section", 1)


def local(
    awaiting_arrivals,
    label_numbers,
    drawn_coarse_codes,
    discrete_prototypes,
    code_raising_operator,
    placement_tier_features,
    label_feature_rows,
    conditioned_gain_mapping,
    conditioned_shift_addend,
    question_answer_operator,
    mixing_return_operator,
    focus_sharpness_exponents,
    prior_resolution_probes,
    prior_resolution_answers,
):
    sections = lax.axis_size("section")
    section_at = lax.axis_index("section")
    group_index = lax.axis_index("tp")
    moments = prior_resolution_probes.shape[1]
    width = question_answer_operator.shape[1]
    column_width = question_answer_operator.shape[3]
    images = drawn_coarse_codes.shape[1]
    resident_pictures = awaiting_arrivals.shape[1]
    class_rows = lax.dynamic_slice_in_dim(label_numbers, sections - 1 - section_at, moments, 0)
    class_part = jnp.take(label_feature_rows, class_rows, axis=0)
    activated_part = jax.nn.silu(class_part.astype(jnp.float32)).astype(jnp.bfloat16)
    gated_response = lax.all_gather(activated_part, "tp", axis=2, tiled=True)
    flat_active = gated_response.reshape(moments * images, width)
    inner_block = 0
    local_mod = conditioned_gain_mapping[inner_block].reshape(width, 3 * column_width)
    modulated = jnp.dot(flat_active, local_mod, preferred_element_type=jnp.float32)
    mod_list = [
        modulated.reshape(moments, images, 3, column_width) + conditioned_shift_addend[inner_block]
    ]
    mod_cols = jnp.stack(mod_list)
    resample_table = resampler()
    emitted = []
    mod_rows = lax.all_to_all(mod_cols, "tp", split_axis=2, concat_axis=4, tiled=True)
    own_tokens = lax.dynamic_slice_in_dim(
        drawn_coarse_codes, group_index * resident_pictures, resident_pictures, 1
    )
    entering = embed(
        own_tokens,
        discrete_prototypes,
        code_raising_operator,
        placement_tier_features,
        resample_table,
    )
    passed_along_activation = awaiting_arrivals[0]
    for clock_tick in range(moments):
        latent_stream = passed_along_activation
        inner_block = 0
        modulation = mod_rows[inner_block, clock_tick]
        normed = norm_mod(latent_stream, modulation[:, 1], modulation[:, 2])
        local_qkv = question_answer_operator[inner_block].reshape(width, 3 * column_width)

        def body_product(portion, offset, local_qkv=local_qkv):
            return jnp.dot(portion, local_qkv, preferred_element_type=jnp.float32).astype(
                jnp.bfloat16
            )

        qkv_cols = body_product(lax.all_gather(normed, "tp", axis=0, tiled=True), jnp.int32(0))
        qkv_cols = qkv_cols.reshape(qkv_cols.shape[0], qkv_cols.shape[1], 3, column_width)
        attended = attention(
            qkv_cols,
            focus_sharpness_exponents[inner_block],
            prior_resolution_probes[inner_block, clock_tick],
            prior_resolution_answers[inner_block, clock_tick],
        )
        projected_cols = project_out(attended, mixing_return_operator[inner_block]).astype(
            jnp.bfloat16
        )
        projected = lax.all_to_all(projected_cols, "tp", split_axis=0, concat_axis=2, tiled=True)
        latent_stream = (
            latent_stream.astype(jnp.float32)
            + modulation[:, 0][:, None, :] * projected.astype(jnp.float32)
        ).astype(jnp.bfloat16)
        emitted.append(latent_stream)
        if clock_tick + 1 < moments:
            arrived = pass_on(latent_stream)
            passed_along_activation = jnp.where(section_at == 0, entering[clock_tick], arrived)
    result = jnp.stack(emitted)
    return result[None]


def solution(mesh):
    in_specs = (
        P("section", "tp", None, None),
        P(),
        P(),
        P(),
        P(),
        P(),
        P(None, "tp"),
        P("section", None, None, "tp"),
        P("section", None, "tp"),
        P("section", None, None, "tp"),
        P("section", None, "tp"),
        P("section", None),
        P("section", None, "tp", None, None),
        P("section", None, "tp", None, None),
    )
    out_specs = P("section", None, "tp", None, None)
    return jax.shard_map(local, mesh=mesh, in_specs=in_specs, out_specs=out_specs, check_vma=False)
```

profile of v0, /device:TPU:4, one launch (start us, length us, event | category | flops | bytes accessed | tf_op | source)
XLA Modules:
  0.0 244.2 jit_solution(13599707762112273153)
XLA Ops:
  0.9 1.2 copy.162
  3.0 16.4 %all_gather.15 = bf16[2,8,1920]{1,0,2:T(2,128)(2,1)S(1)} all-gather(bf16[2,8,240]{1,0,2:T(2,128)(2,1)S(1)} %copy.163), channel_id=1, replica_groups=mesh['section'=4,'tp'=8] {'tp'}, dimensions={2}, use_global_device_ids=true | all-gather | bytes 69120 | tf_op jit(solution)/shard_map/all_gather | solution.py:146
  20.1 2.9 %fusion.17 = f32[1,2,8,3,240]{4,2,3,1,0:T(8,128)S(1)} fusion(bf16[1,1920,3,240]{1,3,2,0:T(8,128)(2,1)} %param.21, bf16[2,8,1920,1]{1,0,2,3:T(2,128)(2,1)S(1)} %bitcast.178, f32[3,240]{1,0:T(4,128)S(1)} %bitcast.180), kind=kOutput, calls=%fused_computation.24 | convolution fusion | flops 44248320 | bytes 2875200 | tf_op jit(solution)/shard_map/dot_general | solution.py:150
  23.7 5.1 %all-to-all-start = ((f32[1,2,8,3,240]{4,1,3,0,2:T(2,128)}), f32[1,2,8,3,240]{4,1,3,0,2:T(2,128)S(1)}, u32[]{:S(2)}, u32[]{:S(2)}) async-start(f32[1,2,8,3,240]{4,1,3,0,2:T(2,128)} %copy.165), calls=%async_computation | async-start | bytes 98304 | tf_op jit(solution)/shard_map/all_to_all | solution.py:157
  29.2 1.5 convert_reduce_fusion.1
  32.4 2.8 %slice_reduce_fusion = (bf16[30,1920]{1,0:T(8,128)(2,1)}, bf16[30,1920]{1,0:T(8,128)(2,1)}) fusion(bf16[1,2,1,30,1920]{4,1,3,2,0:T(2,128)(2,1)} %param.27), kind=kLoop, calls=%fused_computation.77 | loop fusion | bytes 460800 | tf_op jit(solution)/shard_map/slice | solution.py:187
  36.7 17.0 %all_gather.16 = bf16[8,25,1920]{2,1,0:T(8,128)(2,1)S(1)} all-gather(bf16[1,25,1920]{2,1,0:T(8,128)(2,1)S(1)} %fusion.43), channel_id=1, replica_groups=mesh['section'=4,'tp'=8] {'tp'}, dimensions={0}, use_global_device_ids=true | all-gather | bytes 864000 | tf_op jit(solution)/shard_map/all_gather | solution.py:181
  53.6 1.8 convolution_convert_fusion.1
  55.4 1.7 reshape.1148
  58.0 5.2 %all-to-all-start.1 = ((bf16[8,25,3,240]{3,1,2,0:T(8,128)(2,1)}), bf16[8,25,3,240]{3,1,2,0:T(8,128)(2,1)}, u32[]{:S(2)}, u32[]{:S(2)}) async-start(bf16[8,25,3,240]{3,1,2,0:T(8,128)(2,1)} %copy.169), calls=%async_computation.1 | async-start | bytes 786432 | tf_op jit(solution)/shard_map/all_to_all | solution.py:76
  67.0 3.0 %copy.180 = f32[4096,32]{1,0:T(8,128)} copy(f32[4096,32]{0,1:T(8,128)} %param.17) | data formatting | bytes 1048576 | tf_op args[3]
  73.9 2.8 %gather_fusion.1 = f32[30,32]{1,0:T(8,128)} fusion(f32[4096,32]{1,0:T(8,128)} %copy.180, s32[1024]{0:T(1024)S(1)} %pad_clamp_fusion), kind=kCustom, calls=%fused_computation.1 | custom fusion | bytes 7800 | tf_op jit(solution)/shard_map/gather | solution.py:49
  82.2 1.4 copy.173
  83.6 1.8 copy_multiply_fusion.1
  86.5 1.7 slice_multiply_fusion.1
  88.1 1.9 mul.390
  91.4 2.8 %fusion.24 = f32[30,25,55]{2,1,0:T(8,128)S(1)} fusion(f32[1,25,30,64]{3,1,2,0:T(8,128)} %copy_multiply_fusion.1, f32[1,30,30,64]{3,1,2,0:T(8,128)} %copy.175, f32[25,30,64]{2,1,0:T(8,128)S(1)} %multiply_multiply_fusion.1), kind=kOutput, calls=%fused_computation.31 | convolution fusion | flops 31785600 | bytes 779400 | tf_op jit(solution)/shard_map/iqhd,ikhd->ihqk/dot_general | solution.py:97
  95.5 1.7 copy.172
  97.2 3.5 %fusion.12 = bf16[1,25,30,64]{3,1,2,0:T(8,128)(2,1)} fusion(bf16[1,25,30,64]{3,1,2,0:T(8,128)(2,1)} %copy.172, bf16[1,30,30,64]{3,1,2,0:T(8,128)(2,1)} %copy.171, f32[30,25]{1,0:T(8,128)S(1)} %fusion.73, f32[30,25,55]{2,1,0:T(8,128)S(1)} %fusion.24), kind=kOutput, calls=%fused_computation.19 | convolution fusion | flops 5874954 | bytes 475200 | tf_op jit(solution)/shard_map/ihqk,ikhd->iqhd/dot_general | solution.py:101
  102.0 17.0 %all_gather.17 = bf16[8,25,1920]{2,1,0:T(8,128)(2,1)S(1)} all-gather(bf16[1,25,1920]{2,1,0:T(8,128)(2,1)S(1)} %convert_element_type.264), channel_id=1, replica_groups=mesh['section'=4,'tp'=8] {'tp'}, dimensions={0}, use_global_device_ids=true | all-gather | bytes 864000 | tf_op jit(solution)/shard_map/all_gather | solution.py:109
  119.0 2.3 convolution_convert_fusion.5
  121.2 5.2 %all-to-all-start.2 = ((bf16[8,25,240]{2,1,0:T(8,128)(2,1)}), bf16[8,25,240]{2,1,0:T(8,128)(2,1)S(1)}, u32[]{:S(2)}, u32[]{:S(2)}) async-start(bf16[8,25,240]{2,1,0:T(8,128)(2,1)} %convolution_convert_fusion.5), calls=%async_computation.2 | async-start | bytes 262144 | tf_op jit(solution)/shard_map/all_to_all | solution.py:192
  126.7 6.5 %all-to-all-done.2 = bf16[8,25,240]{2,1,0:T(8,128)(2,1)S(1)} async-done(((bf16[8,25,240]{2,1,0:T(8,128)(2,1)}), bf16[8,25,240]{2,1,0:T(8,128)(2,1)S(1)}, u32[]{:S(2)}, u32[]{:S(2)}) %all-to-all-start.2) | async-done | bytes 96032 | tf_op jit(solution)/shard_map/all_to_all | solution.py:192
  133.6 3.4 %collective-permute-start = (bf16[1,25,1920]{2,1,0:T(8,128)(2,1)S(1)}, bf16[1,25,1920]{2,1,0:T(8,128)(2,1)S(1)}, u32[]{:S(2)}, u32[]{:S(2)}) collective-permute-start(bf16[1,25,1920]{2,1,0:T(8,128)(2,1)S(1)} %fusion.44), channel_id=1, source_target_pairs={{0,8},{8,16},{16,24},{1,9},{9,17},{17,25},{2,10},{10,18},{18,26},{... | collective-permute-start | bytes 288008 | tf_op jit(solution)/shard_map/ppermute | solution.py:17
  137.6 3.6 %collective-permute-done = bf16[1,25,1920]{2,1,0:T(8,128)(2,1)S(1)} collective-permute-done((bf16[1,25,1920]{2,1,0:T(8,128)(2,1)S(1)}, bf16[1,25,1920]{2,1,0:T(8,128)(2,1)S(1)}, u32[]{:S(2)}, u32[]{:S(2)}) %collective-permute-start) | collective-permute-done | bytes 96032 | tf_op jit(solution)/shard_map/ppermute | solution.py:17
  141.2 1.3 fusion.74
  142.9 16.3 %all_gather.18 = bf16[8,25,1920]{2,1,0:T(8,128)(2,1)S(1)} all-gather(bf16[1,25,1920]{2,1,0:T(8,128)(2,1)S(1)} %add_convert_fusion.1), channel_id=1, replica_groups=mesh['section'=4,'tp'=8] {'tp'}, dimensions={0}, use_global_device_ids=true | all-gather | bytes 864000 | tf_op jit(solution)/shard_map/all_gather | solution.py:181
  159.2 1.8 convolution_convert_fusion
  161.0 2.4 reshape.1151
  163.4 1.8 copy.187
  165.2 4.3 %all-to-all-start.3 = ((bf16[8,25,3,240]{3,1,2,0:T(8,128)(2,1)}), bf16[8,25,3,240]{3,1,2,0:T(8,128)(2,1)}, u32[]{:S(2)}, u32[]{:S(2)}) async-start(bf16[8,25,3,240]{3,1,2,0:T(8,128)(2,1)} %copy.187), calls=%async_computation.3 | async-start | bytes 786432 | tf_op jit(solution)/shard_map/all_to_all | solution.py:76
  169.5 2.0 reshape.1119
  171.5 2.1 copy.193
  174.5 1.7 copy.189
  177.1 4.7 %all-to-all-done.3 = bf16[8,25,3,240]{3,1,2,0:T(8,128)(2,1)} async-done(((bf16[8,25,3,240]{3,1,2,0:T(8,128)(2,1)}), bf16[8,25,3,240]{3,1,2,0:T(8,128)(2,1)}, u32[]{:S(2)}, u32[]{:S(2)}) %all-to-all-start.3) | async-done | bytes 288032 | tf_op jit(solution)/shard_map/all_to_all | solution.py:76
  181.8 1.9 copy.188
  183.7 1.4 all_to_all.65
  186.8 1.9 mul.431
  189.9 1.9 reshape_squeeze.39
  191.8 1.9 reshape_squeeze.40
  196.4 1.3 copy_multiply_fusion
  198.8 2.7 %fusion.27 = f32[30,25,55]{2,1,0:T(8,128)S(1)} fusion(f32[1,25,30,64]{3,1,2,0:T(8,128)S(1)} %copy_multiply_fusion, f32[1,30,30,64]{3,1,2,0:T(8,128)} %copy.193, f32[25,30,64]{2,1,0:T(8,128)S(1)} %multiply_multiply_fusion), kind=kOutput, calls=%fused_computation.35 | convolution fusion | flops 31785600 | bytes 779400 | tf_op jit(solution)/shard_map/iqhd,ikhd->ihqk/dot_general | solution.py:97
  203.6 3.8 %fusion.13 = bf16[1,25,30,64]{3,1,2,0:T(8,128)(2,1)} fusion(bf16[1,25,30,64]{3,1,2,0:T(8,128)(2,1)} %copy.190, bf16[1,30,30,64]{3,1,2,0:T(8,128)(2,1)} %copy.189, f32[30,25]{1,0:T(8,128)S(1)} %fusion.75, f32[30,25,55]{2,1,0:T(8,128)} %copy-done.5), kind=kOutput, calls=%fused_computation.20 | convolution fusion | flops 5874954 | bytes 475200 | tf_op jit(solution)/shard_map/ihqk,ikhd->iqhd/dot_general | solution.py:101
  207.4 1.7 copy.195
  210.3 16.2 %all_gather.19 = bf16[8,25,1920]{2,1,0:T(8,128)(2,1)S(1)} all-gather(bf16[1,25,1920]{2,1,0:T(8,128)(2,1)S(1)} %convert_element_type.289), channel_id=1, replica_groups=mesh['section'=4,'tp'=8] {'tp'}, dimensions={0}, use_global_device_ids=true | all-gather | bytes 864000 | tf_op jit(solution)/shard_map/all_gather | solution.py:109
  226.5 2.3 convolution_convert_fusion.4
  228.8 4.0 %all-to-all-start.4 = ((bf16[8,25,240]{2,1,0:T(8,128)(2,1)}), bf16[8,25,240]{2,1,0:T(8,128)(2,1)}, u32[]{:S(2)}, u32[]{:S(2)}) async-start(bf16[8,25,240]{2,1,0:T(8,128)(2,1)} %convolution_convert_fusion.4), calls=%async_computation.4 | async-start | bytes 262144 | tf_op jit(solution)/shard_map/all_to_all | solution.py:192
  233.5 6.1 %all-to-all-done.4 = bf16[8,25,240]{2,1,0:T(8,128)(2,1)} async-done(((bf16[8,25,240]{2,1,0:T(8,128)(2,1)}), bf16[8,25,240]{2,1,0:T(8,128)(2,1)}, u32[]{:S(2)}, u32[]{:S(2)}) %all-to-all-start.4) | async-done | bytes 96032 | tf_op jit(solution)/shard_map/all_to_all | solution.py:192
  (142 shorter events, 44.2 us)
Async XLA Ops:
  0.0 53.6 %copy-start = (bf16[1,1920,3,240]{1,3,2,0:T(8,128)(2,1)S(1)}, bf16[1,1920,3,240]{1,3,2,0:T(8,128)(2,1)}, u32[]{:S(2)}) copy-start(bf16[1,1920,3,240]{1,3,2,0:T(8,128)(2,1)} %param.23) | copy-start | bytes 8294404
  2.2 26.7 %copy-start.3 = (bf16[1,1,25,1920]{3,2,1,0:T(8,128)(2,1)S(1)}, bf16[1,1,25,1920]{3,2,1,0:T(8,128)(2,1)}, u32[]{:S(2)}) copy-start(bf16[1,1,25,1920]{3,2,1,0:T(8,128)(2,1)} %param.14) | copy-start | bytes 288004
  2.8 26.5 %copy-start.7 = (bf16[1,2,1,30,1920]{4,1,3,2,0:T(2,128)(2,1)S(1)}, bf16[1,2,1,30,1920]{4,1,3,2,0:T(2,128)(2,1)}, u32[]{:S(2)}) copy-start(bf16[1,2,1,30,1920]{4,1,3,2,0:T(2,128)(2,1)} %param.26) | copy-start | bytes 691204
  23.7 11.5 %all-to-all-start = ((f32[1,2,8,3,240]{4,1,3,0,2:T(2,128)}), f32[1,2,8,3,240]{4,1,3,0,2:T(2,128)S(1)}, u32[]{:S(2)}, u32[]{:S(2)}) async-start(f32[1,2,8,3,240]{4,1,3,0,2:T(2,128)} %copy.165), calls=%async_computation | async-start | bytes 98304 | tf_op jit(solution)/shard_map/all_to_all | solution.py:157
  58.0 18.7 %all-to-all-start.1 = ((bf16[8,25,3,240]{3,1,2,0:T(8,128)(2,1)}), bf16[8,25,3,240]{3,1,2,0:T(8,128)(2,1)}, u32[]{:S(2)}, u32[]{:S(2)}) async-start(bf16[8,25,3,240]{3,1,2,0:T(8,128)(2,1)} %copy.169), calls=%async_computation.1 | async-start | bytes 786432 | tf_op jit(solution)/shard_map/all_to_all | solution.py:76
  64.0 6.7 %copy-start.9 = (f32[5,5,3,3]{1,0,3,2:T(8,128)S(1)}, f32[5,5,3,3]{1,0,3,2:T(8,128)}, u32[]{:S(2)}) copy-start(f32[5,5,3,3]{1,0,3,2:T(8,128)} %broadcast_multiply_fusion.1) | copy-start | bytes 2704
  64.0 7.5 %copy-start.12 = (f32[5,5,2,2]{1,0,3,2:T(8,128)S(1)}, f32[5,5,2,2]{1,0,3,2:T(8,128)}, u32[]{:S(2)}) copy-start(f32[5,5,2,2]{1,0,3,2:T(8,128)} %broadcast_multiply_fusion.2) | copy-start | bytes 1204
  64.0 8.3 %copy-start.19 = (f32[5]{0:T(128)S(1)}, f32[5]{0:T(128)}, u32[]{:S(2)}) copy-start(f32[5]{0:T(128)} %maximum_multiply_fusion.3) | copy-start | bytes 64
  64.0 12.7 %copy-start.20 = (f32[1,30]{1,0:T(1,128)S(1)}, f32[1,30]{1,0:T(1,128)}, u32[]{:S(2)}) copy-start(f32[1,30]{1,0:T(1,128)} %param.25) | copy-start | bytes 364
  78.4 9.8 %copy-start.1 = (bf16[1,25,3,1920]{3,1,2,0:T(8,128)(2,1)}, bf16[1,25,3,1920]{3,1,2,0:T(8,128)(2,1)S(1)}, u32[]{:S(2)}) copy-start(bf16[1,25,3,1920]{3,1,2,0:T(8,128)(2,1)S(1)} %all_to_all.60) | copy-start | bytes 864004
  90.0 4.6 %slice-start = ((bf16[1,25,3,1920]{3,1,2,0:T(8,128)(2,1)}), bf16[1,25,1,1920]{3,1,2,0:T(8,128)(2,1)S(1)}, s32[]{:S(2)}) async-start(bf16[1,25,3,1920]{3,1,2,0:T(8,128)(2,1)} %copy-done.1), calls=%async_computation.5 | async-start | bytes 245760 | tf_op jit(solution)/shard_map/slice | solution.py:82
  100.6 25.8 %copy-start.13 = (f32[30,32]{1,0:T(8,128)S(1)}, f32[30,32]{1,0:T(8,128)}, u32[]{:S(2)}) copy-start(f32[30,32]{1,0:T(8,128)} %gather_fusion.1) | copy-start | bytes 11524
  100.6 25.8 %copy-start.14 = (f32[25,9]{1,0:T(8,128)S(1)}, f32[25,9]{1,0:T(8,128)}, u32[]{:S(2)}) copy-start(f32[25,9]{1,0:T(8,128)} %copy.183) | copy-start | bytes 2704
  100.6 25.8 %copy-start.15 = (f32[25,4]{1,0:T(8,128)S(1)}, f32[25,4]{1,0:T(8,128)}, u32[]{:S(2)}) copy-start(f32[25,4]{1,0:T(8,128)} %copy.182) | copy-start | bytes 1204
  100.6 25.8 %copy-start.16 = (f32[25,1]{1,0:T(8,128)S(1)}, f32[25,1]{1,0:T(8,128)}, u32[]{:S(2)}) copy-start(f32[25,1]{1,0:T(8,128)} %copy.181) | copy-start | bytes 304
  100.6 25.8 %copy-start.17 = (f32[25,16]{1,0:T(8,128)S(1)}, f32[25,16]{1,0:T(8,128)}, u32[]{:S(2)}) copy-start(f32[25,16]{1,0:T(8,128)} %mul.419) | copy-start | bytes 4804
  100.7 32.9 %copy-start.4 = (bf16[1,1,25,1920]{3,2,1,0:T(8,128)(2,1)S(1)}, bf16[1,1,25,1920]{3,2,1,0:T(8,128)(2,1)}, u32[]{:S(2)}) copy-start(bf16[1,1,25,1920]{3,2,1,0:T(8,128)(2,1)} %param.14) | copy-start | bytes 288004
  100.7 32.9 %copy-start.11 = (f32[1920]{0:T(1024)S(1)}, f32[1920]{0:T(1024)}, u32[]{:S(2)}) copy-start(f32[1920]{0:T(1024)} %get-tuple-element.12) | copy-start | bytes 23044
  101.8 35.2 %copy-start.10 = (f32[1,3,1920]{2,0,1:T(1,128)S(1)}, f32[1,3,1920]{2,0,1:T(1,128)}, u32[]{:S(2)}) copy-start(f32[1,3,1920]{2,0,1:T(1,128)} %get-tuple-element.21) | copy-start | bytes 69124
  121.2 11.9 %all-to-all-start.2 = ((bf16[8,25,240]{2,1,0:T(8,128)(2,1)}), bf16[8,25,240]{2,1,0:T(8,128)(2,1)S(1)}, u32[]{:S(2)}, u32[]{:S(2)}) async-start(bf16[8,25,240]{2,1,0:T(8,128)(2,1)} %convolution_convert_fusion.5), calls=%async_computation.2 | async-start | bytes 262144 | tf_op jit(solution)/shard_map/all_to_all | solution.py:192
  133.6 7.7 %collective-permute-start = (bf16[1,25,1920]{2,1,0:T(8,128)(2,1)S(1)}, bf16[1,25,1920]{2,1,0:T(8,128)(2,1)S(1)}, u32[]{:S(2)}, u32[]{:S(2)}) collective-permute-start(bf16[1,25,1920]{2,1,0:T(8,128)(2,1)S(1)} %fusion.44), channel_id=1, source_target_pairs={{0,8},{8,16},{16,24},{1,9},{9,17},{17,25},{2,10},{10,18},{18,26},{... | collective-permute-start | bytes 288008 | tf_op jit(solution)/shard_map/ppermute | solution.py:17
  161.0 12.6 %copy-start.8 = (bf16[30,1920]{1,0:T(8,128)(2,1)S(1)}, bf16[30,1920]{1,0:T(8,128)(2,1)}, u32[]{:S(2)}) copy-start(bf16[30,1920]{1,0:T(8,128)(2,1)} %get-tuple-element.7) | copy-start | bytes 345604
  165.2 16.6 %all-to-all-start.3 = ((bf16[8,25,3,240]{3,1,2,0:T(8,128)(2,1)}), bf16[8,25,3,240]{3,1,2,0:T(8,128)(2,1)}, u32[]{:S(2)}, u32[]{:S(2)}) async-start(bf16[8,25,3,240]{3,1,2,0:T(8,128)(2,1)} %copy.187), calls=%async_computation.3 | async-start | bytes 786432 | tf_op jit(solution)/shard_map/all_to_all | solution.py:76
  185.2 9.7 %copy-start.2 = (bf16[1,25,3,1920]{3,1,2,0:T(8,128)(2,1)}, bf16[1,25,3,1920]{3,1,2,0:T(8,128)(2,1)S(1)}, u32[]{:S(2)}) copy-start(bf16[1,25,3,1920]{3,1,2,0:T(8,128)(2,1)S(1)} %all_to_all.65) | copy-start | bytes 864004
  195.5 7.1 %slice-start.1 = ((bf16[1,25,3,1920]{3,1,2,0:T(8,128)(2,1)}), bf16[1,25,1,1920]{3,1,2,0:T(8,128)(2,1)S(1)}, s32[]{:S(2)}) async-start(bf16[1,25,3,1920]{3,1,2,0:T(8,128)(2,1)} %copy-done.2), calls=%async_computation.6 | async-start | bytes 245760 | tf_op jit(solution)/shard_map/slice | solution.py:82
  201.5 0.8 copy-start.5
  207.4 25.4 %copy-start.6 = (f32[1,1,25,1920]{3,2,1,0:T(8,128)S(1)}, f32[1,1,25,1920]{3,2,1,0:T(8,128)}, u32[]{:S(2)}) copy-start(f32[1,1,25,1920]{3,2,1,0:T(8,128)} %reshape.1149) | copy-start | bytes 576004
  209.2 33.2 %copy-start.18 = (f32[1920]{0:T(1024)S(1)}, f32[1920]{0:T(1024)}, u32[]{:S(2)}) copy-start(f32[1920]{0:T(1024)} %get-tuple-element.9) | copy-start | bytes 23044
  228.8 10.8 %all-to-all-start.4 = ((bf16[8,25,240]{2,1,0:T(8,128)(2,1)}), bf16[8,25,240]{2,1,0:T(8,128)(2,1)}, u32[]{:S(2)}, u32[]{:S(2)}) async-start(bf16[8,25,240]{2,1,0:T(8,128)(2,1)} %convolution_convert_fusion.4), calls=%async_computation.4 | async-start | bytes 262144 | tf_op jit(solution)/shard_map/all_to_all | solution.py:192
where the time goes:
time: 246 us; the launch traced here: 244 us
  blocking collectives  82.9 us (34%)
  local copies, waits for them, and re-layouts  63.8 us (26%)
  starting transfers between devices  27.2 us (11%)
  matrix products  25.3 us (10%)
  other arithmetic  23.5 us (10%)
  waiting for transfers between devices  20.9 us (8%)
    all_gather x2, blocking collectives, local(): lax.all_gather(normed, 'tp', axis=0, tiled=True)  33.3 us
    all_gather x2, blocking collectives, project_out(): lax.all_gather(attended, 'tp', axis=0, tiled=True)  33.2 us
    all_gather x1, blocking collectives, local(): gated_response = lax.all_gather(activated_part, 'tp', axis=2, tiled=True)  16.4 us
    all_to_all x2, waiting for transfers between devices, local(): lax.all_to_all(projected_cols, 'tp', split_axis=0, concat_axis=2, tiled=T...  12.5 us
    all_to_all x2, starting transfers between devices, attention(): lax.all_to_all(qkv_cols, 'tp', split_axis=0, concat_axis=3, tiled=True)  9.52 us
    all_to_all x2, starting transfers between devices, local(): lax.all_to_all(projected_cols, 'tp', split_axis=0, concat_axis=2, tiled=T...  9.2 us
    dot_general x2, matrix products, attention(): jnp.einsum('ihqk,ikhd->iqhd', probabilities, all_values, preferred_elemen...  7.32 us
    reshape x4, local copies, waits for them, and re-layouts, local(): qkv_cols.reshape(qkv_cols.shape[0], qkv_cols.shape[1], 3, column_width)  6.8 us
  transfers between devices with their start and end apart: 6, of which 4 were waited for; matrix products, arithmetic and copies ran while one was open for 12% of the time, Pallas kernels for 0%

commit v1 on v0

--- a/solution.py
+++ b/solution.py
@@ -1,7 +1,10 @@
 import jax
 import jax.numpy as jnp
 from jax import lax
+from jax.experimental import pallas as pl
+from jax.experimental.pallas import tpu as pltpu
 from jax.sharding import PartitionSpec as P
+import numpy as np
 
 FOCUS_GROUPS = 30
 HEAD_DIM = 64
@@ -116,7 +119,7 @@
     return shifted(latent_stream, "section", 1)
 
 
-def local(
+def general(
     awaiting_arrivals,
     label_numbers,
     drawn_coarse_codes,
@@ -202,6 +205,577 @@
     return result[None]
 
 
+SLOT = 32
+F32 = jnp.float32
+BF16 = jnp.bfloat16
+KERNEL_VMEM = 16 * 1024 * 1024
+
+
+def first_head(pair, pair_width, head_dim):
+    return (2 * pair * pair_width + head_dim) // (2 * head_dim)
+
+
+class Plan:
+    def __init__(self, section, tp, args):
+        (arrivals, _, codes, prototypes, _, placement, labels, gain, _, _, _, sharp, probes, _) = args
+        self.section, self.tp = section, tp
+        self.pairs = tp // 2
+        self.width = gain.shape[1]
+        self.cols = gain.shape[3]
+        self.pair_cols = 2 * self.cols
+        self.heads = sharp.shape[1]
+        self.head_dim = self.width // self.heads
+        self.tokens = placement.shape[0]
+        self.ctx = probes.shape[3]
+        self.ticks = probes.shape[1]
+        self.images = codes.shape[1]
+        self.resident = arrivals.shape[1]
+        self.lanes = self.pairs * SLOT
+        self.classes = labels.shape[0]
+        self.vocab, self.code_dim = prototypes.shape
+        starts = [first_head(p, self.pair_cols, self.head_dim) for p in range(self.pairs + 1)]
+        self.starts = starts
+        self.counts = [starts[p + 1] - starts[p] for p in range(self.pairs)]
+        self.most = max(self.counts)
+        self.left = [p * self.pair_cols - starts[p] * self.head_dim for p in range(self.pairs)]
+        self.need = [
+            max(0, starts[p + 1] * self.head_dim - (p + 1) * self.pair_cols)
+            for p in range(self.pairs)
+        ]
+        self.halo = max(self.need)
+        self.rows = max(self.pair_cols + self.halo, self.most * self.head_dim - min(self.left))
+        self.fits = (
+            tp % 2 == 0
+            and self.pairs & (self.pairs - 1) == 0
+            and gain.shape[0] == 1
+            and codes.shape[0] == 1
+            and self.ticks == 2
+            and self.resident == 1
+            and self.images == tp
+            and self.cols % 16 == 0
+            and self.head_dim == HEAD_DIM
+            and starts[-1] == self.heads
+            and max(self.left) <= 0
+            and all(offset % 16 == 0 for offset in self.left)
+            and 0 < self.halo <= self.cols
+            and self.halo % 16 == 0
+            and self.tokens <= SLOT
+            and self.ctx <= SLOT
+            and self.lanes == 128
+        )
+
+
+def dot(left, right, contract=((1,), (0,)), precision=None):
+    return lax.dot_general(
+        left, right, (contract, ((), ())), preferred_element_type=F32, precision=precision
+    )
+
+
+def spread(rows, tick, plan):
+    part = rows[tick * plan.pairs : (tick + 1) * plan.pairs, :]
+    parts = []
+    for _ in range(3):
+        rounded = part.astype(BF16).astype(F32)
+        parts.append(rounded)
+        part = part - rounded
+    count = 3 * plan.pairs
+    stacked = jnp.concatenate(parts, axis=0).astype(BF16)
+    row = lax.broadcasted_iota(jnp.int32, (count, plan.lanes), 0)
+    lane = lax.broadcasted_iota(jnp.int32, (count, plan.lanes), 1)
+    pick = (row % plan.pairs == lane // SLOT).astype(F32).astype(BF16)
+    return dot(stacked, pick, ((0,), (0,)))
+
+
+def label_kernel(plan, labels, table, out, picked):
+    section_at = lax.axis_index("section")
+    place = lax.broadcasted_iota(jnp.int32, (1, plan.classes), 1)
+    row = 0
+    for core in range(2):
+        for tick in range(plan.ticks):
+            for pair in range(plan.pairs):
+                label = labels[tick - section_at + plan.section - 1, 2 * pair + core]
+                picked[row : row + 1, :] = (place == label).astype(F32)
+                row += 1
+    value = dot(picked[...].astype(BF16), table[...], ((1,), (1,)))
+    out[...] = (value / (1.0 + jnp.exp(-value))).astype(BF16)
+
+
+def modulation_kernel(plan, *refs):
+    pairs = plan.pairs
+    near, far = refs[:pairs], refs[pairs : 2 * pairs]
+    matrix, addend, shift, gate, active = refs[2 * pairs :]
+    place = lax.axis_index("tp")
+    core, pair = place % 2, place // 2
+    rows = plan.ticks * plan.images
+    for k in range(pairs):
+        for side, piece in enumerate((near[k], far[k])):
+            value = piece[...].astype(F32)
+            value = jnp.concatenate([value, jnp.zeros((128 - rows, plan.cols), F32)], axis=0).T
+            start = (pair ^ k) * plan.pair_cols + (core if side == 0 else 1 - core) * plan.cols
+            active[pl.ds(pl.multiple_of(start, 16), plan.cols), :] = value.astype(BF16)
+    tokens = active[...]
+    for part in range(3):
+        value = dot(matrix[part], tokens).T[:rows] + addend[part]
+        if part:
+            shift[part - 1] = value
+        else:
+            gate[...] = value
+
+
+def packed_rows(plan):
+    up = lambda rows: rows + -rows % 8
+    first = up(plan.pairs * plan.tokens)
+    second = first + up(plan.ctx)
+    return first, second, second + up(plan.ctx)
+
+
+def stored_kernel(plan, arrival, probes, answers, matrix, edge, *outs):
+    pairs = plan.pairs
+    pair = lax.axis_index("tp") // 2
+    span = plan.most * plan.head_dim
+    key_at, value_at, _ = packed_rows(plan)
+    early, late = outs[:pairs], outs[pairs:]
+    edge[...] = matrix[:, : plan.halo, :]
+    wide = arrival[...].astype(F32)
+    wide_keys, wide_values = probes[...].astype(F32), answers[...].astype(F32)
+    keys = [wide_keys[:, tick, :] for tick in range(plan.ticks)]
+    values = [wide_values[:, tick, :] for tick in range(plan.ticks)]
+    chunks = []
+    for at in range(pairs):
+        chunk = wide[:, at * plan.pair_cols : (at + 1) * plan.pair_cols]
+        chunks.append(
+            jnp.concatenate([chunk, jnp.zeros((plan.tokens, span - plan.pair_cols), F32)], axis=1)
+        )
+    top = jnp.concatenate(
+        chunks + [jnp.zeros((key_at - pairs * plan.tokens, span), F32)], axis=0
+    ).astype(BF16)
+
+    def cut(value, at, rows):
+        start = plan.starts[at] * plan.head_dim
+        reach = min(span, plan.width - start)
+        part = value[:, start : start + reach]
+        if reach < span:
+            part = jnp.concatenate([part, jnp.zeros((plan.ctx, span - reach), F32)], axis=1)
+        return jnp.concatenate([part, jnp.zeros((rows - plan.ctx, span), F32)], axis=0).astype(BF16)
+
+    for k in range(pairs):
+        early[k][:key_at, :] = top
+    for at in range(pairs):
+        pieces = [
+            cut(keys[0], at, value_at - key_at),
+            cut(values[0], at, value_at - key_at),
+            cut(keys[1], at, SLOT),
+            cut(values[1], at, SLOT),
+        ]
+        for k in range(pairs):
+
+            @pl.when((pair ^ k) == at)
+            def _(k=k, pieces=pieces):
+                early[k][key_at:value_at, :] = pieces[0]
+                early[k][value_at:, :] = pieces[1]
+                late[k][0], late[k][1] = pieces[2], pieces[3]
+
+
+def embed_kernel(plan, codes, table, resample, raising, placement, out, full):
+    place = lax.axis_index("tp")
+    core, pair = place % 2, place // 2
+    row = lax.broadcasted_iota(jnp.int32, (plan.vocab, plan.lanes), 0)
+    blank = jnp.zeros((1, SLOT - plan.ctx), jnp.int32)
+    slots = []
+    for image in range(plan.pairs):
+        both = codes[2 * image : 2 * image + 2, :]
+        slots += [jnp.where(core == 0, both[:1], both[1:]), blank]
+    picked = (row == jnp.concatenate(slots, axis=1)).astype(F32)
+    looked = dot(table[...], picked, precision=lax.Precision.HIGHEST)
+    mapped = dot(looked, resample[...], precision=lax.Precision.HIGHEST).astype(BF16)
+    fixed = placement[...].astype(F32)
+    fixed = jnp.concatenate(
+        [fixed, jnp.zeros((SLOT - plan.tokens, plan.width), F32)], axis=0
+    )
+    fixed = jnp.concatenate([fixed] * plan.pairs, axis=0).T
+    full[...] = dot(raising[...], mapped, ((0,), (0,))) + fixed
+    start = pl.multiple_of(pair * plan.pair_cols, 16)
+    out[...] = full[pl.ds(start, plan.pair_cols), :].astype(BF16)
+
+
+def layer_kernel(plan, tick, *refs):
+    pairs = plan.pairs
+    pieces = refs[:pairs]
+    shifts = (refs[pairs : 2 * pairs], refs[2 * pairs : 3 * pairs])
+    stores = refs[3 * pairs : 4 * pairs] if tick else None
+    refs = refs[4 * pairs :] if tick else refs[3 * pairs :]
+    mine, other, near, far, sharp, attended, held = refs[:7]
+    wide, scale_at, offset_at, qkv, cached, *turning = refs[7:]
+    half = plan.ticks * plan.pairs
+    place = lax.axis_index("tp")
+    core, pair = place % 2, place // 2
+    cols, pair_cols, dim, lanes = plan.cols, plan.pair_cols, plan.head_dim, plan.lanes
+
+    for k in range(pairs):
+        at = pair ^ k
+        slot = pl.multiple_of(at * SLOT, SLOT)
+        if tick:
+            start = pl.multiple_of(at * pair_cols, 16)
+            wide[pl.ds(start, pair_cols), :] = pieces[k][...].astype(F32)
+            cached[0, pl.ds(slot, SLOT), :] = stores[k][0]
+            cached[1, pl.ds(slot, SLOT), :] = stores[k][1]
+        else:
+            key_at, value_at, _ = packed_rows(plan)
+            packed = pieces[k][...].astype(F32)
+            chunks = [
+                packed[j * plan.tokens : (j + 1) * plan.tokens, :pair_cols] for j in range(pairs)
+            ]
+            turning[0][pl.ds(slot, SLOT), :] = jnp.concatenate(
+                [
+                    jnp.concatenate(chunks, axis=1),
+                    jnp.zeros((SLOT - plan.tokens, plan.width), F32),
+                ],
+                axis=0,
+            )
+            cached[0, pl.ds(slot, value_at - key_at), :] = packed[key_at:value_at].astype(BF16)
+            cached[1, pl.ds(slot, value_at - key_at), :] = packed[value_at:].astype(BF16)
+        for side in range(2):
+            start = pl.multiple_of(
+                at * pair_cols + (core if side == 0 else 1 - core) * cols, 16
+            )
+            own = pl.ds(pl.multiple_of(core * half, 8), half)
+            scale_at[pl.ds(start, cols), :] = spread(shifts[side][k][0, own, :], tick, plan)
+            offset_at[pl.ds(start, cols), :] = spread(shifts[side][k][1, own, :], tick, plan)
+    if tick == 0:
+        wide[...] = turning[0][...].T
+    value = wide[...]
+    average = jnp.sum(value, axis=0, keepdims=True) * (1.0 / plan.width)
+    centred = value - average
+    variance = jnp.sum(centred * centred, axis=0, keepdims=True) * (1.0 / plan.width)
+    result = centred * lax.rsqrt(variance + 1e-06) * (1.0 + scale_at[...]) + offset_at[...]
+    tokens = result.astype(BF16)
+    start = pl.multiple_of(pair * pair_cols, 16)
+    held[...] = wide[pl.ds(start, pair_cols), :].astype(BF16)
+    if plan.rows > pair_cols + plan.halo:
+        qkv[:, pair_cols + plan.halo :, :] = jnp.zeros(
+            (3, plan.rows - pair_cols - plan.halo, lanes), BF16
+        )
+    for part in range(3):
+        start = pl.multiple_of(core * cols, 16)
+        qkv[part, pl.ds(start, cols), :] = dot(mine[part], tokens).astype(BF16)
+        start = pl.multiple_of((1 - core) * cols, 16)
+        qkv[part, pl.ds(start, cols), :] = dot(other[part], tokens).astype(BF16)
+        edge = jnp.where(core == 1, near[part].astype(F32), far[part].astype(F32)).astype(BF16)
+        qkv[part, pair_cols : pair_cols + plan.halo, :] = dot(edge, tokens).astype(BF16)
+
+    head_at = first_head(pair, pair_cols, dim)
+    begin = head_at * dim - pair * pair_cols
+    row = lax.broadcasted_iota(jnp.int32, (lanes, lanes), 0)
+    lane = lax.broadcasted_iota(jnp.int32, (lanes, lanes), 1)
+    same = row // SLOT == lane // SLOT
+    old_ok = same & (row % SLOT < plan.ctx)
+    new_ok = same & (row % SLOT < plan.tokens)
+    queries, keys, values, lifts, key_scales = [], [], [], [], []
+    for head in range(plan.most):
+        at = pl.ds(pl.multiple_of(begin + head * dim, 16), dim)
+        query, key, value = qkv[0, at, :], qkv[1, at, :], qkv[2, at, :]
+        wide_query, wide_key = query.astype(F32), key.astype(F32)
+        lift = sharp[0, jnp.minimum(head_at + head, plan.heads - 1)]
+        lift = jnp.exp(jnp.minimum(jnp.full((1, lanes), lift, F32), LOG_CAP))
+        lifts.append(
+            lax.rsqrt(jnp.sum(wide_query * wide_query, axis=0, keepdims=True) + 1e-06) * lift
+        )
+        key_scales.append(lax.rsqrt(jnp.sum(wide_key * wide_key, axis=0, keepdims=True) + 1e-06))
+        queries.append(query)
+        keys.append(key)
+        values.append(value)
+    pad = -plan.most % 8
+    key_cols = jnp.concatenate(
+        key_scales + ([jnp.zeros((pad, lanes), F32)] if pad else []), axis=0
+    ).T
+    old_keys, old_values = cached[0], cached[1]
+    for head in range(plan.most):
+        span = slice(head * dim, (head + 1) * dim)
+        old = dot(old_keys[:, span], queries[head]) * lifts[head]
+        new = (
+            dot(keys[head], queries[head], ((0,), (0,)))
+            * key_cols[:, head : head + 1]
+            * lifts[head]
+        )
+        old = jnp.where(old_ok, old, -1e30)
+        new = jnp.where(new_ok, new, -1e30)
+        top = jnp.maximum(
+            jnp.max(old, axis=0, keepdims=True), jnp.max(new, axis=0, keepdims=True)
+        )
+        old, new = jnp.exp(old - top), jnp.exp(new - top)
+        total = 1.0 / (jnp.sum(old, axis=0, keepdims=True) + jnp.sum(new, axis=0, keepdims=True))
+        old, new = (old * total).astype(BF16), (new * total).astype(BF16)
+        mixed = dot(old_values[:, span], old, ((0,), (0,))) + dot(values[head], new)
+        attended[head * dim : (head + 1) * dim, :] = mixed.astype(BF16)
+
+
+def return_kernel(plan, tick, *refs):
+    pairs = plan.pairs
+    pieces = refs[:pairs]
+    mine, other, held, gate_mine, gate_other = refs[pairs : pairs + 5]
+    rest = refs[pairs + 5 :]
+    if tick == 0:
+        entering, onward, *rows = rest[:-3]
+    else:
+        rows = rest[:-3]
+    joined, projected, gate = rest[-3:]
+    place = lax.axis_index("tp")
+    core, pair = place % 2, place // 2
+    cols, pair_cols, dim = plan.cols, plan.pair_cols, plan.head_dim
+    least = min(plan.counts)
+    half = plan.ticks * pairs
+    for k in range(pairs):
+        at = pair ^ k
+        start = first_head(at, pair_cols, dim)
+        count = first_head(at + 1, pair_cols, dim) - start
+        joined[pl.ds(pl.multiple_of(start * dim, 16), least * dim), :] = pieces[k][: least * dim, :]
+        for extra in range(least, plan.most):
+
+            @pl.when(count > extra)
+            def _(k=k, extra=extra, start=start):
+                joined[pl.ds(pl.multiple_of((start + extra) * dim, 16), dim), :] = pieces[k][
+                    extra * dim : (extra + 1) * dim, :
+                ]
+
+    value = joined[...]
+    for side, (matrix, gates) in enumerate(((mine, gate_mine), (other, gate_other))):
+        start = pl.multiple_of((core if side == 0 else 1 - core) * cols, 16)
+        projected[pl.ds(start, cols), :] = dot(matrix[...], value).astype(BF16).astype(F32)
+        gates = gates[pl.ds(pl.multiple_of(core * half, 8), half), :]
+        gate[pl.ds(start, cols), :] = spread(gates, tick, plan)
+    result = held[...].astype(F32) + gate[...] * projected[...]
+    turned = result.T
+    for k in range(pairs):
+        for image in range(pairs):
+
+            @pl.when((pair ^ k) == image)
+            def _(k=k, image=image):
+                rows[k][...] = turned[image * SLOT : image * SLOT + plan.tokens, :].astype(BF16)
+
+    if tick == 0:
+        last = lax.axis_index("section") == plan.section - 1
+        onward[...] = jnp.where(last, entering[...].astype(F32), result).astype(BF16)
+
+
+def gather_kernel(plan, *refs):
+    pairs = plan.pairs
+    pieces, out, full = refs[:-2], refs[-2], refs[-1]
+    pair = lax.axis_index("tp") // 2
+    for tick in range(plan.ticks):
+        for k in range(pairs):
+            for at in range(pairs):
+
+                @pl.when((pair ^ k) == at)
+                def _(tick=tick, k=k, at=at):
+                    full[tick, :, at * plan.pair_cols : (at + 1) * plan.pair_cols] = pieces[
+                        tick * pairs + k
+                    ][...].astype(F32)
+
+    for tick in range(plan.ticks):
+        out[tick] = full[tick].astype(BF16)
+
+
+def resample_blocks(plan):
+    blocks = []
+    for coarse in range(1, SIDE):
+        fine = np.arange(SIDE, dtype=np.float32)
+        rough = np.arange(coarse, dtype=np.float32)
+        one = np.float32(1.0)
+        size, parts = np.float32(SIDE), np.float32(coarse)
+        begins = np.maximum(fine[:, None] / size, rough[None, :] / parts)
+        finish = np.minimum((fine[:, None] + one) / size, (rough[None, :] + one) / parts)
+        crossing = np.maximum(finish - begins, np.float32(0.0)) * size
+        blocks.append(
+            (crossing[:, None, :, None] * crossing[None, :, None, :]).reshape(
+                SIDE * SIDE, coarse * coarse
+            )
+        )
+    table = np.concatenate(blocks, axis=1).astype(np.float32)
+    full = np.zeros((plan.lanes, plan.lanes), np.float32)
+    for image in range(plan.pairs):
+        at = image * SLOT
+        full[at : at + table.shape[1], at : at + table.shape[0]] = table.T
+    return full
+
+
+def paired(plan, *args):
+    (
+        awaiting_arrivals,
+        label_numbers,
+        drawn_coarse_codes,
+        discrete_prototypes,
+        code_raising_operator,
+        placement_tier_features,
+        label_feature_rows,
+        conditioned_gain_mapping,
+        conditioned_shift_addend,
+        question_answer_operator,
+        mixing_return_operator,
+        focus_sharpness_exponents,
+        prior_resolution_probes,
+        prior_resolution_answers,
+    ) = args
+    pairs, tp, cols, pair_cols = plan.pairs, plan.tp, plan.cols, plan.pair_cols
+    width, lanes, dim, ticks = plan.width, plan.lanes, plan.head_dim, plan.ticks
+    rows = ticks * plan.images
+
+    def swap(value, k):
+        return lax.ppermute(value, "tp", [(g, g ^ (2 * k)) for g in range(tp)])
+
+    def across(value):
+        return lax.ppermute(value, "tp", [(g, g ^ 1) for g in range(tp)])
+
+    def around(value):
+        return [value] + [swap(value, k) for k in range(1, pairs)]
+
+    def call(kernel, outs, scratch, values, scalars=(), loose=()):
+        ins = [
+            pltpu.with_memory_space_constraint(
+                v, pltpu.HBM if i in scalars or i in loose else pltpu.VMEM
+            )
+            for i, v in enumerate(values)
+        ]
+        return pl.pallas_call(
+            lambda *refs: kernel(plan, *refs),
+            out_shape=[pltpu.VMEM(shape, dtype) for shape, dtype in outs],
+            in_specs=[
+                pl.BlockSpec(memory_space=pltpu.SMEM if i in scalars else pltpu.VMEM)
+                for i in range(len(values))
+            ],
+            out_specs=[pl.BlockSpec(memory_space=pltpu.VMEM)] * len(outs),
+            scratch_shapes=scratch,
+            compiler_params=pltpu.CompilerParams(vmem_limit_bytes=KERNEL_VMEM),
+        )(*ins)
+
+    span = plan.most * dim
+    (active,) = call(
+        label_kernel,
+        [((rows, cols), BF16)],
+        [pltpu.VMEM((rows, plan.classes), F32)],
+        [label_numbers, label_feature_rows.T],
+        (0,),
+        (1,),
+    )
+    active = around(active)
+    active += [across(piece) for piece in active]
+    shift, gate = call(
+        modulation_kernel,
+        [((2, rows, cols), F32), ((rows, cols), F32)],
+        [pltpu.VMEM((width, 128), BF16)],
+        [
+            *active,
+            jnp.transpose(conditioned_gain_mapping[0], (1, 2, 0)),
+            jnp.transpose(conditioned_shift_addend, (1, 0, 2)),
+        ],
+    )
+    shifts = around(shift)
+    shifts += [across(piece) for piece in shifts]
+    gate_back = across(gate)
+
+    qkv_mine = jnp.transpose(question_answer_operator[0], (1, 2, 0))
+    qkv_other = across(qkv_mine)
+    out_mine = mixing_return_operator[0].T
+    out_other = across(out_mine)
+    edge, *stores = call(
+        stored_kernel,
+        [((3, plan.halo, width), BF16)]
+        + [((packed_rows(plan)[2], span), BF16)] * pairs
+        + [((2, SLOT, span), BF16)] * pairs,
+        [],
+        [
+            awaiting_arrivals[0, 0],
+            jnp.transpose(prior_resolution_probes[0, :, 0], (1, 0, 2)),
+            jnp.transpose(prior_resolution_answers[0, :, 0], (1, 0, 2)),
+            qkv_mine,
+        ],
+        (),
+        (0, 1, 2),
+    )
+    near = lax.ppermute(edge, "tp", [(2 * p + 2, 2 * p + 1) for p in range(pairs) if plan.need[p]])
+    far = across(near)
+    pieces = [stores[0]] + [swap(stores[k], k) for k in range(1, pairs)]
+    later = [stores[pairs]] + [swap(stores[pairs + k], k) for k in range(1, pairs)]
+    (entering,) = call(
+        embed_kernel,
+        [((pair_cols, lanes), BF16)],
+        [pltpu.VMEM((width, lanes), F32)],
+        [
+            drawn_coarse_codes[0],
+            discrete_prototypes.T,
+            jnp.asarray(resample_blocks(plan)),
+            code_raising_operator,
+            placement_tier_features,
+        ],
+        (),
+        range(5),
+    )
+
+    emitted = []
+    for tick in range(ticks):
+        scratch = [
+            pltpu.VMEM((width, lanes), F32),
+            pltpu.VMEM((width, lanes), F32),
+            pltpu.VMEM((width, lanes), F32),
+            pltpu.VMEM((3, plan.rows, lanes), BF16),
+            pltpu.VMEM((2, lanes, span), BF16),
+        ]
+        if tick == 0:
+            scratch.append(pltpu.VMEM((lanes, width), F32))
+        values = [*pieces, *shifts] + (later if tick else [])
+        values += [qkv_mine, qkv_other, near, far, focus_sharpness_exponents]
+        attended, held = call(
+            lambda *refs, tick=tick: layer_kernel(refs[0], tick, *refs[1:]),
+            [((span, lanes), BF16), ((pair_cols, lanes), BF16)],
+            scratch,
+            values,
+            (len(values) - 1,),
+        )
+        outs = [((plan.tokens, pair_cols), BF16)] * pairs
+        extra = []
+        if tick + 1 < ticks:
+            outs = [((pair_cols, lanes), BF16)] + outs
+            extra = [entering]
+        results = call(
+            lambda *refs, tick=tick: return_kernel(refs[0], tick, *refs[1:]),
+            outs,
+            [
+                pltpu.VMEM((width, lanes), BF16),
+                pltpu.VMEM((pair_cols, lanes), F32),
+                pltpu.VMEM((pair_cols, lanes), F32),
+            ],
+            [
+                *around(attended),
+                out_mine,
+                out_other,
+                held,
+                gate,
+                gate_back,
+                *extra,
+            ],
+        )
+        if tick + 1 < ticks:
+            onward = lax.ppermute(
+                results[0],
+                "section",
+                [(s, (s + 1) % plan.section) for s in range(plan.section)],
+            )
+            pieces = around(onward)
+        final = results[-pairs:]
+        emitted += [final[0]] + [swap(final[k], k) for k in range(1, pairs)]
+    (out,) = call(
+        gather_kernel,
+        [((ticks, plan.tokens, width), BF16)],
+        [pltpu.VMEM((ticks, plan.tokens, width), F32)],
+        emitted,
+    )
+    return out[None, :, None]
+
+
+def local(*args):
+    plan = Plan(lax.axis_size("section"), lax.axis_size("tp"), args)
+    return paired(plan, *args) if plan.fits else general(*args)
+
+
 def solution(mesh):
     in_specs = (
         P("section", "tp", None, None),

time: 246 us -> 135 us (0.55)
  blocking collectives: 82.9 us -> 0 us
  local copies, waits for them, and re-layouts: 63.8 us -> 4.4 us
  waiting for transfers between devices: 20.9 us -> 59.9 us
  matrix products: 25.3 us -> 0 us
  other arithmetic: 23.5 us -> 0 us
  starting transfers between devices: 27.2 us -> 49 us
  Pallas kernels: 0 us -> 19.4 us
    all_gather x5 -> x0, blocking collectives: 82.9 us -> none  [the longest x2 33.3 us: local(): lax.all_gather(normed, 'tp', axis=0, tiled=True)]
    ppermute x1 -> x41, waiting for transfers between devices: 3.63 us -> 59.9 us  [the longest x27 52 us: swap(): return lax.ppermute(value, 'tp', [(g, g ^ 2 * k) for g in range(tp)])]
    ppermute x1 -> x41, starting transfers between devices: 3.4 us -> 49 us  [the longest x27 44.7 us: swap(): return lax.ppermute(value, 'tp', [(g, g ^ 2 * k) for g in range(tp)])]
    dot_general x11 -> x0, matrix products: 25.3 us -> none  [the longest x2 7.32 us: attention(): jnp.einsum('ihqk,ikhd->iqhd', probabilities, all_values, preferred_elemen...]
    all_to_all x5 -> x0, starting transfers between devices: 23.9 us -> none  [the longest x2 9.52 us: attention(): lax.all_to_all(qkv_cols, 'tp', split_axis=0, concat_axis=3, tiled=True)]
    pallas_call x0 -> x9, Pallas kernels: none -> 19.4 us  [call(): pl.pallas_call(lambda *refs: kernel(plan, *refs), out_shape=[pltpu.VMEM(s...]
    all_to_all x5 -> x0, waiting for transfers between devices: 17.2 us -> none  [the longest x2 12.5 us: local(): lax.all_to_all(projected_cols, 'tp', split_axis=0, concat_axis=2, tiled=T...]
    another operation x13 -> x0, local copies, waits for them, and re-layouts: 14.9 us -> none  [the longest x4 4.64 us: attention(): cached_values.reshape(images, -1, FOCUS_GROUPS, HEAD_DIM)]
  transfers between devices with their start and end apart: 6 -> 41, of which waited for: 4 -> 19; matrix products, arithmetic and copies ran while one was open for 12% -> 0% of each run, Pallas kernels for 0% -> 10%
where the time goes in v1:
time: 135 us; the launch traced here: 133 us
  waiting for transfers between devices  59.9 us (44%)
  starting transfers between devices  49 us (36%)
  Pallas kernels  19.4 us (14%)
  local copies, waits for them, and re-layouts  4.4 us (3%)
    ppermute x27, waiting for transfers between devices, swap(): return lax.ppermute(value, 'tp', [(g, g ^ 2 * k) for g in range(tp)])  52 us
    ppermute x27, starting transfers between devices, swap(): return lax.ppermute(value, 'tp', [(g, g ^ 2 * k) for g in range(tp)])  44.7 us
    pallas_call x9, Pallas kernels, call(): pl.pallas_call(lambda *refs: kernel(plan, *refs), out_shape=[pltpu.VMEM(s...  19.4 us
    ppermute x12, waiting for transfers between devices, across(): return lax.ppermute(value, 'tp', [(g, g ^ 1) for g in range(tp)])  6.02 us
    unnamed x10, local copies, waits for them, and re-layouts  3.58 us
  transfers between devices with their start and end apart: 41, of which 19 were waited for; matrix products, arithmetic and copies ran while one was open for 0% of the time, Pallas kernels for 10%

profile of v1, /device:TPU:4, one launch (start us, length us, event | category | flops | bytes accessed | tf_op | source)
XLA Modules:
  0.0 132.8 jit_solution(6583904923119650152)
XLA Ops:
  0.5 1.8 %copy-done = bf16[1,1920,3,240]{1,3,2,0:T(8,128)(2,1)S(1)} copy-done((bf16[1,1920,3,240]{1,3,2,0:T(8,128)(2,1)S(1)}, bf16[1,1920,3,240]{1,3,2,0:T(8,128)(2,1)}, u32[]{:S(2)}) %copy-start) | copy-done | bytes 2764824
  2.3 2.0 %shard_map.145 = (bf16[3,32,1920]{2,1,0:T(8,128)(2,1)S(1)}, bf16[168,512]{1,0:T(8,128)(2,1)S(1)}, bf16[168,512]{1,0:T(8,128)(2,1)S(1)}, bf16[168,512]{1,0:T(8,12...) custom-call(bf16[25,1920]{1,0:T(8,128)(2,1)} %bitcast.35, ...), custom_call_target="tpu_custom_call" | custom-call | tf_op jit(solution)/shard_map/pallas_call | solution.py:638
  5.0 1.3 %shard_map.146.refs_0_ = bf16[16,240]{1,0:T(8,128)(2,1)S(1)} custom-call(s32[5,8]{1,0:T(8,128)} %refs_0_.1, bf16[240,1001]{1,0:T(8,128)(2,1)} %bitcast.32), custom_call_target="tpu_custom_call" | custom-call | tf_op jit(solution)/shard_map/pallas_call | solution.py:638
  6.3 3.0 %collective-permute-start.3 = (bf16[16,240]{1,0:T(8,128)(2,1)S(1)}, bf16[16,240]{1,0:T(8,128)(2,1)S(1)}, u32[]{:S(2)}, u32[]{:S(2)}) collective-permute-start(bf16[16,240]{1,0:T(8,128)(2,1)S(1)} %shard_map.146.refs_0_), channel_id=1, source_target_pairs={{0,2},{1,3},{2,0},{3,1},{4,6},{5,7},{6,4},{7,5},{8,10},{9,11},{10,... | collective-permute-start | bytes 23048 | tf_op jit(solution)/shard_map/ppermute | solution.py:623
  9.3 2.6 %collective-permute-start.4 = (bf16[16,240]{1,0:T(8,128)(2,1)S(1)}, bf16[16,240]{1,0:T(8,128)(2,1)S(1)}, u32[]{:S(2)}, u32[]{:S(2)}) collective-permute-start(bf16[16,240]{1,0:T(8,128)(2,1)S(1)} %shard_map.146.refs_0_), channel_id=1, source_target_pairs={{0,4},{1,5},{2,6},{3,7},{4,0},{5,1},{6,2},{7,3},{8,12},{9,13},{10,... | collective-permute-start | bytes 23048 | tf_op jit(solution)/shard_map/ppermute | solution.py:623
  11.9 1.7 %collective-permute-done.3.refs_1_ = bf16[16,240]{1,0:T(8,128)(2,1)S(1)} collective-permute-done((bf16[16,240]{1,0:T(8,128)(2,1)S(1)}, bf16[16,240]{1,0:T(8,128)(2,1)S(1)}, u32[]{:S(2)}, u32[]{:S(2)}) %collective-permute-start.3) | collective-permute-done | bytes 7712 | tf_op jit(solution)/shard_map/ppermute | solution.py:623
  13.6 1.7 %collective-permute-start.5 = (bf16[16,240]{1,0:T(8,128)(2,1)S(1)}, bf16[16,240]{1,0:T(8,128)(2,1)S(1)}, u32[]{:S(2)}, u32[]{:S(2)}) collective-permute-start(bf16[16,240]{1,0:T(8,128)(2,1)S(1)} %shard_map.146.refs_0_), channel_id=1, source_target_pairs={{0,6},{1,7},{2,4},{3,5},{4,2},{5,3},{6,0},{7,1},{8,14},{9,15},{10,... | collective-permute-start | bytes 23048 | tf_op jit(solution)/shard_map/ppermute | solution.py:623
  15.3 3.8 %collective-permute-done.5.refs_3_ = bf16[16,240]{1,0:T(8,128)(2,1)S(1)} collective-permute-done((bf16[16,240]{1,0:T(8,128)(2,1)S(1)}, bf16[16,240]{1,0:T(8,128)(2,1)S(1)}, u32[]{:S(2)}, u32[]{:S(2)}) %collective-permute-start.5) | collective-permute-done | bytes 7712 | tf_op jit(solution)/shard_map/ppermute | solution.py:623
  20.4 1.0 collective-permute-done.9.refs_7_
  21.4 1.8 %copy-done.3 = bf16[1,1920,3,240]{1,3,2,0:T(8,128)(2,1)S(1)} copy-done((bf16[1,1920,3,240]{1,3,2,0:T(8,128)(2,1)S(1)}, bf16[1,1920,3,240]{1,3,2,0:T(8,128)(2,1)}, u32[]{:S(2)}) %copy-start.3) | copy-done | bytes 2764824
  23.2 1.2 shard_map.147
  24.7 2.0 %collective-permute-start.11 = (f32[2,16,240]{2,1,0:T(8,128)S(1)}, f32[2,16,240]{2,1,0:T(8,128)S(1)}, u32[]{:S(2)}, u32[]{:S(2)}) collective-permute-start(f32[2,16,240]{2,1,0:T(8,128)S(1)} %get-tuple-element.33.refs_4_), channel_id=1, source_target_pairs={{0,4},{1,5},{2,6},{3,7},{4,0},{5,1},{6,2},{7,3},{8,12},{9,13},{10,... | collective-permute-start | bytes 92168 | tf_op jit(solution)/shard_map/ppermute | solution.py:623
  26.7 1.7 %collective-permute-done.10.refs_5_ = f32[2,16,240]{2,1,0:T(8,128)S(1)} collective-permute-done((f32[2,16,240]{2,1,0:T(8,128)S(1)}, f32[2,16,240]{2,1,0:T(8,128)S(1)}, u32[]{:S(2)}, u32[]{:S(2)}) %collective-permute-start.10) | collective-permute-done | bytes 30752 | tf_op jit(solution)/shard_map/ppermute | solution.py:623
  28.3 1.1 collective-permute-done.11.refs_6_
  29.5 2.1 %collective-permute-start.12 = (f32[2,16,240]{2,1,0:T(8,128)S(1)}, f32[2,16,240]{2,1,0:T(8,128)S(1)}, u32[]{:S(2)}, u32[]{:S(2)}) collective-permute-start(f32[2,16,240]{2,1,0:T(8,128)S(1)} %get-tuple-element.33.refs_4_), channel_id=1, source_target_pairs={{0,6},{1,7},{2,4},{3,5},{4,2},{5,3},{6,0},{7,1},{8,14},{9,15},{10,... | collective-permute-start | bytes 92168 | tf_op jit(solution)/shard_map/ppermute | solution.py:623
  31.6 3.7 %collective-permute-done.12.refs_7_ = f32[2,16,240]{2,1,0:T(8,128)S(1)} collective-permute-done((f32[2,16,240]{2,1,0:T(8,128)S(1)}, f32[2,16,240]{2,1,0:T(8,128)S(1)}, u32[]{:S(2)}, u32[]{:S(2)}) %collective-permute-start.12) | collective-permute-done | bytes 30752 | tf_op jit(solution)/shard_map/ppermute | solution.py:623
  35.3 1.2 collective-permute-done.13.refs_8_
  36.7 1.0 collective-permute-done.14.refs_9_
  37.9 1.0 collective-permute-done.15.refs_10_
  39.1 1.0 collective-permute-done.16.refs_11_
  40.6 2.5 %collective-permute-start.2 = (bf16[168,512]{1,0:T(8,128)(2,1)S(1)}, bf16[168,512]{1,0:T(8,128)(2,1)S(1)}, u32[]{:S(2)}, u32[]{:S(2)}) collective-permute-start(bf16[168,512]{1,0:T(8,128)(2,1)S(1)} %get-tuple-element.32), channel_id=1, source_target_pairs={{0,6},{1,7},{2,4},{3,5},{4,2},{5,3},{6,0},{7,1},{8,14},{9,15},{10,... | collective-permute-start | bytes 516104 | tf_op jit(solution)/shard_map/ppermute | solution.py:623
  43.1 11.9 %collective-permute-done.1.refs_2_ = bf16[168,512]{1,0:T(8,128)(2,1)S(1)} collective-permute-done((bf16[168,512]{1,0:T(8,128)(2,1)S(1)}, bf16[168,512]{1,0:T(8,128)(2,1)S(1)}, u32[]{:S(2)}, u32[]{:S(2)}) %collective-permute-start.1) | collective-permute-done | bytes 172064 | tf_op jit(solution)/shard_map/ppermute | solution.py:623
  55.0 5.0 %shard_map.148 = (bf16[512,128]{1,0:T(8,128)(2,1)S(1)}, bf16[480,128]{1,0:T(8,128)(2,1)S(1)}) custom-call(bf16[168,512]{1,0:T(8,128)(2,1)S(1)} %get-tuple-element.29.refs_0_, bf16[168,512]{1,0:T(8,128)(2,1)S(1)} %collective-permute-done.refs_1_, bf16[168,512]{1,0:T(8,128)(2,1)S(1)} %collective-permute-done.1.refs_2_, ...), custom_call_target="tpu_custom_call" | custom-call | tf_op jit(solution)/shard_map/pallas_call | solution.py:638
  60.0 4.2 %collective-permute-start.20 = (bf16[512,128]{1,0:T(8,128)(2,1)S(1)}, bf16[512,128]{1,0:T(8,128)(2,1)S(1)}, u32[]{:S(2)}, u32[]{:S(2)}) collective-permute-start(bf16[512,128]{1,0:T(8,128)(2,1)S(1)} %get-tuple-element.35.refs_0_), channel_id=1, source_target_pairs={{0,2},{1,3},{2,0},{3,1},{4,6},{5,7},{6,4},{7,5},{8,10},{9,11},{10,... | collective-permute-start | bytes 393224 | tf_op jit(solution)/shard_map/ppermute | solution.py:623
  64.2 2.4 %collective-permute-start.22 = (bf16[512,128]{1,0:T(8,128)(2,1)S(1)}, bf16[512,128]{1,0:T(8,128)(2,1)S(1)}, u32[]{:S(2)}, u32[]{:S(2)}) collective-permute-start(bf16[512,128]{1,0:T(8,128)(2,1)S(1)} %get-tuple-element.35.refs_0_), channel_id=1, source_target_pairs={{0,6},{1,7},{2,4},{3,5},{4,2},{5,3},{6,0},{7,1},{8,14},{9,15},{10,... | collective-permute-start | bytes 393224 | tf_op jit(solution)/shard_map/ppermute | solution.py:623
  66.7 2.9 %shard_map.149.refs_9_ = bf16[480,128]{1,0:T(8,128)(2,1)S(1)} custom-call(s32[8,30]{1,0:T(8,128)} %bitcast.36, f32[32,4096]{1,0:T(8,128)} %bitcast.31, f32[128,128]{1,0:T(8,128)} %constant.2.clone.refs_2_, bf16[32,1920]{1,0:T(8,128)(2,1)} %refs_3_.1, bf16[25,1920]{1,0:T(8,128)(2,1)} %refs_4_.1), custom_call_target="tpu_custom_call" | custom-call | tf_op jit(solution)/shard_map/pallas_call | solution.py:638
  69.6 7.1 %collective-permute-done.21.refs_2_ = bf16[512,128]{1,0:T(8,128)(2,1)S(1)} collective-permute-done((bf16[512,128]{1,0:T(8,128)(2,1)S(1)}, bf16[512,128]{1,0:T(8,128)(2,1)S(1)}, u32[]{:S(2)}, u32[]{:S(2)}) %collective-permute-start.21) | collective-permute-done | bytes 131104 | tf_op jit(solution)/shard_map/ppermute | solution.py:623
  76.8 1.1 shard_map.150
  77.8 1.7 %collective-permute-start.28 = (bf16[480,128]{1,0:T(8,128)(2,1)S(1)}, bf16[480,128]{1,0:T(8,128)(2,1)S(1)}, u32[]{:S(2)}, u32[]{:S(2)}) collective-permute-start(bf16[480,128]{1,0:T(8,128)(2,1)S(1)} %get-tuple-element.42), channel_id=1, source_target_pairs={{0,8},{8,16},{16,24},{24,0},{1,9},{9,17},{17,25},{25,1},{2,10},{10... | collective-permute-start | bytes 368648 | tf_op jit(solution)/shard_map/ppermute | solution.py:757
  79.6 2.5 %collective-permute-start.32 = (bf16[2,32,512]{2,1,0:T(8,128)(2,1)S(1)}, bf16[2,32,512]{2,1,0:T(8,128)(2,1)S(1)}, u32[]{:S(2)}, u32[]{:S(2)}) collective-permute-start(bf16[2,32,512]{2,1,0:T(8,128)(2,1)S(1)} %get-tuple-element.44), channel_id=1, source_target_pairs={{0,2},{1,3},{2,0},{3,1},{4,6},{5,7},{6,4},{7,5},{8,10},{9,11},{10,... | collective-permute-start | bytes 196616 | tf_op jit(solution)/shard_map/ppermute | solution.py:623
  82.0 1.8 %collective-permute-done.28.refs_0_ = bf16[480,128]{1,0:T(8,128)(2,1)S(1)} collective-permute-done((bf16[480,128]{1,0:T(8,128)(2,1)S(1)}, bf16[480,128]{1,0:T(8,128)(2,1)S(1)}, u32[]{:S(2)}, u32[]{:S(2)}) %collective-permute-start.28) | collective-permute-done | bytes 122912 | tf_op jit(solution)/shard_map/ppermute | solution.py:757
  83.8 2.5 %collective-permute-start.29 = (bf16[480,128]{1,0:T(8,128)(2,1)S(1)}, bf16[480,128]{1,0:T(8,128)(2,1)S(1)}, u32[]{:S(2)}, u32[]{:S(2)}) collective-permute-start(bf16[480,128]{1,0:T(8,128)(2,1)S(1)} %collective-permute-done.28.refs_0_), channel_id=1, source_target_pairs={{0,2},{1,3},{2,0},{3,1},{4,6},{5,7},{6,4},{7,5},{8,10},{9,11},{10,... | collective-permute-start | bytes 368648 | tf_op jit(solution)/shard_map/ppermute | solution.py:623
  86.3 2.4 %collective-permute-start.31 = (bf16[480,128]{1,0:T(8,128)(2,1)S(1)}, bf16[480,128]{1,0:T(8,128)(2,1)S(1)}, u32[]{:S(2)}, u32[]{:S(2)}) collective-permute-start(bf16[480,128]{1,0:T(8,128)(2,1)S(1)} %collective-permute-done.28.refs_0_), channel_id=1, source_target_pairs={{0,6},{1,7},{2,4},{3,5},{4,2},{5,3},{6,0},{7,1},{8,14},{9,15},{10,... | collective-permute-start | bytes 368648 | tf_op jit(solution)/shard_map/ppermute | solution.py:623
  88.7 1.1 collective-permute-start.33
  89.7 2.4 %collective-permute-start.34 = (bf16[2,32,512]{2,1,0:T(8,128)(2,1)S(1)}, bf16[2,32,512]{2,1,0:T(8,128)(2,1)S(1)}, u32[]{:S(2)}, u32[]{:S(2)}) collective-permute-start(bf16[2,32,512]{2,1,0:T(8,128)(2,1)S(1)} %get-tuple-element.46), channel_id=1, source_target_pairs={{0,6},{1,7},{2,4},{3,5},{4,2},{5,3},{6,0},{7,1},{8,14},{9,15},{10,... | collective-permute-start | bytes 196616 | tf_op jit(solution)/shard_map/ppermute | solution.py:623
  92.2 10.7 %collective-permute-done.33.refs_14_ = bf16[2,32,512]{2,1,0:T(8,128)(2,1)S(1)} collective-permute-done((bf16[2,32,512]{2,1,0:T(8,128)(2,1)S(1)}, bf16[2,32,512]{2,1,0:T(8,128)(2,1)S(1)}, u32[]{:S(2)}, u32[]{:S(2)}) %collective-permute-start.33) | collective-permute-done | bytes 65568 | tf_op jit(solution)/shard_map/ppermute | solution.py:623
  102.9 4.4 %shard_map.151 = (bf16[512,128]{1,0:T(8,128)(2,1)S(1)}, bf16[480,128]{1,0:T(8,128)(2,1)S(1)}) custom-call(bf16[480,128]{1,0:T(8,128)(2,1)S(1)} %collective-permute-done.28.refs_0_, bf16[480,128]{1,0:T(8,128)(2,1)S(1)} %collective-permute-done.29.refs_1_, bf16[480,128]{1,0:T(8,128)(2,1)S(1)} %collective-permute-done.30.refs_2_, ...), custom_call_target="tpu_custom_call" | custom-call | tf_op jit(solution)/shard_map/pallas_call | solution.py:638
  107.3 1.3 collective-permute-start.35
  109.2 2.5 %collective-permute-start.37 = (bf16[512,128]{1,0:T(8,128)(2,1)S(1)}, bf16[512,128]{1,0:T(8,128)(2,1)S(1)}, u32[]{:S(2)}, u32[]{:S(2)}) collective-permute-start(bf16[512,128]{1,0:T(8,128)(2,1)S(1)} %get-tuple-element.47.refs_0_), channel_id=1, source_target_pairs={{0,6},{1,7},{2,4},{3,5},{4,2},{5,3},{6,0},{7,1},{8,14},{9,15},{10,... | collective-permute-start | bytes 393224 | tf_op jit(solution)/shard_map/ppermute | solution.py:623
  112.1 1.5 %collective-permute-start.26 = (bf16[25,480]{1,0:T(8,128)(2,1)S(1)}, bf16[25,480]{1,0:T(8,128)(2,1)S(1)}, u32[]{:S(2)}, u32[]{:S(2)}) collective-permute-start(bf16[25,480]{1,0:T(8,128)(2,1)S(1)} %get-tuple-element.40), channel_id=1, source_target_pairs={{0,4},{1,5},{2,6},{3,7},{4,0},{5,1},{6,2},{7,3},{8,12},{9,13},{10,... | collective-permute-start | bytes 72008 | tf_op jit(solution)/shard_map/ppermute | solution.py:623
  113.6 1.7 %collective-permute-done.35.refs_1_ = bf16[512,128]{1,0:T(8,128)(2,1)S(1)} collective-permute-done((bf16[512,128]{1,0:T(8,128)(2,1)S(1)}, bf16[512,128]{1,0:T(8,128)(2,1)S(1)}, u32[]{:S(2)}, u32[]{:S(2)}) %collective-permute-start.35) | collective-permute-done | bytes 131104 | tf_op jit(solution)/shard_map/ppermute | solution.py:623
  115.2 0.9 collective-permute-start.27
  116.1 5.3 %collective-permute-done.36.refs_2_ = bf16[512,128]{1,0:T(8,128)(2,1)S(1)} collective-permute-done((bf16[512,128]{1,0:T(8,128)(2,1)S(1)}, bf16[512,128]{1,0:T(8,128)(2,1)S(1)}, u32[]{:S(2)}, u32[]{:S(2)}) %collective-permute-start.36) | collective-permute-done | bytes 131104 | tf_op jit(solution)/shard_map/ppermute | solution.py:623
  121.4 1.0 shard_map.152
  122.4 3.3 %collective-permute-start.38 = (bf16[25,480]{1,0:T(8,128)(2,1)S(1)}, bf16[25,480]{1,0:T(8,128)(2,1)S(1)}, u32[]{:S(2)}, u32[]{:S(2)}) collective-permute-start(bf16[25,480]{1,0:T(8,128)(2,1)S(1)} %get-tuple-element.50), channel_id=1, source_target_pairs={{0,2},{1,3},{2,0},{3,1},{4,6},{5,7},{6,4},{7,5},{8,10},{9,11},{10,... | collective-permute-start | bytes 72008 | tf_op jit(solution)/shard_map/ppermute | solution.py:623
  125.7 2.4 %collective-permute-start.40 = (bf16[25,480]{1,0:T(8,128)(2,1)S(1)}, bf16[25,480]{1,0:T(8,128)(2,1)S(1)}, u32[]{:S(2)}, u32[]{:S(2)}) collective-permute-start(bf16[25,480]{1,0:T(8,128)(2,1)S(1)} %get-tuple-element.52), channel_id=1, source_target_pairs={{0,6},{1,7},{2,4},{3,5},{4,2},{5,3},{6,0},{7,1},{8,14},{9,15},{10,... | collective-permute-start | bytes 72008 | tf_op jit(solution)/shard_map/ppermute | solution.py:623
  128.2 2.4 %collective-permute-done.39.refs_6_ = bf16[25,480]{1,0:T(8,128)(2,1)S(1)} collective-permute-done((bf16[25,480]{1,0:T(8,128)(2,1)S(1)}, bf16[25,480]{1,0:T(8,128)(2,1)S(1)}, u32[]{:S(2)}, u32[]{:S(2)}) %collective-permute-start.39) | collective-permute-done | bytes 24032 | tf_op jit(solution)/shard_map/ppermute | solution.py:623
  130.6 0.9 collective-permute-done.40.refs_7_
  (54 shorter events, 6.1 us)
Async XLA Ops:
  0.0 21.4 %copy-start.4 = (f32[1,3,240]{2,0,1:T(1,128)S(1)}, f32[1,3,240]{2,0,1:T(1,128)}, u32[]{:S(2)}) copy-start(f32[1,3,240]{2,0,1:T(1,128)} %param.23) | copy-start | bytes 8644
  0.0 55.0 %collective-permute-start.17 = (bf16[3,240,1920]{2,1,0:T(8,128)(2,1)}, bf16[3,240,1920]{2,1,0:T(8,128)(2,1)S(1)}, u32[]{:S(2)}, u32[]{:S(2)}) collective-permute-start(bf16[3,240,1920]{2,1,0:T(8,128)(2,1)} %bitcast.21), channel_id=1, source_target_pairs={{0,1},{1,0},{2,3},{3,2},{4,5},{5,4},{6,7},{7,6},{8,9},{9,8},{10,11... | collective-permute-start | bytes 8294408 | tf_op jit(solution)/shard_map/ppermute | solution.py:626
  0.0 69.6 %collective-permute-start.23 = (bf16[240,1920]{1,0:T(8,128)(2,1)}, bf16[240,1920]{1,0:T(8,128)(2,1)S(1)}, u32[]{:S(2)}, u32[]{:S(2)}) collective-permute-start(bf16[240,1920]{1,0:T(8,128)(2,1)} %bitcast.25), channel_id=1, source_target_pairs={{0,1},{1,0},{2,3},{3,2},{4,5},{5,4},{6,7},{7,6},{8,9},{9,8},{10,11... | collective-permute-start | bytes 2764808 | tf_op jit(solution)/shard_map/ppermute | solution.py:626
  0.5 1.8 %copy-start = (bf16[1,1920,3,240]{1,3,2,0:T(8,128)(2,1)S(1)}, bf16[1,1920,3,240]{1,3,2,0:T(8,128)(2,1)}, u32[]{:S(2)}) copy-start(bf16[1,1920,3,240]{1,3,2,0:T(8,128)(2,1)} %param.24) | copy-start | bytes 8294404
  2.3 52.7 %copy-start.1 = (bf16[1,1920,3,240]{1,3,2,0:T(8,128)(2,1)S(1)}, bf16[1,1920,3,240]{1,3,2,0:T(8,128)(2,1)}, u32[]{:S(2)}) copy-start(bf16[1,1920,3,240]{1,3,2,0:T(8,128)(2,1)} %param.24) | copy-start | bytes 8294404
  4.3 20.1 %collective-permute-start.18 = (bf16[3,32,1920]{2,1,0:T(8,128)(2,1)S(1)}, bf16[3,32,1920]{2,1,0:T(8,128)(2,1)S(1)}, u32[]{:S(2)}, u32[]{:S(2)}) collective-permute-start(bf16[3,32,1920]{2,1,0:T(8,128)(2,1)S(1)} %get-tuple-element.34), channel_id=1, source_target_pairs={{2,1},{6,5},{10,9},{14,13},{18,17},{22,21},{26,25},{30,29}} | collective-permute-start | bytes 1105928 | tf_op jit(solution)/shard_map/ppermute | solution.py:694
  6.3 7.3 %collective-permute-start.3 = (bf16[16,240]{1,0:T(8,128)(2,1)S(1)}, bf16[16,240]{1,0:T(8,128)(2,1)S(1)}, u32[]{:S(2)}, u32[]{:S(2)}) collective-permute-start(bf16[16,240]{1,0:T(8,128)(2,1)S(1)} %shard_map.146.refs_0_), channel_id=1, source_target_pairs={{0,2},{1,3},{2,0},{3,1},{4,6},{5,7},{6,4},{7,5},{8,10},{9,11},{10,... | collective-permute-start | bytes 23048 | tf_op jit(solution)/shard_map/ppermute | solution.py:623
  9.3 6.0 %collective-permute-start.4 = (bf16[16,240]{1,0:T(8,128)(2,1)S(1)}, bf16[16,240]{1,0:T(8,128)(2,1)S(1)}, u32[]{:S(2)}, u32[]{:S(2)}) collective-permute-start(bf16[16,240]{1,0:T(8,128)(2,1)S(1)} %shard_map.146.refs_0_), channel_id=1, source_target_pairs={{0,4},{1,5},{2,6},{3,7},{4,0},{5,1},{6,2},{7,3},{8,12},{9,13},{10,... | collective-permute-start | bytes 23048 | tf_op jit(solution)/shard_map/ppermute | solution.py:623
  13.6 5.4 %collective-permute-start.5 = (bf16[16,240]{1,0:T(8,128)(2,1)S(1)}, bf16[16,240]{1,0:T(8,128)(2,1)S(1)}, u32[]{:S(2)}, u32[]{:S(2)}) collective-permute-start(bf16[16,240]{1,0:T(8,128)(2,1)S(1)} %shard_map.146.refs_0_), channel_id=1, source_target_pairs={{0,6},{1,7},{2,4},{3,5},{4,2},{5,3},{6,0},{7,1},{8,14},{9,15},{10,... | collective-permute-start | bytes 23048 | tf_op jit(solution)/shard_map/ppermute | solution.py:623
  15.3 3.8 %collective-permute-start.6 = (bf16[16,240]{1,0:T(8,128)(2,1)S(1)}, bf16[16,240]{1,0:T(8,128)(2,1)S(1)}, u32[]{:S(2)}, u32[]{:S(2)}) collective-permute-start(bf16[16,240]{1,0:T(8,128)(2,1)S(1)} %shard_map.146.refs_0_), channel_id=1, source_target_pairs={{0,1},{1,0},{2,3},{3,2},{4,5},{5,4},{6,7},{7,6},{8,9},{9,8},{10,11... | collective-permute-start | bytes 23048 | tf_op jit(solution)/shard_map/ppermute | solution.py:626
  19.1 1.2 collective-permute-start.7
  19.1 1.3 %collective-permute-start.8 = (bf16[16,240]{1,0:T(8,128)(2,1)S(1)}, bf16[16,240]{1,0:T(8,128)(2,1)S(1)}, u32[]{:S(2)}, u32[]{:S(2)}) collective-permute-start(bf16[16,240]{1,0:T(8,128)(2,1)S(1)} %collective-permute-done.4.refs_2_), channel_id=1, source_target_pairs={{0,1},{1,0},{2,3},{3,2},{4,5},{5,4},{6,7},{7,6},{8,9},{9,8},{10,11... | collective-permute-start | bytes 23048 | tf_op jit(solution)/shard_map/ppermute | solution.py:626
  20.3 1.2 collective-permute-start.9
  21.4 1.8 %copy-start.3 = (bf16[1,1920,3,240]{1,3,2,0:T(8,128)(2,1)S(1)}, bf16[1,1920,3,240]{1,3,2,0:T(8,128)(2,1)}, u32[]{:S(2)}) copy-start(bf16[1,1920,3,240]{1,3,2,0:T(8,128)(2,1)} %param.22) | copy-start | bytes 8294404
  24.4 3.9 %collective-permute-start.10 = (f32[2,16,240]{2,1,0:T(8,128)S(1)}, f32[2,16,240]{2,1,0:T(8,128)S(1)}, u32[]{:S(2)}, u32[]{:S(2)}) collective-permute-start(f32[2,16,240]{2,1,0:T(8,128)S(1)} %get-tuple-element.33.refs_4_), channel_id=1, source_target_pairs={{0,2},{1,3},{2,0},{3,1},{4,6},{5,7},{6,4},{7,5},{8,10},{9,11},{10,... | collective-permute-start | bytes 92168 | tf_op jit(solution)/shard_map/ppermute | solution.py:623
  24.4 30.5 %collective-permute-start.19 = (bf16[3,32,1920]{2,1,0:T(8,128)(2,1)S(1)}, bf16[3,32,1920]{2,1,0:T(8,128)(2,1)S(1)}, u32[]{:S(2)}, u32[]{:S(2)}) collective-permute-start(bf16[3,32,1920]{2,1,0:T(8,128)(2,1)S(1)} %collective-permute-done.18.refs_14_.refs_18_), channel_id=1, source_target_pairs={{0,1},{1,0},{2,3},{3,2},{4,5},{5,4},{6,7},{7,6},{8,9},{9,8},{10,11... | collective-permute-start | bytes 1105928 | tf_op jit(solution)/shard_map/ppermute | solution.py:626
  24.7 4.8 %collective-permute-start.11 = (f32[2,16,240]{2,1,0:T(8,128)S(1)}, f32[2,16,240]{2,1,0:T(8,128)S(1)}, u32[]{:S(2)}, u32[]{:S(2)}) collective-permute-start(f32[2,16,240]{2,1,0:T(8,128)S(1)} %get-tuple-element.33.refs_4_), channel_id=1, source_target_pairs={{0,4},{1,5},{2,6},{3,7},{4,0},{5,1},{6,2},{7,3},{8,12},{9,13},{10,... | collective-permute-start | bytes 92168 | tf_op jit(solution)/shard_map/ppermute | solution.py:623
  28.3 12.2 %collective-permute-start = (bf16[168,512]{1,0:T(8,128)(2,1)S(1)}, bf16[168,512]{1,0:T(8,128)(2,1)S(1)}, u32[]{:S(2)}, u32[]{:S(2)}) collective-permute-start(bf16[168,512]{1,0:T(8,128)(2,1)S(1)} %get-tuple-element.30), channel_id=1, source_target_pairs={{0,2},{1,3},{2,0},{3,1},{4,6},{5,7},{6,4},{7,5},{8,10},{9,11},{10,... | collective-permute-start | bytes 516104 | tf_op jit(solution)/shard_map/ppermute | solution.py:623
  29.5 5.8 %collective-permute-start.12 = (f32[2,16,240]{2,1,0:T(8,128)S(1)}, f32[2,16,240]{2,1,0:T(8,128)S(1)}, u32[]{:S(2)}, u32[]{:S(2)}) collective-permute-start(f32[2,16,240]{2,1,0:T(8,128)S(1)} %get-tuple-element.33.refs_4_), channel_id=1, source_target_pairs={{0,6},{1,7},{2,4},{3,5},{4,2},{5,3},{6,0},{7,1},{8,14},{9,15},{10,... | collective-permute-start | bytes 92168 | tf_op jit(solution)/shard_map/ppermute | solution.py:623
  35.3 1.2 collective-permute-start.13
  36.5 1.2 collective-permute-start.14
  37.7 1.2 collective-permute-start.15
  38.9 1.2 collective-permute-start.16
  40.1 14.8 %collective-permute-start.1 = (bf16[168,512]{1,0:T(8,128)(2,1)S(1)}, bf16[168,512]{1,0:T(8,128)(2,1)S(1)}, u32[]{:S(2)}, u32[]{:S(2)}) collective-permute-start(bf16[168,512]{1,0:T(8,128)(2,1)S(1)} %get-tuple-element.31), channel_id=1, source_target_pairs={{0,4},{1,5},{2,6},{3,7},{4,0},{5,1},{6,2},{7,3},{8,12},{9,13},{10,... | collective-permute-start | bytes 516104 | tf_op jit(solution)/shard_map/ppermute | solution.py:623
  40.6 14.4 %collective-permute-start.2 = (bf16[168,512]{1,0:T(8,128)(2,1)S(1)}, bf16[168,512]{1,0:T(8,128)(2,1)S(1)}, u32[]{:S(2)}, u32[]{:S(2)}) collective-permute-start(bf16[168,512]{1,0:T(8,128)(2,1)S(1)} %get-tuple-element.32), channel_id=1, source_target_pairs={{0,6},{1,7},{2,4},{3,5},{4,2},{5,3},{6,0},{7,1},{8,14},{9,15},{10,... | collective-permute-start | bytes 516104 | tf_op jit(solution)/shard_map/ppermute | solution.py:623
  55.0 21.8 %copy-start.2 = (bf16[1,1920,240]{1,2,0:T(8,128)(2,1)S(1)}, bf16[1,1920,240]{1,2,0:T(8,128)(2,1)}, u32[]{:S(2)}) copy-start(bf16[1,1920,240]{1,2,0:T(8,128)(2,1)} %param.25) | copy-start | bytes 2764804
  60.0 9.6 %collective-permute-start.20 = (bf16[512,128]{1,0:T(8,128)(2,1)S(1)}, bf16[512,128]{1,0:T(8,128)(2,1)S(1)}, u32[]{:S(2)}, u32[]{:S(2)}) collective-permute-start(bf16[512,128]{1,0:T(8,128)(2,1)S(1)} %get-tuple-element.35.refs_0_), channel_id=1, source_target_pairs={{0,2},{1,3},{2,0},{3,1},{4,6},{5,7},{6,4},{7,5},{8,10},{9,11},{10,... | collective-permute-start | bytes 393224 | tf_op jit(solution)/shard_map/ppermute | solution.py:623
  64.2 12.6 %collective-permute-start.21 = (bf16[512,128]{1,0:T(8,128)(2,1)S(1)}, bf16[512,128]{1,0:T(8,128)(2,1)S(1)}, u32[]{:S(2)}, u32[]{:S(2)}) collective-permute-start(bf16[512,128]{1,0:T(8,128)(2,1)S(1)} %get-tuple-element.35.refs_0_), channel_id=1, source_target_pairs={{0,4},{1,5},{2,6},{3,7},{4,0},{5,1},{6,2},{7,3},{8,12},{9,13},{10,... | collective-permute-start | bytes 393224 | tf_op jit(solution)/shard_map/ppermute | solution.py:623
  64.2 12.6 %collective-permute-start.22 = (bf16[512,128]{1,0:T(8,128)(2,1)S(1)}, bf16[512,128]{1,0:T(8,128)(2,1)S(1)}, u32[]{:S(2)}, u32[]{:S(2)}) collective-permute-start(bf16[512,128]{1,0:T(8,128)(2,1)S(1)} %get-tuple-element.35.refs_0_), channel_id=1, source_target_pairs={{0,6},{1,7},{2,4},{3,5},{4,2},{5,3},{6,0},{7,1},{8,14},{9,15},{10,... | collective-permute-start | bytes 393224 | tf_op jit(solution)/shard_map/ppermute | solution.py:623
  66.7 2.9 %collective-permute-start.24 = (f32[16,240]{1,0:T(8,128)S(1)}, f32[16,240]{1,0:T(8,128)S(1)}, u32[]{:S(2)}, u32[]{:S(2)}) collective-permute-start(f32[16,240]{1,0:T(8,128)S(1)} %get-tuple-element.37.refs_7_), channel_id=1, source_target_pairs={{0,1},{1,0},{2,3},{3,2},{4,5},{5,4},{6,7},{7,6},{8,9},{9,8},{10,11... | collective-permute-start | bytes 46088 | tf_op jit(solution)/shard_map/ppermute | solution.py:626
  77.8 6.0 %collective-permute-start.28 = (bf16[480,128]{1,0:T(8,128)(2,1)S(1)}, bf16[480,128]{1,0:T(8,128)(2,1)S(1)}, u32[]{:S(2)}, u32[]{:S(2)}) collective-permute-start(bf16[480,128]{1,0:T(8,128)(2,1)S(1)} %get-tuple-element.42), channel_id=1, source_target_pairs={{0,8},{8,16},{16,24},{24,0},{1,9},{9,17},{17,25},{25,1},{2,10},{10... | collective-permute-start | bytes 368648 | tf_op jit(solution)/shard_map/ppermute | solution.py:757
  79.6 10.2 %collective-permute-start.32 = (bf16[2,32,512]{2,1,0:T(8,128)(2,1)S(1)}, bf16[2,32,512]{2,1,0:T(8,128)(2,1)S(1)}, u32[]{:S(2)}, u32[]{:S(2)}) collective-permute-start(bf16[2,32,512]{2,1,0:T(8,128)(2,1)S(1)} %get-tuple-element.44), channel_id=1, source_target_pairs={{0,2},{1,3},{2,0},{3,1},{4,6},{5,7},{6,4},{7,5},{8,10},{9,11},{10,... | collective-permute-start | bytes 196616 | tf_op jit(solution)/shard_map/ppermute | solution.py:623
  83.8 19.0 %collective-permute-start.29 = (bf16[480,128]{1,0:T(8,128)(2,1)S(1)}, bf16[480,128]{1,0:T(8,128)(2,1)S(1)}, u32[]{:S(2)}, u32[]{:S(2)}) collective-permute-start(bf16[480,128]{1,0:T(8,128)(2,1)S(1)} %collective-permute-done.28.refs_0_), channel_id=1, source_target_pairs={{0,2},{1,3},{2,0},{3,1},{4,6},{5,7},{6,4},{7,5},{8,10},{9,11},{10,... | collective-permute-start | bytes 368648 | tf_op jit(solution)/shard_map/ppermute | solution.py:623
  86.3 16.6 %collective-permute-start.30 = (bf16[480,128]{1,0:T(8,128)(2,1)S(1)}, bf16[480,128]{1,0:T(8,128)(2,1)S(1)}, u32[]{:S(2)}, u32[]{:S(2)}) collective-permute-start(bf16[480,128]{1,0:T(8,128)(2,1)S(1)} %collective-permute-done.28.refs_0_), channel_id=1, source_target_pairs={{0,4},{1,5},{2,6},{3,7},{4,0},{5,1},{6,2},{7,3},{8,12},{9,13},{10,... | collective-permute-start | bytes 368648 | tf_op jit(solution)/shard_map/ppermute | solution.py:623
  86.3 16.6 %collective-permute-start.31 = (bf16[480,128]{1,0:T(8,128)(2,1)S(1)}, bf16[480,128]{1,0:T(8,128)(2,1)S(1)}, u32[]{:S(2)}, u32[]{:S(2)}) collective-permute-start(bf16[480,128]{1,0:T(8,128)(2,1)S(1)} %collective-permute-done.28.refs_0_), channel_id=1, source_target_pairs={{0,6},{1,7},{2,4},{3,5},{4,2},{5,3},{6,0},{7,1},{8,14},{9,15},{10,... | collective-permute-start | bytes 368648 | tf_op jit(solution)/shard_map/ppermute | solution.py:623
  88.7 14.2 %collective-permute-start.33 = (bf16[2,32,512]{2,1,0:T(8,128)(2,1)S(1)}, bf16[2,32,512]{2,1,0:T(8,128)(2,1)S(1)}, u32[]{:S(2)}, u32[]{:S(2)}) collective-permute-start(bf16[2,32,512]{2,1,0:T(8,128)(2,1)S(1)} %get-tuple-element.45), channel_id=1, source_target_pairs={{0,4},{1,5},{2,6},{3,7},{4,0},{5,1},{6,2},{7,3},{8,12},{9,13},{10,... | collective-permute-start | bytes 196616 | tf_op jit(solution)/shard_map/ppermute | solution.py:623
  89.7 13.1 %collective-permute-start.34 = (bf16[2,32,512]{2,1,0:T(8,128)(2,1)S(1)}, bf16[2,32,512]{2,1,0:T(8,128)(2,1)S(1)}, u32[]{:S(2)}, u32[]{:S(2)}) collective-permute-start(bf16[2,32,512]{2,1,0:T(8,128)(2,1)S(1)} %get-tuple-element.46), channel_id=1, source_target_pairs={{0,6},{1,7},{2,4},{3,5},{4,2},{5,3},{6,0},{7,1},{8,14},{9,15},{10,... | collective-permute-start | bytes 196616 | tf_op jit(solution)/shard_map/ppermute | solution.py:623
  107.3 8.0 %collective-permute-start.35 = (bf16[512,128]{1,0:T(8,128)(2,1)S(1)}, bf16[512,128]{1,0:T(8,128)(2,1)S(1)}, u32[]{:S(2)}, u32[]{:S(2)}) collective-permute-start(bf16[512,128]{1,0:T(8,128)(2,1)S(1)} %get-tuple-element.47.refs_0_), channel_id=1, source_target_pairs={{0,2},{1,3},{2,0},{3,1},{4,6},{5,7},{6,4},{7,5},{8,10},{9,11},{10,... | collective-permute-start | bytes 393224 | tf_op jit(solution)/shard_map/ppermute | solution.py:623
  108.6 12.8 %collective-permute-start.36 = (bf16[512,128]{1,0:T(8,128)(2,1)S(1)}, bf16[512,128]{1,0:T(8,128)(2,1)S(1)}, u32[]{:S(2)}, u32[]{:S(2)}) collective-permute-start(bf16[512,128]{1,0:T(8,128)(2,1)S(1)} %get-tuple-element.47.refs_0_), channel_id=1, source_target_pairs={{0,4},{1,5},{2,6},{3,7},{4,0},{5,1},{6,2},{7,3},{8,12},{9,13},{10,... | collective-permute-start | bytes 393224 | tf_op jit(solution)/shard_map/ppermute | solution.py:623
  109.2 12.2 %collective-permute-start.37 = (bf16[512,128]{1,0:T(8,128)(2,1)S(1)}, bf16[512,128]{1,0:T(8,128)(2,1)S(1)}, u32[]{:S(2)}, u32[]{:S(2)}) collective-permute-start(bf16[512,128]{1,0:T(8,128)(2,1)S(1)} %get-tuple-element.47.refs_0_), channel_id=1, source_target_pairs={{0,6},{1,7},{2,4},{3,5},{4,2},{5,3},{6,0},{7,1},{8,14},{9,15},{10,... | collective-permute-start | bytes 393224 | tf_op jit(solution)/shard_map/ppermute | solution.py:623
  111.7 14.0 %collective-permute-start.25 = (bf16[25,480]{1,0:T(8,128)(2,1)S(1)}, bf16[25,480]{1,0:T(8,128)(2,1)S(1)}, u32[]{:S(2)}, u32[]{:S(2)}) collective-permute-start(bf16[25,480]{1,0:T(8,128)(2,1)S(1)} %get-tuple-element.39), channel_id=1, source_target_pairs={{0,2},{1,3},{2,0},{3,1},{4,6},{5,7},{6,4},{7,5},{8,10},{9,11},{10,... | collective-permute-start | bytes 72008 | tf_op jit(solution)/shard_map/ppermute | solution.py:623
  112.1 16.1 %collective-permute-start.26 = (bf16[25,480]{1,0:T(8,128)(2,1)S(1)}, bf16[25,480]{1,0:T(8,128)(2,1)S(1)}, u32[]{:S(2)}, u32[]{:S(2)}) collective-permute-start(bf16[25,480]{1,0:T(8,128)(2,1)S(1)} %get-tuple-element.40), channel_id=1, source_target_pairs={{0,4},{1,5},{2,6},{3,7},{4,0},{5,1},{6,2},{7,3},{8,12},{9,13},{10,... | collective-permute-start | bytes 72008 | tf_op jit(solution)/shard_map/ppermute | solution.py:623
  115.2 12.9 %collective-permute-start.27 = (bf16[25,480]{1,0:T(8,128)(2,1)S(1)}, bf16[25,480]{1,0:T(8,128)(2,1)S(1)}, u32[]{:S(2)}, u32[]{:S(2)}) collective-permute-start(bf16[25,480]{1,0:T(8,128)(2,1)S(1)} %get-tuple-element.41), channel_id=1, source_target_pairs={{0,6},{1,7},{2,4},{3,5},{4,2},{5,3},{6,0},{7,1},{8,14},{9,15},{10,... | collective-permute-start | bytes 72008 | tf_op jit(solution)/shard_map/ppermute | solution.py:623
  122.4 5.8 %collective-permute-start.38 = (bf16[25,480]{1,0:T(8,128)(2,1)S(1)}, bf16[25,480]{1,0:T(8,128)(2,1)S(1)}, u32[]{:S(2)}, u32[]{:S(2)}) collective-permute-start(bf16[25,480]{1,0:T(8,128)(2,1)S(1)} %get-tuple-element.50), channel_id=1, source_target_pairs={{0,2},{1,3},{2,0},{3,1},{4,6},{5,7},{6,4},{7,5},{8,10},{9,11},{10,... | collective-permute-start | bytes 72008 | tf_op jit(solution)/shard_map/ppermute | solution.py:623
  125.7 4.8 %collective-permute-start.39 = (bf16[25,480]{1,0:T(8,128)(2,1)S(1)}, bf16[25,480]{1,0:T(8,128)(2,1)S(1)}, u32[]{:S(2)}, u32[]{:S(2)}) collective-permute-start(bf16[25,480]{1,0:T(8,128)(2,1)S(1)} %get-tuple-element.51), channel_id=1, source_target_pairs={{0,4},{1,5},{2,6},{3,7},{4,0},{5,1},{6,2},{7,3},{8,12},{9,13},{10,... | collective-permute-start | bytes 72008 | tf_op jit(solution)/shard_map/ppermute | solution.py:623
  125.7 5.7 %collective-permute-start.40 = (bf16[25,480]{1,0:T(8,128)(2,1)S(1)}, bf16[25,480]{1,0:T(8,128)(2,1)S(1)}, u32[]{:S(2)}, u32[]{:S(2)}) collective-permute-start(bf16[25,480]{1,0:T(8,128)(2,1)S(1)} %get-tuple-element.52), channel_id=1, source_target_pairs={{0,6},{1,7},{2,4},{3,5},{4,2},{5,3},{6,0},{7,1},{8,14},{9,15},{10,... | collective-permute-start | bytes 72008 | tf_op jit(solution)/shard_map/ppermute | solution.py:623

commit v2 on v1

--- a/solution.py
+++ b/solution.py
@@ -230,6 +230,8 @@
         self.ticks = probes.shape[1]
         self.images = codes.shape[1]
         self.resident = arrivals.shape[1]
+        self.used = self.pairs * self.tokens
+        self.dense = self.used + -self.used % 8
         self.lanes = self.pairs * SLOT
         self.classes = labels.shape[0]
         self.vocab, self.code_dim = prototypes.shape
@@ -271,6 +273,13 @@
     )
 
 
+def image_of(token, plan):
+    image = jnp.zeros(token.shape, jnp.int32)
+    for at in range(1, plan.pairs + 1):
+        image += (token >= at * plan.tokens).astype(jnp.int32)
+    return image
+
+
 def spread(rows, tick, plan):
     part = rows[tick * plan.pairs : (tick + 1) * plan.pairs, :]
     parts = []
@@ -282,22 +291,8 @@
     stacked = jnp.concatenate(parts, axis=0).astype(BF16)
     row = lax.broadcasted_iota(jnp.int32, (count, plan.lanes), 0)
     lane = lax.broadcasted_iota(jnp.int32, (count, plan.lanes), 1)
-    pick = (row % plan.pairs == lane // SLOT).astype(F32).astype(BF16)
+    pick = (row % plan.pairs == image_of(lane, plan)).astype(F32).astype(BF16)
     return dot(stacked, pick, ((0,), (0,)))
-
-
-def label_kernel(plan, labels, table, out, picked):
-    section_at = lax.axis_index("section")
-    place = lax.broadcasted_iota(jnp.int32, (1, plan.classes), 1)
-    row = 0
-    for core in range(2):
-        for tick in range(plan.ticks):
-            for pair in range(plan.pairs):
-                label = labels[tick - section_at + plan.section - 1, 2 * pair + core]
-                picked[row : row + 1, :] = (place == label).astype(F32)
-                row += 1
-    value = dot(picked[...].astype(BF16), table[...], ((1,), (1,)))
-    out[...] = (value / (1.0 + jnp.exp(-value))).astype(BF16)
 
 
 def modulation_kernel(plan, *refs):
@@ -322,61 +317,67 @@
             gate[...] = value
 
 
-def packed_rows(plan):
-    up = lambda rows: rows + -rows % 8
-    first = up(plan.pairs * plan.tokens)
-    second = first + up(plan.ctx)
-    return first, second, second + up(plan.ctx)
-
-
-def stored_kernel(plan, arrival, probes, answers, matrix, edge, *outs):
+def opening_kernel(
+    plan, labels, table, arrival, probes, answers, matrix, gain, active, edge, gained, *outs
+):
+    *outs, picked, arrived = outs
+    halo = pltpu.make_async_copy(matrix.at[:, : plan.halo, :], edge, arrived.at[0])
+    halo.start()
+    fetch = pltpu.make_async_copy(gain, gained, arrived.at[1])
+    fetch.start()
     pairs = plan.pairs
     pair = lax.axis_index("tp") // 2
+    section_at = lax.axis_index("section")
+    place = lax.broadcasted_iota(jnp.int32, (1, plan.classes), 1)
+    row = 0
+    for core in range(2):
+        for tick in range(plan.ticks):
+            for other in range(pairs):
+                label = labels[tick - section_at + plan.section - 1, 2 * other + core]
+                picked[row : row + 1, :] = (place == label).astype(F32)
+                row += 1
+    value = dot(picked[...].astype(BF16), table[...], ((1,), (1,)))
+    active[...] = (value / (1.0 + jnp.exp(-value))).astype(BF16)
+
     span = plan.most * plan.head_dim
-    key_at, value_at, _ = packed_rows(plan)
-    early, late = outs[:pairs], outs[pairs:]
-    edge[...] = matrix[:, : plan.halo, :]
+    first, stores = outs[0], outs[1:]
     wide = arrival[...].astype(F32)
-    wide_keys, wide_values = probes[...].astype(F32), answers[...].astype(F32)
-    keys = [wide_keys[:, tick, :] for tick in range(plan.ticks)]
-    values = [wide_values[:, tick, :] for tick in range(plan.ticks)]
     chunks = []
     for at in range(pairs):
         chunk = wide[:, at * plan.pair_cols : (at + 1) * plan.pair_cols]
         chunks.append(
             jnp.concatenate([chunk, jnp.zeros((plan.tokens, span - plan.pair_cols), F32)], axis=1)
         )
-    top = jnp.concatenate(
-        chunks + [jnp.zeros((key_at - pairs * plan.tokens, span), F32)], axis=0
+    first[...] = jnp.concatenate(
+        chunks + [jnp.zeros((first.shape[0] - pairs * plan.tokens, span), F32)], axis=0
     ).astype(BF16)
 
-    def cut(value, at, rows):
-        start = plan.starts[at] * plan.head_dim
-        reach = min(span, plan.width - start)
-        part = value[:, start : start + reach]
-        if reach < span:
-            part = jnp.concatenate([part, jnp.zeros((plan.ctx, span - reach), F32)], axis=1)
-        return jnp.concatenate([part, jnp.zeros((rows - plan.ctx, span), F32)], axis=0).astype(BF16)
-
-    for k in range(pairs):
-        early[k][:key_at, :] = top
-    for at in range(pairs):
-        pieces = [
-            cut(keys[0], at, value_at - key_at),
-            cut(values[0], at, value_at - key_at),
-            cut(keys[1], at, SLOT),
-            cut(values[1], at, SLOT),
-        ]
-        for k in range(pairs):
-
-            @pl.when((pair ^ k) == at)
-            def _(k=k, pieces=pieces):
-                early[k][key_at:value_at, :] = pieces[0]
-                early[k][value_at:, :] = pieces[1]
-                late[k][0], late[k][1] = pieces[2], pieces[3]
-
-
-def embed_kernel(plan, codes, table, resample, raising, placement, out, full):
+    for source, stored in enumerate((probes, answers)):
+        full = stored[...].astype(F32)
+        for tick in range(plan.ticks):
+            value = full[:, tick, :]
+            for at in range(pairs):
+                start = plan.starts[at] * plan.head_dim
+                reach = min(span, plan.width - start)
+                part = value[:, start : start + reach]
+                if reach < span:
+                    part = jnp.concatenate(
+                        [part, jnp.zeros((plan.ctx, span - reach), F32)], axis=1
+                    )
+                part = jnp.concatenate(
+                    [part, jnp.zeros((SLOT - plan.ctx, span), F32)], axis=0
+                ).astype(BF16)
+                for k in range(pairs):
+
+                    @pl.when((pair ^ k) == at)
+                    def _(k=k, part=part, tick=tick, source=source):
+                        stores[tick * pairs + k][source] = part
+
+    halo.wait()
+    fetch.wait()
+
+
+def embed_kernel(plan, codes, table, resample, raising, placement, out):
     place = lax.axis_index("tp")
     core, pair = place % 2, place // 2
     row = lax.broadcasted_iota(jnp.int32, (plan.vocab, plan.lanes), 0)
@@ -388,52 +389,45 @@
     picked = (row == jnp.concatenate(slots, axis=1)).astype(F32)
     looked = dot(table[...], picked, precision=lax.Precision.HIGHEST)
     mapped = dot(looked, resample[...], precision=lax.Precision.HIGHEST).astype(BF16)
-    fixed = placement[...].astype(F32)
     fixed = jnp.concatenate(
-        [fixed, jnp.zeros((SLOT - plan.tokens, plan.width), F32)], axis=0
-    )
-    fixed = jnp.concatenate([fixed] * plan.pairs, axis=0).T
-    full[...] = dot(raising[...], mapped, ((0,), (0,))) + fixed
-    start = pl.multiple_of(pair * plan.pair_cols, 16)
-    out[...] = full[pl.ds(start, plan.pair_cols), :].astype(BF16)
-
-
-def layer_kernel(plan, tick, *refs):
+        [placement[...].astype(F32)] * plan.pairs
+        + [jnp.zeros((plan.lanes - plan.used, plan.width), F32)],
+        axis=0,
+    )
+    full = (dot(mapped, raising[...], ((0,), (0,))) + fixed)[: plan.dense].astype(BF16)
+    for at in range(plan.pairs):
+
+        @pl.when(pair == at)
+        def _(at=at):
+            out[...] = full[:, at * plan.pair_cols : (at + 1) * plan.pair_cols]
+
+
+def project(plan, tick, pieces, shifts, weights, held, qkv, wide, scale_at, offset_at, turning):
     pairs = plan.pairs
-    pieces = refs[:pairs]
-    shifts = (refs[pairs : 2 * pairs], refs[2 * pairs : 3 * pairs])
-    stores = refs[3 * pairs : 4 * pairs] if tick else None
-    refs = refs[4 * pairs :] if tick else refs[3 * pairs :]
-    mine, other, near, far, sharp, attended, held = refs[:7]
-    wide, scale_at, offset_at, qkv, cached, *turning = refs[7:]
+    mine, other, near, far = weights
     half = plan.ticks * plan.pairs
     place = lax.axis_index("tp")
     core, pair = place % 2, place // 2
-    cols, pair_cols, dim, lanes = plan.cols, plan.pair_cols, plan.head_dim, plan.lanes
-
+    cols, pair_cols, lanes = plan.cols, plan.pair_cols, plan.lanes
+    turning[plan.used :, :] = jnp.zeros((lanes - plan.used, plan.width), F32)
     for k in range(pairs):
         at = pair ^ k
-        slot = pl.multiple_of(at * SLOT, SLOT)
-        if tick:
-            start = pl.multiple_of(at * pair_cols, 16)
-            wide[pl.ds(start, pair_cols), :] = pieces[k][...].astype(F32)
-            cached[0, pl.ds(slot, SLOT), :] = stores[k][0]
-            cached[1, pl.ds(slot, SLOT), :] = stores[k][1]
-        else:
-            key_at, value_at, _ = packed_rows(plan)
-            packed = pieces[k][...].astype(F32)
+        piece = pieces[k][...].astype(F32)
+        if tick == 0:
             chunks = [
-                packed[j * plan.tokens : (j + 1) * plan.tokens, :pair_cols] for j in range(pairs)
+                piece[j * plan.tokens : (j + 1) * plan.tokens, :pair_cols] for j in range(pairs)
             ]
-            turning[0][pl.ds(slot, SLOT), :] = jnp.concatenate(
-                [
-                    jnp.concatenate(chunks, axis=1),
-                    jnp.zeros((SLOT - plan.tokens, plan.width), F32),
-                ],
-                axis=0,
-            )
-            cached[0, pl.ds(slot, value_at - key_at), :] = packed[key_at:value_at].astype(BF16)
-            cached[1, pl.ds(slot, value_at - key_at), :] = packed[value_at:].astype(BF16)
+            piece = jnp.concatenate(chunks, axis=1)
+        for place_at in range(pairs):
+
+            @pl.when(at == place_at)
+            def _(place_at=place_at, piece=piece):
+                if tick:
+                    span = slice(place_at * pair_cols, (place_at + 1) * pair_cols)
+                    turning[: plan.used, span] = piece[: plan.used]
+                else:
+                    turning[place_at * plan.tokens : (place_at + 1) * plan.tokens, :] = piece
+
         for side in range(2):
             start = pl.multiple_of(
                 at * pair_cols + (core if side == 0 else 1 - core) * cols, 16
@@ -441,9 +435,8 @@
             own = pl.ds(pl.multiple_of(core * half, 8), half)
             scale_at[pl.ds(start, cols), :] = spread(shifts[side][k][0, own, :], tick, plan)
             offset_at[pl.ds(start, cols), :] = spread(shifts[side][k][1, own, :], tick, plan)
-    if tick == 0:
-        wide[...] = turning[0][...].T
-    value = wide[...]
+    value = turning[...].T
+    wide[...] = value
     average = jnp.sum(value, axis=0, keepdims=True) * (1.0 / plan.width)
     centred = value - average
     variance = jnp.sum(centred * centred, axis=0, keepdims=True) * (1.0 / plan.width)
@@ -463,13 +456,21 @@
         edge = jnp.where(core == 1, near[part].astype(F32), far[part].astype(F32)).astype(BF16)
         qkv[part, pair_cols : pair_cols + plan.halo, :] = dot(edge, tokens).astype(BF16)
 
+
+def attend(plan, stores, qkv, sharp, attended, cached, mixed_at):
+    pairs, pair_cols, dim, lanes = plan.pairs, plan.pair_cols, plan.head_dim, plan.lanes
+    pair = lax.axis_index("tp") // 2
+    for k in range(pairs):
+        slot = pl.multiple_of((pair ^ k) * SLOT, SLOT)
+        cached[0, pl.ds(slot, SLOT), :] = stores[k][0]
+        cached[1, pl.ds(slot, SLOT), :] = stores[k][1]
     head_at = first_head(pair, pair_cols, dim)
     begin = head_at * dim - pair * pair_cols
     row = lax.broadcasted_iota(jnp.int32, (lanes, lanes), 0)
     lane = lax.broadcasted_iota(jnp.int32, (lanes, lanes), 1)
-    same = row // SLOT == lane // SLOT
-    old_ok = same & (row % SLOT < plan.ctx)
-    new_ok = same & (row % SLOT < plan.tokens)
+    image = image_of(lane, plan)
+    old_ok = (row // SLOT == image) & (row % SLOT < plan.ctx)
+    new_ok = (image_of(row, plan) == image) & (row < plan.used)
     queries, keys, values, lifts, key_scales = [], [], [], [], []
     for head in range(plan.most):
         at = pl.ds(pl.multiple_of(begin + head * dim, 16), dim)
@@ -506,7 +507,40 @@
         total = 1.0 / (jnp.sum(old, axis=0, keepdims=True) + jnp.sum(new, axis=0, keepdims=True))
         old, new = (old * total).astype(BF16), (new * total).astype(BF16)
         mixed = dot(old_values[:, span], old, ((0,), (0,))) + dot(values[head], new)
-        attended[head * dim : (head + 1) * dim, :] = mixed.astype(BF16)
+        mixed_at[head * dim : (head + 1) * dim, :] = mixed
+    attended[...] = mixed_at[...].T[: plan.dense].astype(BF16)
+
+
+def project_kernel(plan, tick, *refs):
+    pairs = plan.pairs
+    project(
+        plan,
+        tick,
+        refs[:pairs],
+        (refs[pairs : 2 * pairs], refs[2 * pairs : 3 * pairs]),
+        refs[3 * pairs : 3 * pairs + 4],
+        *refs[3 * pairs + 4 :],
+    )
+
+
+def attend_kernel(plan, *refs):
+    attend(plan, refs[: plan.pairs], *refs[plan.pairs :])
+
+
+def layer_kernel(plan, tick, *refs):
+    pairs = plan.pairs
+    attended, held, cached, mixed_at, qkv, *rest = refs[4 * pairs + 5 :]
+    project(
+        plan,
+        tick,
+        refs[:pairs],
+        (refs[pairs : 2 * pairs], refs[2 * pairs : 3 * pairs]),
+        refs[4 * pairs : 4 * pairs + 4],
+        held,
+        qkv,
+        *rest,
+    )
+    attend(plan, refs[3 * pairs : 4 * pairs], qkv, refs[4 * pairs + 4], attended, cached, mixed_at)
 
 
 def return_kernel(plan, tick, *refs):
@@ -521,26 +555,21 @@
     joined, projected, gate = rest[-3:]
     place = lax.axis_index("tp")
     core, pair = place % 2, place // 2
-    cols, pair_cols, dim = plan.cols, plan.pair_cols, plan.head_dim
-    least = min(plan.counts)
+    cols, dim = plan.cols, plan.head_dim
     half = plan.ticks * pairs
+    joined[plan.used :, :] = jnp.zeros((plan.lanes - plan.used, plan.width), BF16)
     for k in range(pairs):
-        at = pair ^ k
-        start = first_head(at, pair_cols, dim)
-        count = first_head(at + 1, pair_cols, dim) - start
-        joined[pl.ds(pl.multiple_of(start * dim, 16), least * dim), :] = pieces[k][: least * dim, :]
-        for extra in range(least, plan.most):
-
-            @pl.when(count > extra)
-            def _(k=k, extra=extra, start=start):
-                joined[pl.ds(pl.multiple_of((start + extra) * dim, 16), dim), :] = pieces[k][
-                    extra * dim : (extra + 1) * dim, :
-                ]
+        for at in range(pairs):
+
+            @pl.when((pair ^ k) == at)
+            def _(k=k, at=at):
+                start, count = plan.starts[at] * dim, plan.counts[at] * dim
+                joined[: plan.dense, start : start + count] = pieces[k][:, :count]
 
     value = joined[...]
     for side, (matrix, gates) in enumerate(((mine, gate_mine), (other, gate_other))):
         start = pl.multiple_of((core if side == 0 else 1 - core) * cols, 16)
-        projected[pl.ds(start, cols), :] = dot(matrix[...], value).astype(BF16).astype(F32)
+        projected[pl.ds(start, cols), :] = dot(matrix[...], value, ((1,), (1,))).astype(BF16).astype(F32)
         gates = gates[pl.ds(pl.multiple_of(core * half, 8), half), :]
         gate[pl.ds(start, cols), :] = spread(gates, tick, plan)
     result = held[...].astype(F32) + gate[...] * projected[...]
@@ -550,11 +579,11 @@
 
             @pl.when((pair ^ k) == image)
             def _(k=k, image=image):
-                rows[k][...] = turned[image * SLOT : image * SLOT + plan.tokens, :].astype(BF16)
+                rows[k][...] = turned[image * plan.tokens : (image + 1) * plan.tokens, :].astype(BF16)
 
     if tick == 0:
         last = lax.axis_index("section") == plan.section - 1
-        onward[...] = jnp.where(last, entering[...].astype(F32), result).astype(BF16)
+        onward[...] = jnp.where(last, entering[...].astype(F32), turned[: plan.dense]).astype(BF16)
 
 
 def gather_kernel(plan, *refs):
@@ -571,8 +600,7 @@
                         tick * pairs + k
                     ][...].astype(F32)
 
-    for tick in range(plan.ticks):
-        out[tick] = full[tick].astype(BF16)
+    out[...] = jnp.stack([full[tick] for tick in range(plan.ticks)], axis=1).astype(BF16)
 
 
 def resample_blocks(plan):
@@ -594,7 +622,8 @@
     full = np.zeros((plan.lanes, plan.lanes), np.float32)
     for image in range(plan.pairs):
         at = image * SLOT
-        full[at : at + table.shape[1], at : at + table.shape[0]] = table.T
+        to = image * plan.tokens
+        full[at : at + table.shape[1], to : to + table.shape[0]] = table.T
     return full
 
 
@@ -628,18 +657,24 @@
     def around(value):
         return [value] + [swap(value, k) for k in range(1, pairs)]
 
-    def call(kernel, outs, scratch, values, scalars=(), loose=()):
+    def call(kernel, outs, scratch, values, scalars=(), loose=(), raw=(), space=pltpu.VMEM):
         ins = [
             pltpu.with_memory_space_constraint(
-                v, pltpu.HBM if i in scalars or i in loose else pltpu.VMEM
+                v, pltpu.HBM if i in (*scalars, *loose, *raw) else pltpu.VMEM
             )
             for i, v in enumerate(values)
         ]
         return pl.pallas_call(
             lambda *refs: kernel(plan, *refs),
-            out_shape=[pltpu.VMEM(shape, dtype) for shape, dtype in outs],
+            out_shape=[space(shape, dtype) for shape, dtype in outs],
             in_specs=[
-                pl.BlockSpec(memory_space=pltpu.SMEM if i in scalars else pltpu.VMEM)
+                pl.BlockSpec(
+                    memory_space=pltpu.SMEM
+                    if i in scalars
+                    else pl.ANY
+                    if i in raw
+                    else pltpu.VMEM
+                )
                 for i in range(len(values))
             ],
             out_specs=[pl.BlockSpec(memory_space=pltpu.VMEM)] * len(outs),
@@ -648,13 +683,29 @@
         )(*ins)
 
     span = plan.most * dim
-    (active,) = call(
-        label_kernel,
-        [((rows, cols), BF16)],
-        [pltpu.VMEM((rows, plan.classes), F32)],
-        [label_numbers, label_feature_rows.T],
+    qkv_mine = jnp.transpose(question_answer_operator[0], (1, 2, 0))
+    active, edge, mod_matrix, first, *stores = call(
+        opening_kernel,
+        [
+            ((rows, cols), BF16),
+            ((3, plan.halo, width), BF16),
+            ((3, cols, width), BF16),
+            ((plan.dense, span), BF16),
+        ]
+        + [((2, SLOT, span), BF16)] * (ticks * pairs),
+        [pltpu.VMEM((rows, plan.classes), F32), pltpu.SemaphoreType.DMA((2,))],
+        [
+            label_numbers,
+            label_feature_rows.T,
+            awaiting_arrivals[0, 0],
+            jnp.transpose(prior_resolution_probes[0, :, 0], (1, 0, 2)),
+            jnp.transpose(prior_resolution_answers[0, :, 0], (1, 0, 2)),
+            qkv_mine,
+            jnp.transpose(conditioned_gain_mapping[0], (1, 2, 0)),
+        ],
         (0,),
-        (1,),
+        (1, 2, 3, 4),
+        (5, 6),
     )
     active = around(active)
     active += [across(piece) for piece in active]
@@ -664,7 +715,7 @@
         [pltpu.VMEM((width, 128), BF16)],
         [
             *active,
-            jnp.transpose(conditioned_gain_mapping[0], (1, 2, 0)),
+            mod_matrix,
             jnp.transpose(conditioned_shift_addend, (1, 0, 2)),
         ],
     )
@@ -672,33 +723,21 @@
     shifts += [across(piece) for piece in shifts]
     gate_back = across(gate)
 
-    qkv_mine = jnp.transpose(question_answer_operator[0], (1, 2, 0))
     qkv_other = across(qkv_mine)
     out_mine = mixing_return_operator[0].T
     out_other = across(out_mine)
-    edge, *stores = call(
-        stored_kernel,
-        [((3, plan.halo, width), BF16)]
-        + [((packed_rows(plan)[2], span), BF16)] * pairs
-        + [((2, SLOT, span), BF16)] * pairs,
-        [],
-        [
-            awaiting_arrivals[0, 0],
-            jnp.transpose(prior_resolution_probes[0, :, 0], (1, 0, 2)),
-            jnp.transpose(prior_resolution_answers[0, :, 0], (1, 0, 2)),
-            qkv_mine,
-        ],
-        (),
-        (0, 1, 2),
-    )
     near = lax.ppermute(edge, "tp", [(2 * p + 2, 2 * p + 1) for p in range(pairs) if plan.need[p]])
     far = across(near)
-    pieces = [stores[0]] + [swap(stores[k], k) for k in range(1, pairs)]
-    later = [stores[pairs]] + [swap(stores[pairs + k], k) for k in range(1, pairs)]
+    pieces = around(first)
+    cached = [
+        [stores[tick * pairs]]
+        + [swap(stores[tick * pairs + k], k) for k in range(1, pairs)]
+        for tick in range(ticks)
+    ]
     (entering,) = call(
         embed_kernel,
-        [((pair_cols, lanes), BF16)],
-        [pltpu.VMEM((width, lanes), F32)],
+        [((plan.dense, pair_cols), BF16)],
+        [],
         [
             drawn_coarse_codes[0],
             discrete_prototypes.T,
@@ -706,40 +745,46 @@
             code_raising_operator,
             placement_tier_features,
         ],
-        (),
-        range(5),
     )
 
     emitted = []
     for tick in range(ticks):
-        scratch = [
-            pltpu.VMEM((width, lanes), F32),
-            pltpu.VMEM((width, lanes), F32),
-            pltpu.VMEM((width, lanes), F32),
-            pltpu.VMEM((3, plan.rows, lanes), BF16),
-            pltpu.VMEM((2, lanes, span), BF16),
-        ]
+        wide = [pltpu.VMEM((width, lanes), F32)] * 3 + [pltpu.VMEM((lanes, width), F32)]
+        heads_of = [pltpu.VMEM((2, lanes, span), BF16), pltpu.VMEM((span, lanes), F32)]
+        weights = [qkv_mine, qkv_other, near, far]
         if tick == 0:
-            scratch.append(pltpu.VMEM((lanes, width), F32))
-        values = [*pieces, *shifts] + (later if tick else [])
-        values += [qkv_mine, qkv_other, near, far, focus_sharpness_exponents]
-        attended, held = call(
-            lambda *refs, tick=tick: layer_kernel(refs[0], tick, *refs[1:]),
-            [((span, lanes), BF16), ((pair_cols, lanes), BF16)],
-            scratch,
-            values,
-            (len(values) - 1,),
-        )
+            held, qkv = call(
+                lambda *refs: project_kernel(refs[0], 0, *refs[1:]),
+                [((pair_cols, lanes), BF16), ((3, plan.rows, lanes), BF16)],
+                wide,
+                [*pieces, *shifts, *weights],
+            )
+            (attended,) = call(
+                attend_kernel,
+                [((plan.dense, span), BF16)],
+                heads_of,
+                [*cached[tick], qkv, focus_sharpness_exponents],
+                (pairs + 1,),
+            )
+        else:
+            values = [*pieces, *shifts, *cached[tick], *weights, focus_sharpness_exponents]
+            attended, held = call(
+                lambda *refs, tick=tick: layer_kernel(refs[0], tick, *refs[1:]),
+                [((plan.dense, span), BF16), ((pair_cols, lanes), BF16)],
+                heads_of + [pltpu.VMEM((3, plan.rows, lanes), BF16)] + wide,
+                values,
+                (len(values) - 1,),
+            )
         outs = [((plan.tokens, pair_cols), BF16)] * pairs
         extra = []
         if tick + 1 < ticks:
-            outs = [((pair_cols, lanes), BF16)] + outs
+            outs = [((plan.dense, pair_cols), BF16)] + outs
             extra = [entering]
         results = call(
             lambda *refs, tick=tick: return_kernel(refs[0], tick, *refs[1:]),
             outs,
             [
-                pltpu.VMEM((width, lanes), BF16),
+                pltpu.VMEM((lanes, width), BF16),
                 pltpu.VMEM((pair_cols, lanes), F32),
                 pltpu.VMEM((pair_cols, lanes), F32),
             ],
@@ -764,11 +809,12 @@
         emitted += [final[0]] + [swap(final[k], k) for k in range(1, pairs)]
     (out,) = call(
         gather_kernel,
-        [((ticks, plan.tokens, width), BF16)],
+        [((plan.tokens, ticks, width), BF16)],
         [pltpu.VMEM((ticks, plan.tokens, width), F32)],
         emitted,
-    )
-    return out[None, :, None]
+        space=pltpu.HBM,
+    )
+    return jnp.transpose(out, (1, 0, 2))[None, :, None]
 
 
 def local(*args):

time: 135 us -> 126 us (0.933)
  waiting for transfers between devices: 59.9 us -> 43.6 us
  starting transfers between devices: 49 us -> 58.8 us
  local copies, waits for them, and re-layouts: 4.4 us -> 0.04 us
  Pallas kernels: 19.4 us -> 21.6 us
    ppermute x27 -> x30, waiting for transfers between devices: 52 us -> 36.2 us  [swap(): return lax.ppermute(value, 'tp', [(g, g ^ 2 * k) for g in range(tp)])]
    ppermute x12, starting transfers between devices: 1.91 us -> 9.79 us  [across(): return lax.ppermute(value, 'tp', [(g, g ^ 1) for g in range(tp)])]
    unnamed x10 -> x16, local copies, waits for them, and re-layouts: 3.58 us -> 0.04 us
    pallas_call x9, Pallas kernels: 19.4 us -> 21.6 us  [call(): pl.pallas_call(lambda *refs: kernel(plan, *refs), out_shape=[space(shape,...]
    ppermute x27 -> x30, starting transfers between devices: 44.7 us -> 46.5 us  [swap(): return lax.ppermute(value, 'tp', [(g, g ^ 2 * k) for g in range(tp)])]
  transfers between devices with their start and end apart: 41 -> 44, of which waited for: 19 -> 18; matrix products, arithmetic and copies ran while one was open for 0% -> 0% of each run, Pallas kernels for 10% -> 11%
where the time goes in v2:
time: 126 us; the launch traced here: 124 us
  starting transfers between devices  58.8 us (47%)
  waiting for transfers between devices  43.6 us (35%)
  Pallas kernels  21.6 us (17%)
    ppermute x30, starting transfers between devices, swap(): return lax.ppermute(value, 'tp', [(g, g ^ 2 * k) for g in range(tp)])  46.5 us
    ppermute x30, waiting for transfers between devices, swap(): return lax.ppermute(value, 'tp', [(g, g ^ 2 * k) for g in range(tp)])  36.2 us
    pallas_call x9, Pallas kernels, call(): pl.pallas_call(lambda *refs: kernel(plan, *refs), out_shape=[space(shape,...  21.6 us
    ppermute x12, starting transfers between devices, across(): return lax.ppermute(value, 'tp', [(g, g ^ 1) for g in range(tp)])  9.79 us
    ppermute x12, waiting for transfers between devices, across(): return lax.ppermute(value, 'tp', [(g, g ^ 1) for g in range(tp)])  4.97 us
  transfers between devices with their start and end apart: 44, of which 18 were waited for; matrix products, arithmetic and copies ran while one was open for 0% of the time, Pallas kernels for 11%

profile of v2, /device:TPU:4, one launch (start us, length us, event | category | flops | bytes accessed | tf_op | source)
XLA Modules:
  0.0 124.3 jit_solution(12399214340117575081)
XLA Ops:
  0.5 3.3 %shard_map.145 = (bf16[16,240]{1,0:T(8,128)(2,1)S(1)}, bf16[3,32,1920]{2,1,0:T(8,128)(2,1)S(1)}, bf16[3,240,1920]{2,1,0:T(8,128)(2,1)S(1)}, bf16[104,512]{1,0:T(...) custom-call(s32[5,8]{1,0:T(8,128)} %refs_0_.1, ...), custom_call_target="tpu_custom_call" | custom-call | tf_op jit(solution)/shard_map/pallas_call | solution.py:667
  4.6 8.3 %collective-permute-start.22 = (bf16[3,32,1920]{2,1,0:T(8,128)(2,1)S(1)}, bf16[3,32,1920]{2,1,0:T(8,128)(2,1)S(1)}, u32[]{:S(2)}, u32[]{:S(2)}) collective-permute-start(bf16[3,32,1920]{2,1,0:T(8,128)(2,1)S(1)} %collective-permute-done.21.refs_14_.refs_18_), channel_id=1, source_target_pairs={{0,1},{1,0},{2,3},{3,2},{4,5},{5,4},{6,7},{7,6},{8,9},{9,8},{10,11... | collective-permute-start | bytes 1105928 | tf_op jit(solution)/shard_map/ppermute | solution.py:655
  12.9 2.6 %collective-permute-start.7 = (bf16[16,240]{1,0:T(8,128)(2,1)S(1)}, bf16[16,240]{1,0:T(8,128)(2,1)S(1)}, u32[]{:S(2)}, u32[]{:S(2)}) collective-permute-start(bf16[16,240]{1,0:T(8,128)(2,1)S(1)} %get-tuple-element.37.refs_0_), channel_id=1, source_target_pairs={{0,4},{1,5},{2,6},{3,7},{4,0},{5,1},{6,2},{7,3},{8,12},{9,13},{10,... | collective-permute-start | bytes 23048 | tf_op jit(solution)/shard_map/ppermute | solution.py:652
  15.5 1.1 collective-permute-done.6.refs_1_
  16.6 2.0 %collective-permute-start.8 = (bf16[16,240]{1,0:T(8,128)(2,1)S(1)}, bf16[16,240]{1,0:T(8,128)(2,1)S(1)}, u32[]{:S(2)}, u32[]{:S(2)}) collective-permute-start(bf16[16,240]{1,0:T(8,128)(2,1)S(1)} %get-tuple-element.37.refs_0_), channel_id=1, source_target_pairs={{0,6},{1,7},{2,4},{3,5},{4,2},{5,3},{6,0},{7,1},{8,14},{9,15},{10,... | collective-permute-start | bytes 23048 | tf_op jit(solution)/shard_map/ppermute | solution.py:652
  18.6 3.4 %collective-permute-done.8.refs_3_ = bf16[16,240]{1,0:T(8,128)(2,1)S(1)} collective-permute-done((bf16[16,240]{1,0:T(8,128)(2,1)S(1)}, bf16[16,240]{1,0:T(8,128)(2,1)S(1)}, u32[]{:S(2)}, u32[]{:S(2)}) %collective-permute-start.8) | collective-permute-done | bytes 7712 | tf_op jit(solution)/shard_map/ppermute | solution.py:652
  23.4 1.0 collective-permute-done.12.refs_7_
  24.4 1.2 shard_map.146
  25.6 2.6 %collective-permute-start.14 = (f32[2,16,240]{2,1,0:T(8,128)S(1)}, f32[2,16,240]{2,1,0:T(8,128)S(1)}, u32[]{:S(2)}, u32[]{:S(2)}) collective-permute-start(f32[2,16,240]{2,1,0:T(8,128)S(1)} %get-tuple-element.39.refs_4_), channel_id=1, source_target_pairs={{0,4},{1,5},{2,6},{3,7},{4,0},{5,1},{6,2},{7,3},{8,12},{9,13},{10,... | collective-permute-start | bytes 92168 | tf_op jit(solution)/shard_map/ppermute | solution.py:652
  28.1 1.7 %collective-permute-done.13.refs_5_ = f32[2,16,240]{2,1,0:T(8,128)S(1)} collective-permute-done((f32[2,16,240]{2,1,0:T(8,128)S(1)}, f32[2,16,240]{2,1,0:T(8,128)S(1)}, u32[]{:S(2)}, u32[]{:S(2)}) %collective-permute-start.13) | collective-permute-done | bytes 30752 | tf_op jit(solution)/shard_map/ppermute | solution.py:652
  29.8 2.0 %collective-permute-start.15 = (f32[2,16,240]{2,1,0:T(8,128)S(1)}, f32[2,16,240]{2,1,0:T(8,128)S(1)}, u32[]{:S(2)}, u32[]{:S(2)}) collective-permute-start(f32[2,16,240]{2,1,0:T(8,128)S(1)} %get-tuple-element.39.refs_4_), channel_id=1, source_target_pairs={{0,6},{1,7},{2,4},{3,5},{4,2},{5,3},{6,0},{7,1},{8,14},{9,15},{10,... | collective-permute-start | bytes 92168 | tf_op jit(solution)/shard_map/ppermute | solution.py:652
  31.9 3.7 %collective-permute-done.15.refs_7_ = f32[2,16,240]{2,1,0:T(8,128)S(1)} collective-permute-done((f32[2,16,240]{2,1,0:T(8,128)S(1)}, f32[2,16,240]{2,1,0:T(8,128)S(1)}, u32[]{:S(2)}, u32[]{:S(2)}) %collective-permute-start.15) | collective-permute-done | bytes 30752 | tf_op jit(solution)/shard_map/ppermute | solution.py:652
  35.6 1.2 collective-permute-done.17.refs_9_
  36.9 1.0 collective-permute-done.18.refs_10_
  38.1 1.0 collective-permute-done.19.refs_11_
  39.2 2.6 %collective-permute-start.4 = (bf16[104,512]{1,0:T(8,128)(2,1)S(1)}, bf16[104,512]{1,0:T(8,128)(2,1)S(1)}, u32[]{:S(2)}, u32[]{:S(2)}) collective-permute-start(bf16[104,512]{1,0:T(8,128)(2,1)S(1)} %get-tuple-element.36.refs_0_), channel_id=1, source_target_pairs={{0,4},{1,5},{2,6},{3,7},{4,0},{5,1},{6,2},{7,3},{8,12},{9,13},{10,... | collective-permute-start | bytes 319496 | tf_op jit(solution)/shard_map/ppermute | solution.py:652
  41.8 1.8 %collective-permute-start.5 = (bf16[104,512]{1,0:T(8,128)(2,1)S(1)}, bf16[104,512]{1,0:T(8,128)(2,1)S(1)}, u32[]{:S(2)}, u32[]{:S(2)}) collective-permute-start(bf16[104,512]{1,0:T(8,128)(2,1)S(1)} %get-tuple-element.36.refs_0_), channel_id=1, source_target_pairs={{0,6},{1,7},{2,4},{3,5},{4,2},{5,3},{6,0},{7,1},{8,14},{9,15},{10,... | collective-permute-start | bytes 319496 | tf_op jit(solution)/shard_map/ppermute | solution.py:652
  43.6 6.9 %collective-permute-done.4.refs_2_ = bf16[104,512]{1,0:T(8,128)(2,1)S(1)} collective-permute-done((bf16[104,512]{1,0:T(8,128)(2,1)S(1)}, bf16[104,512]{1,0:T(8,128)(2,1)S(1)}, u32[]{:S(2)}, u32[]{:S(2)}) %collective-permute-start.4) | collective-permute-done | bytes 106528 | tf_op jit(solution)/shard_map/ppermute | solution.py:652
  50.5 2.6 %collective-permute-start.1 = (bf16[2,32,512]{2,1,0:T(8,128)(2,1)S(1)}, bf16[2,32,512]{2,1,0:T(8,128)(2,1)S(1)}, u32[]{:S(2)}, u32[]{:S(2)}) collective-permute-start(bf16[2,32,512]{2,1,0:T(8,128)(2,1)S(1)} %get-tuple-element.34), channel_id=1, source_target_pairs={{0,4},{1,5},{2,6},{3,7},{4,0},{5,1},{6,2},{7,3},{8,12},{9,13},{10,... | collective-permute-start | bytes 196616 | tf_op jit(solution)/shard_map/ppermute | solution.py:652
  53.2 1.8 %collective-permute-start.2 = (bf16[2,32,512]{2,1,0:T(8,128)(2,1)S(1)}, bf16[2,32,512]{2,1,0:T(8,128)(2,1)S(1)}, u32[]{:S(2)}, u32[]{:S(2)}) collective-permute-start(bf16[2,32,512]{2,1,0:T(8,128)(2,1)S(1)} %get-tuple-element.35), channel_id=1, source_target_pairs={{0,6},{1,7},{2,4},{3,5},{4,2},{5,3},{6,0},{7,1},{8,14},{9,15},{10,... | collective-permute-start | bytes 196616 | tf_op jit(solution)/shard_map/ppermute | solution.py:652
  55.0 3.9 %shard_map.147 = (bf16[480,128]{1,0:T(8,128)(2,1)S(1)}, bf16[3,544,128]{2,1,0:T(8,128)(2,1)S(1)}) custom-call(bf16[104,512]{1,0:T(8,128)(2,1)S(1)} %get-tuple-element.36.refs_0_, bf16[104,512]{1,0:T(8,128)(2,1)S(1)} %collective-permute-done.3.refs_1_, bf16[104,512]{1,0:T(8,128)(2,1)S(1)} %collective-permute-done.4.refs_2_, ...), custom_call_target="tpu_custom_call" | custom-call | tf_op jit(solution)/shard_map/pallas_call | solution.py:667
  59.3 1.7 %shard_map.148.refs_0_ = bf16[104,512]{1,0:T(8,128)(2,1)S(1)} custom-call(bf16[2,32,512]{2,1,0:T(8,128)(2,1)S(1)} %get-tuple-element.32.refs_0_, bf16[2,32,512]{2,1,0:T(8,128)(2,1)S(1)} %collective-permute-done.refs_1_, bf16[2,32,512]{2,1,0:T(8,128)(2,1)S(1)} %collective-permute-done.1.refs_2_, bf16[2,32,512]{2,1,0:T(8,128)(2,1)S(1)} %collective-permute-done.2.refs_3_, ...), custom_call_target="tpu_custom_call" | custom-call | tf_op jit(solution)/shard_map/pallas_call | solution.py:667
  61.1 2.3 %collective-permute-start.24 = (bf16[104,512]{1,0:T(8,128)(2,1)S(1)}, bf16[104,512]{1,0:T(8,128)(2,1)S(1)}, u32[]{:S(2)}, u32[]{:S(2)}) collective-permute-start(bf16[104,512]{1,0:T(8,128)(2,1)S(1)} %shard_map.148.refs_0_), channel_id=1, source_target_pairs={{0,4},{1,5},{2,6},{3,7},{4,0},{5,1},{6,2},{7,3},{8,12},{9,13},{10,... | collective-permute-start | bytes 319496 | tf_op jit(solution)/shard_map/ppermute | solution.py:652
  63.5 2.0 %collective-permute-start.25 = (bf16[104,512]{1,0:T(8,128)(2,1)S(1)}, bf16[104,512]{1,0:T(8,128)(2,1)S(1)}, u32[]{:S(2)}, u32[]{:S(2)}) collective-permute-start(bf16[104,512]{1,0:T(8,128)(2,1)S(1)} %shard_map.148.refs_0_), channel_id=1, source_target_pairs={{0,6},{1,7},{2,4},{3,5},{4,2},{5,3},{6,0},{7,1},{8,14},{9,15},{10,... | collective-permute-start | bytes 319496 | tf_op jit(solution)/shard_map/ppermute | solution.py:652
  65.5 1.8 %shard_map.149.refs_9_ = bf16[104,480]{1,0:T(8,128)(2,1)S(1)} custom-call(s32[8,30]{1,0:T(8,128)S(1)} %bitcast.31, f32[32,4096]{1,0:T(8,128)S(1)} %bitcast.30, f32[128,128]{1,0:T(8,128)S(1)} %copy-done.5, bf16[32,1920]{1,0:T(8,128)(2,1)S(1)} %copy-done.3, bf16[25,1920]{1,0:T(8,128)(2,1)S(1)} %copy-done.4), custom_call_target="tpu_custom_call" | custom-call | tf_op jit(solution)/shard_map/pallas_call | solution.py:667
  67.4 3.8 %collective-permute-done.24.refs_2_ = bf16[104,512]{1,0:T(8,128)(2,1)S(1)} collective-permute-done((bf16[104,512]{1,0:T(8,128)(2,1)S(1)}, bf16[104,512]{1,0:T(8,128)(2,1)S(1)}, u32[]{:S(2)}, u32[]{:S(2)}) %collective-permute-start.24) | collective-permute-done | bytes 106528 | tf_op jit(solution)/shard_map/ppermute | solution.py:652
  71.2 1.3 %shard_map.150 = (bf16[104,480]{1,0:T(8,128)(2,1)S(1)}, bf16[25,480]{1,0:T(8,128)(2,1)S(1)}, bf16[25,480]{1,0:T(8,128)(2,1)S(1)}, bf16[25,480]{1,0:T(8,128)(2,1)S(1)}, bf16[25,480]{1,0:T(8,128)(2,1)S(1)}) custom-call(bf16[104,512]{1,0:T(8,128)(2,1)S(1)} %shard_map.148.refs_0_, bf16[104,512]{1,0:T(8,128)(2,1)S(1)} %collective-permute-done.23.refs_1_, ...), custom_call_target="tpu_custom_call" | custom-call | tf_op jit(solution)/shard_map/pallas_call | solution.py:667
  72.4 1.7 %collective-permute-start.31 = (bf16[104,480]{1,0:T(8,128)(2,1)S(1)}, bf16[104,480]{1,0:T(8,128)(2,1)S(1)}, u32[]{:S(2)}, u32[]{:S(2)}) collective-permute-start(bf16[104,480]{1,0:T(8,128)(2,1)S(1)} %get-tuple-element.48), channel_id=1, source_target_pairs={{0,8},{8,16},{16,24},{24,0},{1,9},{9,17},{17,25},{25,1},{2,10},{10... | collective-permute-start | bytes 299528 | tf_op jit(solution)/shard_map/ppermute | solution.py:802
  74.2 1.7 %collective-permute-start.35 = (bf16[2,32,512]{2,1,0:T(8,128)(2,1)S(1)}, bf16[2,32,512]{2,1,0:T(8,128)(2,1)S(1)}, u32[]{:S(2)}, u32[]{:S(2)}) collective-permute-start(bf16[2,32,512]{2,1,0:T(8,128)(2,1)S(1)} %get-tuple-element.50), channel_id=1, source_target_pairs={{0,2},{1,3},{2,0},{3,1},{4,6},{5,7},{6,4},{7,5},{8,10},{9,11},{10,... | collective-permute-start | bytes 196616 | tf_op jit(solution)/shard_map/ppermute | solution.py:652
  75.9 2.4 %collective-permute-done.31.refs_0_ = bf16[104,480]{1,0:T(8,128)(2,1)S(1)} collective-permute-done((bf16[104,480]{1,0:T(8,128)(2,1)S(1)}, bf16[104,480]{1,0:T(8,128)(2,1)S(1)}, u32[]{:S(2)}, u32[]{:S(2)}) %collective-permute-start.31) | collective-permute-done | bytes 99872 | tf_op jit(solution)/shard_map/ppermute | solution.py:802
  78.3 1.7 %collective-permute-start.32 = (bf16[104,480]{1,0:T(8,128)(2,1)S(1)}, bf16[104,480]{1,0:T(8,128)(2,1)S(1)}, u32[]{:S(2)}, u32[]{:S(2)}) collective-permute-start(bf16[104,480]{1,0:T(8,128)(2,1)S(1)} %collective-permute-done.31.refs_0_), channel_id=1, source_target_pairs={{0,2},{1,3},{2,0},{3,1},{4,6},{5,7},{6,4},{7,5},{8,10},{9,11},{10,... | collective-permute-start | bytes 299528 | tf_op jit(solution)/shard_map/ppermute | solution.py:652
  80.8 1.8 %collective-permute-start.34 = (bf16[104,480]{1,0:T(8,128)(2,1)S(1)}, bf16[104,480]{1,0:T(8,128)(2,1)S(1)}, u32[]{:S(2)}, u32[]{:S(2)}) collective-permute-start(bf16[104,480]{1,0:T(8,128)(2,1)S(1)} %collective-permute-done.31.refs_0_), channel_id=1, source_target_pairs={{0,6},{1,7},{2,4},{3,5},{4,2},{5,3},{6,0},{7,1},{8,14},{9,15},{10,... | collective-permute-start | bytes 299528 | tf_op jit(solution)/shard_map/ppermute | solution.py:652
  82.7 1.3 %collective-permute-start.36 = (bf16[2,32,512]{2,1,0:T(8,128)(2,1)S(1)}, bf16[2,32,512]{2,1,0:T(8,128)(2,1)S(1)}, u32[]{:S(2)}, u32[]{:S(2)}) collective-permute-start(bf16[2,32,512]{2,1,0:T(8,128)(2,1)S(1)} %get-tuple-element.51), channel_id=1, source_target_pairs={{0,4},{1,5},{2,6},{3,7},{4,0},{5,1},{6,2},{7,3},{8,12},{9,13},{10,... | collective-permute-start | bytes 196616 | tf_op jit(solution)/shard_map/ppermute | solution.py:652
  84.0 1.9 %collective-permute-start.37 = (bf16[2,32,512]{2,1,0:T(8,128)(2,1)S(1)}, bf16[2,32,512]{2,1,0:T(8,128)(2,1)S(1)}, u32[]{:S(2)}, u32[]{:S(2)}) collective-permute-start(bf16[2,32,512]{2,1,0:T(8,128)(2,1)S(1)} %get-tuple-element.52), channel_id=1, source_target_pairs={{0,6},{1,7},{2,4},{3,5},{4,2},{5,3},{6,0},{7,1},{8,14},{9,15},{10,... | collective-permute-start | bytes 196616 | tf_op jit(solution)/shard_map/ppermute | solution.py:652
  85.8 8.5 %collective-permute-done.36.refs_14_ = bf16[2,32,512]{2,1,0:T(8,128)(2,1)S(1)} collective-permute-done((bf16[2,32,512]{2,1,0:T(8,128)(2,1)S(1)}, bf16[2,32,512]{2,1,0:T(8,128)(2,1)S(1)}, u32[]{:S(2)}, u32[]{:S(2)}) %collective-permute-start.36) | collective-permute-done | bytes 65568 | tf_op jit(solution)/shard_map/ppermute | solution.py:652
  94.3 5.8 %shard_map.151 = (bf16[104,512]{1,0:T(8,128)(2,1)S(1)}, bf16[480,128]{1,0:T(8,128)(2,1)S(1)}) custom-call(bf16[104,480]{1,0:T(8,128)(2,1)S(1)} %collective-permute-done.31.refs_0_, bf16[104,480]{1,0:T(8,128)(2,1)S(1)} %collective-permute-done.32.refs_1_, bf16[104,480]{1,0:T(8,128)(2,1)S(1)} %collective-permute-done.33.refs_2_, ...), custom_call_target="tpu_custom_call" | custom-call | tf_op jit(solution)/shard_map/pallas_call | solution.py:667
  100.1 1.3 %collective-permute-start.38 = (bf16[104,512]{1,0:T(8,128)(2,1)S(1)}, bf16[104,512]{1,0:T(8,128)(2,1)S(1)}, u32[]{:S(2)}, u32[]{:S(2)}) collective-permute-start(bf16[104,512]{1,0:T(8,128)(2,1)S(1)} %get-tuple-element.53.refs_0_), channel_id=1, source_target_pairs={{0,2},{1,3},{2,0},{3,1},{4,6},{5,7},{6,4},{7,5},{8,10},{9,11},{10,... | collective-permute-start | bytes 319496 | tf_op jit(solution)/shard_map/ppermute | solution.py:652
  101.4 1.4 %collective-permute-start.39 = (bf16[104,512]{1,0:T(8,128)(2,1)S(1)}, bf16[104,512]{1,0:T(8,128)(2,1)S(1)}, u32[]{:S(2)}, u32[]{:S(2)}) collective-permute-start(bf16[104,512]{1,0:T(8,128)(2,1)S(1)} %get-tuple-element.53.refs_0_), channel_id=1, source_target_pairs={{0,4},{1,5},{2,6},{3,7},{4,0},{5,1},{6,2},{7,3},{8,12},{9,13},{10,... | collective-permute-start | bytes 319496 | tf_op jit(solution)/shard_map/ppermute | solution.py:652
  102.9 1.7 %collective-permute-start.40 = (bf16[104,512]{1,0:T(8,128)(2,1)S(1)}, bf16[104,512]{1,0:T(8,128)(2,1)S(1)}, u32[]{:S(2)}, u32[]{:S(2)}) collective-permute-start(bf16[104,512]{1,0:T(8,128)(2,1)S(1)} %get-tuple-element.53.refs_0_), channel_id=1, source_target_pairs={{0,6},{1,7},{2,4},{3,5},{4,2},{5,3},{6,0},{7,1},{8,14},{9,15},{10,... | collective-permute-start | bytes 319496 | tf_op jit(solution)/shard_map/ppermute | solution.py:652
  104.9 2.3 %collective-permute-start.29 = (bf16[25,480]{1,0:T(8,128)(2,1)S(1)}, bf16[25,480]{1,0:T(8,128)(2,1)S(1)}, u32[]{:S(2)}, u32[]{:S(2)}) collective-permute-start(bf16[25,480]{1,0:T(8,128)(2,1)S(1)} %get-tuple-element.46), channel_id=1, source_target_pairs={{0,4},{1,5},{2,6},{3,7},{4,0},{5,1},{6,2},{7,3},{8,12},{9,13},{10,... | collective-permute-start | bytes 72008 | tf_op jit(solution)/shard_map/ppermute | solution.py:652
  107.5 2.3 %collective-permute-start.30 = (bf16[25,480]{1,0:T(8,128)(2,1)S(1)}, bf16[25,480]{1,0:T(8,128)(2,1)S(1)}, u32[]{:S(2)}, u32[]{:S(2)}) collective-permute-start(bf16[25,480]{1,0:T(8,128)(2,1)S(1)} %get-tuple-element.47), channel_id=1, source_target_pairs={{0,6},{1,7},{2,4},{3,5},{4,2},{5,3},{6,0},{7,1},{8,14},{9,15},{10,... | collective-permute-start | bytes 72008 | tf_op jit(solution)/shard_map/ppermute | solution.py:652
  109.7 2.5 %collective-permute-done.39.refs_2_ = bf16[104,512]{1,0:T(8,128)(2,1)S(1)} collective-permute-done((bf16[104,512]{1,0:T(8,128)(2,1)S(1)}, bf16[104,512]{1,0:T(8,128)(2,1)S(1)}, u32[]{:S(2)}, u32[]{:S(2)}) %collective-permute-start.39) | collective-permute-done | bytes 106528 | tf_op jit(solution)/shard_map/ppermute | solution.py:652
  112.2 1.2 shard_map.152
  113.5 3.0 %collective-permute-start.41 = (bf16[25,480]{1,0:T(8,128)(2,1)S(1)}, bf16[25,480]{1,0:T(8,128)(2,1)S(1)}, u32[]{:S(2)}, u32[]{:S(2)}) collective-permute-start(bf16[25,480]{1,0:T(8,128)(2,1)S(1)} %get-tuple-element.56), channel_id=1, source_target_pairs={{0,2},{1,3},{2,0},{3,1},{4,6},{5,7},{6,4},{7,5},{8,10},{9,11},{10,... | collective-permute-start | bytes 72008 | tf_op jit(solution)/shard_map/ppermute | solution.py:652
  117.1 1.8 %collective-permute-start.43 = (bf16[25,480]{1,0:T(8,128)(2,1)S(1)}, bf16[25,480]{1,0:T(8,128)(2,1)S(1)}, u32[]{:S(2)}, u32[]{:S(2)}) collective-permute-start(bf16[25,480]{1,0:T(8,128)(2,1)S(1)} %get-tuple-element.58), channel_id=1, source_target_pairs={{0,6},{1,7},{2,4},{3,5},{4,2},{5,3},{6,0},{7,1},{8,14},{9,15},{10,... | collective-permute-start | bytes 72008 | tf_op jit(solution)/shard_map/ppermute | solution.py:652
  118.9 2.4 %collective-permute-done.42.refs_6_ = bf16[25,480]{1,0:T(8,128)(2,1)S(1)} collective-permute-done((bf16[25,480]{1,0:T(8,128)(2,1)S(1)}, bf16[25,480]{1,0:T(8,128)(2,1)S(1)}, u32[]{:S(2)}, u32[]{:S(2)}) %collective-permute-start.42) | collective-permute-done | bytes 24032 | tf_op jit(solution)/shard_map/ppermute | solution.py:652
  121.3 1.6 %collective-permute-done.43.refs_7_ = bf16[25,480]{1,0:T(8,128)(2,1)S(1)} collective-permute-done((bf16[25,480]{1,0:T(8,128)(2,1)S(1)}, bf16[25,480]{1,0:T(8,128)(2,1)S(1)}, u32[]{:S(2)}, u32[]{:S(2)}) %collective-permute-start.43) | collective-permute-done | bytes 24032 | tf_op jit(solution)/shard_map/ppermute | solution.py:652
  122.9 1.5 %shard_map.153 = bf16[25,2,1920]{2,1,0:T(2,128)(2,1)} custom-call(bf16[25,480]{1,0:T(8,128)(2,1)S(1)} %get-tuple-element.44.refs_0_, bf16[25,480]{1,0:T(8,128)(2,1)S(1)} %collective-permute-done.28.refs_1_, bf16[25,480]{1,0:T(8,128)(2,1)S(1)} %collective-permute-done.29.refs_2_, bf16[25,480]{1,0:T(8,128)(2,1)S(1)} %collective-permute-done.30.refs_3_, ...), custom_call_target="tpu_custom_call" | custom-call | tf_op jit(solution)/shard_map/pallas_call | solution.py:667
  (65 shorter events, 5.6 us)
Async XLA Ops:
  0.0 55.0 %collective-permute-start.20 = (bf16[3,240,1920]{2,1,0:T(8,128)(2,1)}, bf16[3,240,1920]{2,1,0:T(8,128)(2,1)S(1)}, u32[]{:S(2)}, u32[]{:S(2)}) collective-permute-start(bf16[3,240,1920]{2,1,0:T(8,128)(2,1)} %bitcast.23), channel_id=1, source_target_pairs={{0,1},{1,0},{2,3},{3,2},{4,5},{5,4},{6,7},{7,6},{8,9},{9,8},{10,11... | collective-permute-start | bytes 8294408 | tf_op jit(solution)/shard_map/ppermute | solution.py:655
  0.0 67.4 %collective-permute-start.26 = (bf16[240,1920]{1,0:T(8,128)(2,1)}, bf16[240,1920]{1,0:T(8,128)(2,1)S(1)}, u32[]{:S(2)}, u32[]{:S(2)}) collective-permute-start(bf16[240,1920]{1,0:T(8,128)(2,1)} %bitcast.27), channel_id=1, source_target_pairs={{0,1},{1,0},{2,3},{3,2},{4,5},{5,4},{6,7},{7,6},{8,9},{9,8},{10,11... | collective-permute-start | bytes 2764808 | tf_op jit(solution)/shard_map/ppermute | solution.py:655
  0.5 23.8 %copy-start.7 = (f32[1,3,240]{2,0,1:T(1,128)S(1)}, f32[1,3,240]{2,0,1:T(1,128)}, u32[]{:S(2)}) copy-start(f32[1,3,240]{2,0,1:T(1,128)} %param.23) | copy-start | bytes 8644
  3.8 51.3 %copy-start = (bf16[1,1920,3,240]{1,3,2,0:T(8,128)(2,1)S(1)}, bf16[1,1920,3,240]{1,3,2,0:T(8,128)(2,1)}, u32[]{:S(2)}) copy-start(bf16[1,1920,3,240]{1,3,2,0:T(8,128)(2,1)} %param.24) | copy-start | bytes 8294404
  3.8 0.8 collective-permute-start.21
  4.6 48.5 %collective-permute-start.22 = (bf16[3,32,1920]{2,1,0:T(8,128)(2,1)S(1)}, bf16[3,32,1920]{2,1,0:T(8,128)(2,1)S(1)}, u32[]{:S(2)}, u32[]{:S(2)}) collective-permute-start(bf16[3,32,1920]{2,1,0:T(8,128)(2,1)S(1)} %collective-permute-done.21.refs_14_.refs_18_), channel_id=1, source_target_pairs={{0,1},{1,0},{2,3},{3,2},{4,5},{5,4},{6,7},{7,6},{8,9},{9,8},{10,11... | collective-permute-start | bytes 1105928 | tf_op jit(solution)/shard_map/ppermute | solution.py:655
  12.9 3.7 %collective-permute-start.6 = (bf16[16,240]{1,0:T(8,128)(2,1)S(1)}, bf16[16,240]{1,0:T(8,128)(2,1)S(1)}, u32[]{:S(2)}, u32[]{:S(2)}) collective-permute-start(bf16[16,240]{1,0:T(8,128)(2,1)S(1)} %get-tuple-element.37.refs_0_), channel_id=1, source_target_pairs={{0,2},{1,3},{2,0},{3,1},{4,6},{5,7},{6,4},{7,5},{8,10},{9,11},{10,... | collective-permute-start | bytes 23048 | tf_op jit(solution)/shard_map/ppermute | solution.py:652
  12.9 5.7 %collective-permute-start.7 = (bf16[16,240]{1,0:T(8,128)(2,1)S(1)}, bf16[16,240]{1,0:T(8,128)(2,1)S(1)}, u32[]{:S(2)}, u32[]{:S(2)}) collective-permute-start(bf16[16,240]{1,0:T(8,128)(2,1)S(1)} %get-tuple-element.37.refs_0_), channel_id=1, source_target_pairs={{0,4},{1,5},{2,6},{3,7},{4,0},{5,1},{6,2},{7,3},{8,12},{9,13},{10,... | collective-permute-start | bytes 23048 | tf_op jit(solution)/shard_map/ppermute | solution.py:652
  16.6 5.4 %collective-permute-start.8 = (bf16[16,240]{1,0:T(8,128)(2,1)S(1)}, bf16[16,240]{1,0:T(8,128)(2,1)S(1)}, u32[]{:S(2)}, u32[]{:S(2)}) collective-permute-start(bf16[16,240]{1,0:T(8,128)(2,1)S(1)} %get-tuple-element.37.refs_0_), channel_id=1, source_target_pairs={{0,6},{1,7},{2,4},{3,5},{4,2},{5,3},{6,0},{7,1},{8,14},{9,15},{10,... | collective-permute-start | bytes 23048 | tf_op jit(solution)/shard_map/ppermute | solution.py:652
  18.6 3.4 %collective-permute-start.9 = (bf16[16,240]{1,0:T(8,128)(2,1)S(1)}, bf16[16,240]{1,0:T(8,128)(2,1)S(1)}, u32[]{:S(2)}, u32[]{:S(2)}) collective-permute-start(bf16[16,240]{1,0:T(8,128)(2,1)S(1)} %get-tuple-element.37.refs_0_), channel_id=1, source_target_pairs={{0,1},{1,0},{2,3},{3,2},{4,5},{5,4},{6,7},{7,6},{8,9},{9,8},{10,11... | collective-permute-start | bytes 23048 | tf_op jit(solution)/shard_map/ppermute | solution.py:655
  22.0 1.2 collective-permute-start.10
  22.0 1.3 %collective-permute-start.11 = (bf16[16,240]{1,0:T(8,128)(2,1)S(1)}, bf16[16,240]{1,0:T(8,128)(2,1)S(1)}, u32[]{:S(2)}, u32[]{:S(2)}) collective-permute-start(bf16[16,240]{1,0:T(8,128)(2,1)S(1)} %collective-permute-done.7.refs_2_), channel_id=1, source_target_pairs={{0,1},{1,0},{2,3},{3,2},{4,5},{5,4},{6,7},{7,6},{8,9},{9,8},{10,11... | collective-permute-start | bytes 23048 | tf_op jit(solution)/shard_map/ppermute | solution.py:655
  23.2 1.2 collective-permute-start.12
  25.5 4.3 %collective-permute-start.13 = (f32[2,16,240]{2,1,0:T(8,128)S(1)}, f32[2,16,240]{2,1,0:T(8,128)S(1)}, u32[]{:S(2)}, u32[]{:S(2)}) collective-permute-start(f32[2,16,240]{2,1,0:T(8,128)S(1)} %get-tuple-element.39.refs_4_), channel_id=1, source_target_pairs={{0,2},{1,3},{2,0},{3,1},{4,6},{5,7},{6,4},{7,5},{8,10},{9,11},{10,... | collective-permute-start | bytes 92168 | tf_op jit(solution)/shard_map/ppermute | solution.py:652
  25.6 6.3 %collective-permute-start.14 = (f32[2,16,240]{2,1,0:T(8,128)S(1)}, f32[2,16,240]{2,1,0:T(8,128)S(1)}, u32[]{:S(2)}, u32[]{:S(2)}) collective-permute-start(f32[2,16,240]{2,1,0:T(8,128)S(1)} %get-tuple-element.39.refs_4_), channel_id=1, source_target_pairs={{0,4},{1,5},{2,6},{3,7},{4,0},{5,1},{6,2},{7,3},{8,12},{9,13},{10,... | collective-permute-start | bytes 92168 | tf_op jit(solution)/shard_map/ppermute | solution.py:652
  29.8 5.7 %collective-permute-start.15 = (f32[2,16,240]{2,1,0:T(8,128)S(1)}, f32[2,16,240]{2,1,0:T(8,128)S(1)}, u32[]{:S(2)}, u32[]{:S(2)}) collective-permute-start(f32[2,16,240]{2,1,0:T(8,128)S(1)} %get-tuple-element.39.refs_4_), channel_id=1, source_target_pairs={{0,6},{1,7},{2,4},{3,5},{4,2},{5,3},{6,0},{7,1},{8,14},{9,15},{10,... | collective-permute-start | bytes 92168 | tf_op jit(solution)/shard_map/ppermute | solution.py:652
  31.8 3.7 %collective-permute-start.16 = (f32[2,16,240]{2,1,0:T(8,128)S(1)}, f32[2,16,240]{2,1,0:T(8,128)S(1)}, u32[]{:S(2)}, u32[]{:S(2)}) collective-permute-start(f32[2,16,240]{2,1,0:T(8,128)S(1)} %get-tuple-element.39.refs_4_), channel_id=1, source_target_pairs={{0,1},{1,0},{2,3},{3,2},{4,5},{5,4},{6,7},{7,6},{8,9},{9,8},{10,11... | collective-permute-start | bytes 92168 | tf_op jit(solution)/shard_map/ppermute | solution.py:655
  35.5 6.2 %collective-permute-start.3 = (bf16[104,512]{1,0:T(8,128)(2,1)S(1)}, bf16[104,512]{1,0:T(8,128)(2,1)S(1)}, u32[]{:S(2)}, u32[]{:S(2)}) collective-permute-start(bf16[104,512]{1,0:T(8,128)(2,1)S(1)} %get-tuple-element.36.refs_0_), channel_id=1, source_target_pairs={{0,2},{1,3},{2,0},{3,1},{4,6},{5,7},{6,4},{7,5},{8,10},{9,11},{10,... | collective-permute-start | bytes 319496 | tf_op jit(solution)/shard_map/ppermute | solution.py:652
  35.6 1.2 collective-permute-start.17
  36.8 1.2 collective-permute-start.18
  38.0 1.2 collective-permute-start.19
  39.2 11.3 %collective-permute-start.4 = (bf16[104,512]{1,0:T(8,128)(2,1)S(1)}, bf16[104,512]{1,0:T(8,128)(2,1)S(1)}, u32[]{:S(2)}, u32[]{:S(2)}) collective-permute-start(bf16[104,512]{1,0:T(8,128)(2,1)S(1)} %get-tuple-element.36.refs_0_), channel_id=1, source_target_pairs={{0,4},{1,5},{2,6},{3,7},{4,0},{5,1},{6,2},{7,3},{8,12},{9,13},{10,... | collective-permute-start | bytes 319496 | tf_op jit(solution)/shard_map/ppermute | solution.py:652
  41.8 8.8 %collective-permute-start.5 = (bf16[104,512]{1,0:T(8,128)(2,1)S(1)}, bf16[104,512]{1,0:T(8,128)(2,1)S(1)}, u32[]{:S(2)}, u32[]{:S(2)}) collective-permute-start(bf16[104,512]{1,0:T(8,128)(2,1)S(1)} %get-tuple-element.36.refs_0_), channel_id=1, source_target_pairs={{0,6},{1,7},{2,4},{3,5},{4,2},{5,3},{6,0},{7,1},{8,14},{9,15},{10,... | collective-permute-start | bytes 319496 | tf_op jit(solution)/shard_map/ppermute | solution.py:652
  50.5 8.4 %collective-permute-start = (bf16[2,32,512]{2,1,0:T(8,128)(2,1)S(1)}, bf16[2,32,512]{2,1,0:T(8,128)(2,1)S(1)}, u32[]{:S(2)}, u32[]{:S(2)}) collective-permute-start(bf16[2,32,512]{2,1,0:T(8,128)(2,1)S(1)} %get-tuple-element.33), channel_id=1, source_target_pairs={{0,2},{1,3},{2,0},{3,1},{4,6},{5,7},{6,4},{7,5},{8,10},{9,11},{10,... | collective-permute-start | bytes 196616 | tf_op jit(solution)/shard_map/ppermute | solution.py:652
  50.5 8.4 %collective-permute-start.1 = (bf16[2,32,512]{2,1,0:T(8,128)(2,1)S(1)}, bf16[2,32,512]{2,1,0:T(8,128)(2,1)S(1)}, u32[]{:S(2)}, u32[]{:S(2)}) collective-permute-start(bf16[2,32,512]{2,1,0:T(8,128)(2,1)S(1)} %get-tuple-element.34), channel_id=1, source_target_pairs={{0,4},{1,5},{2,6},{3,7},{4,0},{5,1},{6,2},{7,3},{8,12},{9,13},{10,... | collective-permute-start | bytes 196616 | tf_op jit(solution)/shard_map/ppermute | solution.py:652
  53.1 12.4 %copy-start.5 = (f32[128,128]{1,0:T(8,128)S(1)}, f32[128,128]{1,0:T(8,128)}, u32[]{:S(2)}) copy-start(f32[128,128]{1,0:T(8,128)} %constant.2.clone.refs_2_) | copy-start | bytes 196612
  53.2 18.0 %copy-start.1 = (bf16[1,1920,240]{1,2,0:T(8,128)(2,1)S(1)}, bf16[1,1920,240]{1,2,0:T(8,128)(2,1)}, u32[]{:S(2)}) copy-start(bf16[1,1920,240]{1,2,0:T(8,128)(2,1)} %param.25) | copy-start | bytes 2764804
  53.2 6.1 %collective-permute-start.2 = (bf16[2,32,512]{2,1,0:T(8,128)(2,1)S(1)}, bf16[2,32,512]{2,1,0:T(8,128)(2,1)S(1)}, u32[]{:S(2)}, u32[]{:S(2)}) collective-permute-start(bf16[2,32,512]{2,1,0:T(8,128)(2,1)S(1)} %get-tuple-element.35), channel_id=1, source_target_pairs={{0,6},{1,7},{2,4},{3,5},{4,2},{5,3},{6,0},{7,1},{8,14},{9,15},{10,... | collective-permute-start | bytes 196616 | tf_op jit(solution)/shard_map/ppermute | solution.py:652
  61.0 6.4 %collective-permute-start.23 = (bf16[104,512]{1,0:T(8,128)(2,1)S(1)}, bf16[104,512]{1,0:T(8,128)(2,1)S(1)}, u32[]{:S(2)}, u32[]{:S(2)}) collective-permute-start(bf16[104,512]{1,0:T(8,128)(2,1)S(1)} %shard_map.148.refs_0_), channel_id=1, source_target_pairs={{0,2},{1,3},{2,0},{3,1},{4,6},{5,7},{6,4},{7,5},{8,10},{9,11},{10,... | collective-permute-start | bytes 319496 | tf_op jit(solution)/shard_map/ppermute | solution.py:652
  61.1 10.1 %collective-permute-start.24 = (bf16[104,512]{1,0:T(8,128)(2,1)S(1)}, bf16[104,512]{1,0:T(8,128)(2,1)S(1)}, u32[]{:S(2)}, u32[]{:S(2)}) collective-permute-start(bf16[104,512]{1,0:T(8,128)(2,1)S(1)} %shard_map.148.refs_0_), channel_id=1, source_target_pairs={{0,4},{1,5},{2,6},{3,7},{4,0},{5,1},{6,2},{7,3},{8,12},{9,13},{10,... | collective-permute-start | bytes 319496 | tf_op jit(solution)/shard_map/ppermute | solution.py:652
  63.5 7.7 %collective-permute-start.25 = (bf16[104,512]{1,0:T(8,128)(2,1)S(1)}, bf16[104,512]{1,0:T(8,128)(2,1)S(1)}, u32[]{:S(2)}, u32[]{:S(2)}) collective-permute-start(bf16[104,512]{1,0:T(8,128)(2,1)S(1)} %shard_map.148.refs_0_), channel_id=1, source_target_pairs={{0,6},{1,7},{2,4},{3,5},{4,2},{5,3},{6,0},{7,1},{8,14},{9,15},{10,... | collective-permute-start | bytes 319496 | tf_op jit(solution)/shard_map/ppermute | solution.py:652
  65.5 1.9 %collective-permute-start.27 = (f32[16,240]{1,0:T(8,128)S(1)}, f32[16,240]{1,0:T(8,128)S(1)}, u32[]{:S(2)}, u32[]{:S(2)}) collective-permute-start(f32[16,240]{1,0:T(8,128)S(1)} %get-tuple-element.43.refs_7_), channel_id=1, source_target_pairs={{0,1},{1,0},{2,3},{3,2},{4,5},{5,4},{6,7},{7,6},{8,9},{9,8},{10,11... | collective-permute-start | bytes 46088 | tf_op jit(solution)/shard_map/ppermute | solution.py:655
  72.4 5.8 %collective-permute-start.31 = (bf16[104,480]{1,0:T(8,128)(2,1)S(1)}, bf16[104,480]{1,0:T(8,128)(2,1)S(1)}, u32[]{:S(2)}, u32[]{:S(2)}) collective-permute-start(bf16[104,480]{1,0:T(8,128)(2,1)S(1)} %get-tuple-element.48), channel_id=1, source_target_pairs={{0,8},{8,16},{16,24},{24,0},{1,9},{9,17},{17,25},{25,1},{2,10},{10... | collective-permute-start | bytes 299528 | tf_op jit(solution)/shard_map/ppermute | solution.py:802
  74.2 9.8 %collective-permute-start.35 = (bf16[2,32,512]{2,1,0:T(8,128)(2,1)S(1)}, bf16[2,32,512]{2,1,0:T(8,128)(2,1)S(1)}, u32[]{:S(2)}, u32[]{:S(2)}) collective-permute-start(bf16[2,32,512]{2,1,0:T(8,128)(2,1)S(1)} %get-tuple-element.50), channel_id=1, source_target_pairs={{0,2},{1,3},{2,0},{3,1},{4,6},{5,7},{6,4},{7,5},{8,10},{9,11},{10,... | collective-permute-start | bytes 196616 | tf_op jit(solution)/shard_map/ppermute | solution.py:652
  78.3 16.0 %collective-permute-start.32 = (bf16[104,480]{1,0:T(8,128)(2,1)S(1)}, bf16[104,480]{1,0:T(8,128)(2,1)S(1)}, u32[]{:S(2)}, u32[]{:S(2)}) collective-permute-start(bf16[104,480]{1,0:T(8,128)(2,1)S(1)} %collective-permute-done.31.refs_0_), channel_id=1, source_target_pairs={{0,2},{1,3},{2,0},{3,1},{4,6},{5,7},{6,4},{7,5},{8,10},{9,11},{10,... | collective-permute-start | bytes 299528 | tf_op jit(solution)/shard_map/ppermute | solution.py:652
  80.0 14.3 %collective-permute-start.33 = (bf16[104,480]{1,0:T(8,128)(2,1)S(1)}, bf16[104,480]{1,0:T(8,128)(2,1)S(1)}, u32[]{:S(2)}, u32[]{:S(2)}) collective-permute-start(bf16[104,480]{1,0:T(8,128)(2,1)S(1)} %collective-permute-done.31.refs_0_), channel_id=1, source_target_pairs={{0,4},{1,5},{2,6},{3,7},{4,0},{5,1},{6,2},{7,3},{8,12},{9,13},{10,... | collective-permute-start | bytes 299528 | tf_op jit(solution)/shard_map/ppermute | solution.py:652
  80.8 13.5 %collective-permute-start.34 = (bf16[104,480]{1,0:T(8,128)(2,1)S(1)}, bf16[104,480]{1,0:T(8,128)(2,1)S(1)}, u32[]{:S(2)}, u32[]{:S(2)}) collective-permute-start(bf16[104,480]{1,0:T(8,128)(2,1)S(1)} %collective-permute-done.31.refs_0_), channel_id=1, source_target_pairs={{0,6},{1,7},{2,4},{3,5},{4,2},{5,3},{6,0},{7,1},{8,14},{9,15},{10,... | collective-permute-start | bytes 299528 | tf_op jit(solution)/shard_map/ppermute | solution.py:652
  82.7 11.6 %collective-permute-start.36 = (bf16[2,32,512]{2,1,0:T(8,128)(2,1)S(1)}, bf16[2,32,512]{2,1,0:T(8,128)(2,1)S(1)}, u32[]{:S(2)}, u32[]{:S(2)}) collective-permute-start(bf16[2,32,512]{2,1,0:T(8,128)(2,1)S(1)} %get-tuple-element.51), channel_id=1, source_target_pairs={{0,4},{1,5},{2,6},{3,7},{4,0},{5,1},{6,2},{7,3},{8,12},{9,13},{10,... | collective-permute-start | bytes 196616 | tf_op jit(solution)/shard_map/ppermute | solution.py:652
  84.0 10.3 %collective-permute-start.37 = (bf16[2,32,512]{2,1,0:T(8,128)(2,1)S(1)}, bf16[2,32,512]{2,1,0:T(8,128)(2,1)S(1)}, u32[]{:S(2)}, u32[]{:S(2)}) collective-permute-start(bf16[2,32,512]{2,1,0:T(8,128)(2,1)S(1)} %get-tuple-element.52), channel_id=1, source_target_pairs={{0,6},{1,7},{2,4},{3,5},{4,2},{5,3},{6,0},{7,1},{8,14},{9,15},{10,... | collective-permute-start | bytes 196616 | tf_op jit(solution)/shard_map/ppermute | solution.py:652
  100.1 7.3 %collective-permute-start.38 = (bf16[104,512]{1,0:T(8,128)(2,1)S(1)}, bf16[104,512]{1,0:T(8,128)(2,1)S(1)}, u32[]{:S(2)}, u32[]{:S(2)}) collective-permute-start(bf16[104,512]{1,0:T(8,128)(2,1)S(1)} %get-tuple-element.53.refs_0_), channel_id=1, source_target_pairs={{0,2},{1,3},{2,0},{3,1},{4,6},{5,7},{6,4},{7,5},{8,10},{9,11},{10,... | collective-permute-start | bytes 319496 | tf_op jit(solution)/shard_map/ppermute | solution.py:652
  101.4 10.8 %collective-permute-start.39 = (bf16[104,512]{1,0:T(8,128)(2,1)S(1)}, bf16[104,512]{1,0:T(8,128)(2,1)S(1)}, u32[]{:S(2)}, u32[]{:S(2)}) collective-permute-start(bf16[104,512]{1,0:T(8,128)(2,1)S(1)} %get-tuple-element.53.refs_0_), channel_id=1, source_target_pairs={{0,4},{1,5},{2,6},{3,7},{4,0},{5,1},{6,2},{7,3},{8,12},{9,13},{10,... | collective-permute-start | bytes 319496 | tf_op jit(solution)/shard_map/ppermute | solution.py:652
  102.9 9.4 %collective-permute-start.40 = (bf16[104,512]{1,0:T(8,128)(2,1)S(1)}, bf16[104,512]{1,0:T(8,128)(2,1)S(1)}, u32[]{:S(2)}, u32[]{:S(2)}) collective-permute-start(bf16[104,512]{1,0:T(8,128)(2,1)S(1)} %get-tuple-element.53.refs_0_), channel_id=1, source_target_pairs={{0,6},{1,7},{2,4},{3,5},{4,2},{5,3},{6,0},{7,1},{8,14},{9,15},{10,... | collective-permute-start | bytes 319496 | tf_op jit(solution)/shard_map/ppermute | solution.py:652
  104.6 12.5 %collective-permute-start.28 = (bf16[25,480]{1,0:T(8,128)(2,1)S(1)}, bf16[25,480]{1,0:T(8,128)(2,1)S(1)}, u32[]{:S(2)}, u32[]{:S(2)}) collective-permute-start(bf16[25,480]{1,0:T(8,128)(2,1)S(1)} %get-tuple-element.45), channel_id=1, source_target_pairs={{0,2},{1,3},{2,0},{3,1},{4,6},{5,7},{6,4},{7,5},{8,10},{9,11},{10,... | collective-permute-start | bytes 72008 | tf_op jit(solution)/shard_map/ppermute | solution.py:652
  104.9 14.0 %collective-permute-start.29 = (bf16[25,480]{1,0:T(8,128)(2,1)S(1)}, bf16[25,480]{1,0:T(8,128)(2,1)S(1)}, u32[]{:S(2)}, u32[]{:S(2)}) collective-permute-start(bf16[25,480]{1,0:T(8,128)(2,1)S(1)} %get-tuple-element.46), channel_id=1, source_target_pairs={{0,4},{1,5},{2,6},{3,7},{4,0},{5,1},{6,2},{7,3},{8,12},{9,13},{10,... | collective-permute-start | bytes 72008 | tf_op jit(solution)/shard_map/ppermute | solution.py:652
  107.5 11.5 %collective-permute-start.30 = (bf16[25,480]{1,0:T(8,128)(2,1)S(1)}, bf16[25,480]{1,0:T(8,128)(2,1)S(1)}, u32[]{:S(2)}, u32[]{:S(2)}) collective-permute-start(bf16[25,480]{1,0:T(8,128)(2,1)S(1)} %get-tuple-element.47), channel_id=1, source_target_pairs={{0,6},{1,7},{2,4},{3,5},{4,2},{5,3},{6,0},{7,1},{8,14},{9,15},{10,... | collective-permute-start | bytes 72008 | tf_op jit(solution)/shard_map/ppermute | solution.py:652
  113.5 5.4 %collective-permute-start.41 = (bf16[25,480]{1,0:T(8,128)(2,1)S(1)}, bf16[25,480]{1,0:T(8,128)(2,1)S(1)}, u32[]{:S(2)}, u32[]{:S(2)}) collective-permute-start(bf16[25,480]{1,0:T(8,128)(2,1)S(1)} %get-tuple-element.56), channel_id=1, source_target_pairs={{0,2},{1,3},{2,0},{3,1},{4,6},{5,7},{6,4},{7,5},{8,10},{9,11},{10,... | collective-permute-start | bytes 72008 | tf_op jit(solution)/shard_map/ppermute | solution.py:652
  116.5 4.8 %collective-permute-start.42 = (bf16[25,480]{1,0:T(8,128)(2,1)S(1)}, bf16[25,480]{1,0:T(8,128)(2,1)S(1)}, u32[]{:S(2)}, u32[]{:S(2)}) collective-permute-start(bf16[25,480]{1,0:T(8,128)(2,1)S(1)} %get-tuple-element.57), channel_id=1, source_target_pairs={{0,4},{1,5},{2,6},{3,7},{4,0},{5,1},{6,2},{7,3},{8,12},{9,13},{10,... | collective-permute-start | bytes 72008 | tf_op jit(solution)/shard_map/ppermute | solution.py:652
  117.1 5.7 %collective-permute-start.43 = (bf16[25,480]{1,0:T(8,128)(2,1)S(1)}, bf16[25,480]{1,0:T(8,128)(2,1)S(1)}, u32[]{:S(2)}, u32[]{:S(2)}) collective-permute-start(bf16[25,480]{1,0:T(8,128)(2,1)S(1)} %get-tuple-element.58), channel_id=1, source_target_pairs={{0,6},{1,7},{2,4},{3,5},{4,2},{5,3},{6,0},{7,1},{8,14},{9,15},{10,... | collective-permute-start | bytes 72008 | tf_op jit(solution)/shard_map/ppermute | solution.py:652
  (4 other events, 49.5 us)

commit v3 on v2

--- a/solution.py
+++ b/solution.py
@@ -371,7 +371,7 @@
 
                     @pl.when((pair ^ k) == at)
                     def _(k=k, part=part, tick=tick, source=source):
-                        stores[tick * pairs + k][source] = part
+                        stores[k][2 * tick + source] = part
 
     halo.wait()
     fetch.wait()
@@ -409,23 +409,29 @@
     place = lax.axis_index("tp")
     core, pair = place % 2, place // 2
     cols, pair_cols, lanes = plan.cols, plan.pair_cols, plan.lanes
-    turning[plan.used :, :] = jnp.zeros((lanes - plan.used, plan.width), F32)
+    if tick == 0:
+        turning[plan.used :, :] = jnp.zeros((lanes - plan.used, plan.width), F32)
     for k in range(pairs):
         at = pair ^ k
-        piece = pieces[k][...].astype(F32)
-        if tick == 0:
+        if tick:
+            piece = jnp.concatenate(
+                [
+                    pieces[k][...].astype(F32),
+                    jnp.zeros((lanes - plan.dense, pair_cols), F32),
+                ],
+                axis=0,
+            )
+            wide[pl.ds(pl.multiple_of(at * pair_cols, 16), pair_cols), :] = piece.T
+        else:
+            piece = pieces[k][: plan.dense, :].astype(F32)
             chunks = [
                 piece[j * plan.tokens : (j + 1) * plan.tokens, :pair_cols] for j in range(pairs)
             ]
             piece = jnp.concatenate(chunks, axis=1)
-        for place_at in range(pairs):
-
-            @pl.when(at == place_at)
-            def _(place_at=place_at, piece=piece):
-                if tick:
-                    span = slice(place_at * pair_cols, (place_at + 1) * pair_cols)
-                    turning[: plan.used, span] = piece[: plan.used]
-                else:
+            for place_at in range(pairs):
+
+                @pl.when(at == place_at)
+                def _(place_at=place_at, piece=piece):
                     turning[place_at * plan.tokens : (place_at + 1) * plan.tokens, :] = piece
 
         for side in range(2):
@@ -435,8 +441,9 @@
             own = pl.ds(pl.multiple_of(core * half, 8), half)
             scale_at[pl.ds(start, cols), :] = spread(shifts[side][k][0, own, :], tick, plan)
             offset_at[pl.ds(start, cols), :] = spread(shifts[side][k][1, own, :], tick, plan)
-    value = turning[...].T
-    wide[...] = value
+    if tick == 0:
+        wide[...] = turning[...].T
+    value = wide[...]
     average = jnp.sum(value, axis=0, keepdims=True) * (1.0 / plan.width)
     centred = value - average
     variance = jnp.sum(centred * centred, axis=0, keepdims=True) * (1.0 / plan.width)
@@ -457,13 +464,13 @@
         qkv[part, pair_cols : pair_cols + plan.halo, :] = dot(edge, tokens).astype(BF16)
 
 
-def attend(plan, stores, qkv, sharp, attended, cached, mixed_at):
+def attend(plan, tick, stores, qkv, sharp, attended, cached, mixed_at):
     pairs, pair_cols, dim, lanes = plan.pairs, plan.pair_cols, plan.head_dim, plan.lanes
     pair = lax.axis_index("tp") // 2
     for k in range(pairs):
         slot = pl.multiple_of((pair ^ k) * SLOT, SLOT)
-        cached[0, pl.ds(slot, SLOT), :] = stores[k][0]
-        cached[1, pl.ds(slot, SLOT), :] = stores[k][1]
+        cached[0, pl.ds(slot, SLOT), :] = stores[k][2 * tick]
+        cached[1, pl.ds(slot, SLOT), :] = stores[k][2 * tick + 1]
     head_at = first_head(pair, pair_cols, dim)
     begin = head_at * dim - pair * pair_cols
     row = lax.broadcasted_iota(jnp.int32, (lanes, lanes), 0)
@@ -524,7 +531,7 @@
 
 
 def attend_kernel(plan, *refs):
-    attend(plan, refs[: plan.pairs], *refs[plan.pairs :])
+    attend(plan, 0, refs[: plan.pairs], *refs[plan.pairs :])
 
 
 def layer_kernel(plan, tick, *refs):
@@ -540,7 +547,7 @@
         qkv,
         *rest,
     )
-    attend(plan, refs[3 * pairs : 4 * pairs], qkv, refs[4 * pairs + 4], attended, cached, mixed_at)
+    attend(plan, tick, refs[3 * pairs : 4 * pairs], qkv, refs[4 * pairs + 4], attended, cached, mixed_at)
 
 
 def return_kernel(plan, tick, *refs):
@@ -692,7 +699,7 @@
             ((3, cols, width), BF16),
             ((plan.dense, span), BF16),
         ]
-        + [((2, SLOT, span), BF16)] * (ticks * pairs),
+        + [((2 * ticks, SLOT, span), BF16)] * pairs,
         [pltpu.VMEM((rows, plan.classes), F32), pltpu.SemaphoreType.DMA((2,))],
         [
             label_numbers,
@@ -729,11 +736,7 @@
     near = lax.ppermute(edge, "tp", [(2 * p + 2, 2 * p + 1) for p in range(pairs) if plan.need[p]])
     far = across(near)
     pieces = around(first)
-    cached = [
-        [stores[tick * pairs]]
-        + [swap(stores[tick * pairs + k], k) for k in range(1, pairs)]
-        for tick in range(ticks)
-    ]
+    stored = [stores[0]] + [swap(stores[k], k) for k in range(1, pairs)]
     (entering,) = call(
         embed_kernel,
         [((plan.dense, pair_cols), BF16)],
@@ -763,11 +766,11 @@
                 attend_kernel,
                 [((plan.dense, span), BF16)],
                 heads_of,
-                [*cached[tick], qkv, focus_sharpness_exponents],
+                [*stored, qkv, focus_sharpness_exponents],
                 (pairs + 1,),
             )
         else:
-            values = [*pieces, *shifts, *cached[tick], *weights, focus_sharpness_exponents]
+            values = [*pieces, *shifts, *stored, *weights, focus_sharpness_exponents]
             attended, held = call(
                 lambda *refs, tick=tick: layer_kernel(refs[0], tick, *refs[1:]),
                 [((plan.dense, span), BF16), ((pair_cols, lanes), BF16)],

time: 126 us -> 127 us (level)
  the two profiles are of different devices: /device:TPU:4 before, /device:TPU:0 now
where the time goes in v3:
time: 127 us
  starting transfers between devices  57.9 us (46%)
  waiting for transfers between devices  48 us (38%)
  Pallas kernels  20.6 us (16%)
    ppermute x27, starting transfers between devices, swap(): return lax.ppermute(value, 'tp', [(g, g ^ 2 * k) for g in range(tp)])  46.5 us
    ppermute x27, waiting for transfers between devices, swap(): return lax.ppermute(value, 'tp', [(g, g ^ 2 * k) for g in range(tp)])  37.7 us
    pallas_call x9, Pallas kernels, call(): pl.pallas_call(lambda *refs: kernel(plan, *refs), out_shape=[space(shape,...  20.6 us
    ppermute x12, starting transfers between devices, across(): return lax.ppermute(value, 'tp', [(g, g ^ 1) for g in range(tp)])  10.1 us
    ppermute x1, waiting for transfers between devices, paired(): lax.ppermute(results[0], 'section', [(s, (s + 1) % plan.section) for s in...  5.33 us
    ppermute x12, waiting for transfers between devices, across(): return lax.ppermute(value, 'tp', [(g, g ^ 1) for g in range(tp)])  4.97 us
  transfers between devices with their start and end apart: 41, of which 17 were waited for; matrix products, arithmetic and copies ran while one was open for 0% of the time, Pallas kernels for 10%

profile of v3, /device:TPU:0, one launch (start us, length us, event | category | flops | bytes accessed | tf_op | source)
XLA Modules:
  0.0 126.7 jit_solution(2091217312337241295)
XLA Ops:
  0.5 3.3 %shard_map.145 = (bf16[16,240]{1,0:T(8,128)(2,1)S(1)}, bf16[3,32,1920]{2,1,0:T(8,128)(2,1)S(1)}, bf16[3,240,1920]{2,1,0:T(8,128)(2,1)S(1)}, bf16[104,512]{1,0:T(...) custom-call(s32[5,8]{1,0:T(8,128)} %refs_0_.1, ...), custom_call_target="tpu_custom_call" | custom-call | tf_op jit(solution)/shard_map/pallas_call | solution.py:674
  3.8 0.8 collective-permute-start.21
  4.7 0.8 collective-permute-start.26
  5.5 7.8 %collective-permute-start.22 = (bf16[3,32,1920]{2,1,0:T(8,128)(2,1)S(1)}, bf16[3,32,1920]{2,1,0:T(8,128)(2,1)S(1)}, u32[]{:S(2)}, u32[]{:S(2)}) collective-permute-start(bf16[3,32,1920]{2,1,0:T(8,128)(2,1)S(1)} %collective-permute-done.21.refs_14_.refs_18_), channel_id=1, source_target_pairs={{0,1},{1,0},{2,3},{3,2},{4,5},{5,4},{6,7},{7,6},{8,9},{9,8},{10,11... | collective-permute-start | bytes 1105928 | tf_op jit(solution)/shard_map/ppermute | solution.py:662
  13.3 3.8 %collective-permute-start.7 = (bf16[16,240]{1,0:T(8,128)(2,1)S(1)}, bf16[16,240]{1,0:T(8,128)(2,1)S(1)}, u32[]{:S(2)}, u32[]{:S(2)}) collective-permute-start(bf16[16,240]{1,0:T(8,128)(2,1)S(1)} %get-tuple-element.33.refs_0_), channel_id=1, source_target_pairs={{0,4},{1,5},{2,6},{3,7},{4,0},{5,1},{6,2},{7,3},{8,12},{9,13},{10,... | collective-permute-start | bytes 23048 | tf_op jit(solution)/shard_map/ppermute | solution.py:659
  17.0 3.1 %collective-permute-start.8 = (bf16[16,240]{1,0:T(8,128)(2,1)S(1)}, bf16[16,240]{1,0:T(8,128)(2,1)S(1)}, u32[]{:S(2)}, u32[]{:S(2)}) collective-permute-start(bf16[16,240]{1,0:T(8,128)(2,1)S(1)} %get-tuple-element.33.refs_0_), channel_id=1, source_target_pairs={{0,6},{1,7},{2,4},{3,5},{4,2},{5,3},{6,0},{7,1},{8,14},{9,15},{10,... | collective-permute-start | bytes 23048 | tf_op jit(solution)/shard_map/ppermute | solution.py:659
  20.1 2.4 %collective-permute-done.8.refs_3_ = bf16[16,240]{1,0:T(8,128)(2,1)S(1)} collective-permute-done((bf16[16,240]{1,0:T(8,128)(2,1)S(1)}, bf16[16,240]{1,0:T(8,128)(2,1)S(1)}, u32[]{:S(2)}, u32[]{:S(2)}) %collective-permute-start.8) | collective-permute-done | bytes 7712 | tf_op jit(solution)/shard_map/ppermute | solution.py:659
  23.8 1.0 collective-permute-done.12.refs_7_
  24.8 1.2 shard_map.146
  26.4 3.3 %collective-permute-start.14 = (f32[2,16,240]{2,1,0:T(8,128)S(1)}, f32[2,16,240]{2,1,0:T(8,128)S(1)}, u32[]{:S(2)}, u32[]{:S(2)}) collective-permute-start(f32[2,16,240]{2,1,0:T(8,128)S(1)} %get-tuple-element.35.refs_4_), channel_id=1, source_target_pairs={{0,4},{1,5},{2,6},{3,7},{4,0},{5,1},{6,2},{7,3},{8,12},{9,13},{10,... | collective-permute-start | bytes 92168 | tf_op jit(solution)/shard_map/ppermute | solution.py:659
  29.9 3.4 %collective-permute-start.15 = (f32[2,16,240]{2,1,0:T(8,128)S(1)}, f32[2,16,240]{2,1,0:T(8,128)S(1)}, u32[]{:S(2)}, u32[]{:S(2)}) collective-permute-start(f32[2,16,240]{2,1,0:T(8,128)S(1)} %get-tuple-element.35.refs_4_), channel_id=1, source_target_pairs={{0,6},{1,7},{2,4},{3,5},{4,2},{5,3},{6,0},{7,1},{8,14},{9,15},{10,... | collective-permute-start | bytes 92168 | tf_op jit(solution)/shard_map/ppermute | solution.py:659
  33.4 2.3 %collective-permute-done.15.refs_7_ = f32[2,16,240]{2,1,0:T(8,128)S(1)} collective-permute-done((f32[2,16,240]{2,1,0:T(8,128)S(1)}, f32[2,16,240]{2,1,0:T(8,128)S(1)}, u32[]{:S(2)}, u32[]{:S(2)}) %collective-permute-start.15) | collective-permute-done | bytes 30752 | tf_op jit(solution)/shard_map/ppermute | solution.py:659
  35.7 1.2 collective-permute-done.17.refs_9_
  37.0 1.0 collective-permute-done.18.refs_10_
  38.2 1.0 collective-permute-done.19.refs_11_
  39.3 4.3 %collective-permute-start.4 = (bf16[104,512]{1,0:T(8,128)(2,1)S(1)}, bf16[104,512]{1,0:T(8,128)(2,1)S(1)}, u32[]{:S(2)}, u32[]{:S(2)}) collective-permute-start(bf16[104,512]{1,0:T(8,128)(2,1)S(1)} %get-tuple-element.32.refs_0_), channel_id=1, source_target_pairs={{0,4},{1,5},{2,6},{3,7},{4,0},{5,1},{6,2},{7,3},{8,12},{9,13},{10,... | collective-permute-start | bytes 319496 | tf_op jit(solution)/shard_map/ppermute | solution.py:659
  44.1 7.1 %collective-permute-done.4.refs_2_ = bf16[104,512]{1,0:T(8,128)(2,1)S(1)} collective-permute-done((bf16[104,512]{1,0:T(8,128)(2,1)S(1)}, bf16[104,512]{1,0:T(8,128)(2,1)S(1)}, u32[]{:S(2)}, u32[]{:S(2)}) %collective-permute-start.4) | collective-permute-done | bytes 106528 | tf_op jit(solution)/shard_map/ppermute | solution.py:659
  51.6 3.4 %collective-permute-start.1 = (bf16[4,32,512]{2,1,0:T(8,128)(2,1)S(1)}, bf16[4,32,512]{2,1,0:T(8,128)(2,1)S(1)}, u32[]{:S(2)}, u32[]{:S(2)}) collective-permute-start(bf16[4,32,512]{2,1,0:T(8,128)(2,1)S(1)} %get-tuple-element.30), channel_id=1, source_target_pairs={{0,4},{1,5},{2,6},{3,7},{4,0},{5,1},{6,2},{7,3},{8,12},{9,13},{10,... | collective-permute-start | bytes 393224 | tf_op jit(solution)/shard_map/ppermute | solution.py:659
  55.0 1.6 %collective-permute-start.2 = (bf16[4,32,512]{2,1,0:T(8,128)(2,1)S(1)}, bf16[4,32,512]{2,1,0:T(8,128)(2,1)S(1)}, u32[]{:S(2)}, u32[]{:S(2)}) collective-permute-start(bf16[4,32,512]{2,1,0:T(8,128)(2,1)S(1)} %get-tuple-element.31), channel_id=1, source_target_pairs={{0,6},{1,7},{2,4},{3,5},{4,2},{5,3},{6,0},{7,1},{8,14},{9,15},{10,... | collective-permute-start | bytes 393224 | tf_op jit(solution)/shard_map/ppermute | solution.py:659
  56.6 3.9 %shard_map.147 = (bf16[480,128]{1,0:T(8,128)(2,1)S(1)}, bf16[3,544,128]{2,1,0:T(8,128)(2,1)S(1)}) custom-call(bf16[104,512]{1,0:T(8,128)(2,1)S(1)} %get-tuple-element.32.refs_0_, bf16[104,512]{1,0:T(8,128)(2,1)S(1)} %collective-permute-done.3.refs_1_, bf16[104,512]{1,0:T(8,128)(2,1)S(1)} %collective-permute-done.4.refs_2_, ...), custom_call_target="tpu_custom_call" | custom-call | tf_op jit(solution)/shard_map/pallas_call | solution.py:674
  60.5 4.5 %collective-permute-done.1.refs_2_.refs_14_ = bf16[4,32,512]{2,1,0:T(8,128)(2,1)S(1)} collective-permute-done((bf16[4,32,512]{2,1,0:T(8,128)(2,1)S(1)}, bf16[4,32,512]{2,1,0:T(8,128)(2,1)S(1)}, u32[]{:S(2)}, u32[]{:S(2)}) %collective-permute-start.1) | collective-permute-done | bytes 131104 | tf_op jit(solution)/shard_map/ppermute | solution.py:659
  64.9 1.7 %shard_map.148.refs_0_ = bf16[104,512]{1,0:T(8,128)(2,1)S(1)} custom-call(bf16[4,32,512]{2,1,0:T(8,128)(2,1)S(1)} %get-tuple-element.28.refs_0_.refs_12_, bf16[4,32,512]{2,1,0:T(8,128)(2,1)S(1)} %collective-permute-done.refs_1_.refs_13_, bf16[4,32,512]{2,1,0:T(8,128)(2,1)S(1)} %collective-permute-done.1.refs_2_.refs_14_, ...), custom_call_target="tpu_custom_call" | custom-call | tf_op jit(solution)/shard_map/pallas_call | solution.py:674
  66.7 2.1 %collective-permute-start.23 = (bf16[104,512]{1,0:T(8,128)(2,1)S(1)}, bf16[104,512]{1,0:T(8,128)(2,1)S(1)}, u32[]{:S(2)}, u32[]{:S(2)}) collective-permute-start(bf16[104,512]{1,0:T(8,128)(2,1)S(1)} %shard_map.148.refs_0_), channel_id=1, source_target_pairs={{0,2},{1,3},{2,0},{3,1},{4,6},{5,7},{6,4},{7,5},{8,10},{9,11},{10,... | collective-permute-start | bytes 319496 | tf_op jit(solution)/shard_map/ppermute | solution.py:659
  68.8 0.8 collective-permute-start.24
  69.6 1.6 %collective-permute-start.25 = (bf16[104,512]{1,0:T(8,128)(2,1)S(1)}, bf16[104,512]{1,0:T(8,128)(2,1)S(1)}, u32[]{:S(2)}, u32[]{:S(2)}) collective-permute-start(bf16[104,512]{1,0:T(8,128)(2,1)S(1)} %shard_map.148.refs_0_), channel_id=1, source_target_pairs={{0,6},{1,7},{2,4},{3,5},{4,2},{5,3},{6,0},{7,1},{8,14},{9,15},{10,... | collective-permute-start | bytes 319496 | tf_op jit(solution)/shard_map/ppermute | solution.py:659
  71.2 1.8 %shard_map.149.refs_9_ = bf16[104,480]{1,0:T(8,128)(2,1)S(1)} custom-call(s32[8,30]{1,0:T(8,128)S(1)} %bitcast.31, f32[32,4096]{1,0:T(8,128)S(1)} %bitcast.30, f32[128,128]{1,0:T(8,128)S(1)} %copy-done.5, bf16[32,1920]{1,0:T(8,128)(2,1)S(1)} %copy-done.3, bf16[25,1920]{1,0:T(8,128)(2,1)S(1)} %copy-done.4), custom_call_target="tpu_custom_call" | custom-call | tf_op jit(solution)/shard_map/pallas_call | solution.py:674
  73.1 5.5 %collective-permute-done.24.refs_2_ = bf16[104,512]{1,0:T(8,128)(2,1)S(1)} collective-permute-done((bf16[104,512]{1,0:T(8,128)(2,1)S(1)}, bf16[104,512]{1,0:T(8,128)(2,1)S(1)}, u32[]{:S(2)}, u32[]{:S(2)}) %collective-permute-start.24) | collective-permute-done | bytes 106528 | tf_op jit(solution)/shard_map/ppermute | solution.py:659
  78.7 1.3 shard_map.150
  80.4 5.3 %collective-permute-done.31.refs_0_ = bf16[104,480]{1,0:T(8,128)(2,1)S(1)} collective-permute-done((bf16[104,480]{1,0:T(8,128)(2,1)S(1)}, bf16[104,480]{1,0:T(8,128)(2,1)S(1)}, u32[]{:S(2)}, u32[]{:S(2)}) %collective-permute-start.31) | collective-permute-done | bytes 99872 | tf_op jit(solution)/shard_map/ppermute | solution.py:805
  85.8 1.8 %collective-permute-start.32 = (bf16[104,480]{1,0:T(8,128)(2,1)S(1)}, bf16[104,480]{1,0:T(8,128)(2,1)S(1)}, u32[]{:S(2)}, u32[]{:S(2)}) collective-permute-start(bf16[104,480]{1,0:T(8,128)(2,1)S(1)} %collective-permute-done.31.refs_0_), channel_id=1, source_target_pairs={{0,2},{1,3},{2,0},{3,1},{4,6},{5,7},{6,4},{7,5},{8,10},{9,11},{10,... | collective-permute-start | bytes 299528 | tf_op jit(solution)/shard_map/ppermute | solution.py:659
  87.6 0.7 collective-permute-start.33
  88.3 1.9 %collective-permute-start.34 = (bf16[104,480]{1,0:T(8,128)(2,1)S(1)}, bf16[104,480]{1,0:T(8,128)(2,1)S(1)}, u32[]{:S(2)}, u32[]{:S(2)}) collective-permute-start(bf16[104,480]{1,0:T(8,128)(2,1)S(1)} %collective-permute-done.31.refs_0_), channel_id=1, source_target_pairs={{0,6},{1,7},{2,4},{3,5},{4,2},{5,3},{6,0},{7,1},{8,14},{9,15},{10,... | collective-permute-start | bytes 299528 | tf_op jit(solution)/shard_map/ppermute | solution.py:659
  90.8 5.9 %collective-permute-done.33.refs_2_ = bf16[104,480]{1,0:T(8,128)(2,1)S(1)} collective-permute-done((bf16[104,480]{1,0:T(8,128)(2,1)S(1)}, bf16[104,480]{1,0:T(8,128)(2,1)S(1)}, u32[]{:S(2)}, u32[]{:S(2)}) %collective-permute-start.33) | collective-permute-done | bytes 99872 | tf_op jit(solution)/shard_map/ppermute | solution.py:659
  96.7 4.7 %shard_map.151 = (bf16[104,512]{1,0:T(8,128)(2,1)S(1)}, bf16[480,128]{1,0:T(8,128)(2,1)S(1)}) custom-call(bf16[104,480]{1,0:T(8,128)(2,1)S(1)} %collective-permute-done.31.refs_0_, bf16[104,480]{1,0:T(8,128)(2,1)S(1)} %collective-permute-done.32.refs_1_, bf16[104,480]{1,0:T(8,128)(2,1)S(1)} %collective-permute-done.33.refs_2_, ...), custom_call_target="tpu_custom_call" | custom-call | tf_op jit(solution)/shard_map/pallas_call | solution.py:674
  101.3 1.8 %collective-permute-start.35 = (bf16[104,512]{1,0:T(8,128)(2,1)S(1)}, bf16[104,512]{1,0:T(8,128)(2,1)S(1)}, u32[]{:S(2)}, u32[]{:S(2)}) collective-permute-start(bf16[104,512]{1,0:T(8,128)(2,1)S(1)} %get-tuple-element.45.refs_0_), channel_id=1, source_target_pairs={{0,2},{1,3},{2,0},{3,1},{4,6},{5,7},{6,4},{7,5},{8,10},{9,11},{10,... | collective-permute-start | bytes 319496 | tf_op jit(solution)/shard_map/ppermute | solution.py:659
  103.1 1.0 collective-permute-start.36
  104.1 1.7 %collective-permute-start.37 = (bf16[104,512]{1,0:T(8,128)(2,1)S(1)}, bf16[104,512]{1,0:T(8,128)(2,1)S(1)}, u32[]{:S(2)}, u32[]{:S(2)}) collective-permute-start(bf16[104,512]{1,0:T(8,128)(2,1)S(1)} %get-tuple-element.45.refs_0_), channel_id=1, source_target_pairs={{0,6},{1,7},{2,4},{3,5},{4,2},{5,3},{6,0},{7,1},{8,14},{9,15},{10,... | collective-permute-start | bytes 319496 | tf_op jit(solution)/shard_map/ppermute | solution.py:659
  105.8 0.8 collective-permute-start.28
  106.6 1.9 %collective-permute-start.29 = (bf16[25,480]{1,0:T(8,128)(2,1)S(1)}, bf16[25,480]{1,0:T(8,128)(2,1)S(1)}, u32[]{:S(2)}, u32[]{:S(2)}) collective-permute-start(bf16[25,480]{1,0:T(8,128)(2,1)S(1)} %get-tuple-element.42), channel_id=1, source_target_pairs={{0,4},{1,5},{2,6},{3,7},{4,0},{5,1},{6,2},{7,3},{8,12},{9,13},{10,... | collective-permute-start | bytes 72008 | tf_op jit(solution)/shard_map/ppermute | solution.py:659
  108.5 1.7 %collective-permute-start.30 = (bf16[25,480]{1,0:T(8,128)(2,1)S(1)}, bf16[25,480]{1,0:T(8,128)(2,1)S(1)}, u32[]{:S(2)}, u32[]{:S(2)}) collective-permute-start(bf16[25,480]{1,0:T(8,128)(2,1)S(1)} %get-tuple-element.43), channel_id=1, source_target_pairs={{0,6},{1,7},{2,4},{3,5},{4,2},{5,3},{6,0},{7,1},{8,14},{9,15},{10,... | collective-permute-start | bytes 72008 | tf_op jit(solution)/shard_map/ppermute | solution.py:659
  110.2 4.8 %collective-permute-done.36.refs_2_ = bf16[104,512]{1,0:T(8,128)(2,1)S(1)} collective-permute-done((bf16[104,512]{1,0:T(8,128)(2,1)S(1)}, bf16[104,512]{1,0:T(8,128)(2,1)S(1)}, u32[]{:S(2)}, u32[]{:S(2)}) %collective-permute-start.36) | collective-permute-done | bytes 106528 | tf_op jit(solution)/shard_map/ppermute | solution.py:659
  115.0 1.2 shard_map.152
  116.2 2.2 %collective-permute-start.38 = (bf16[25,480]{1,0:T(8,128)(2,1)S(1)}, bf16[25,480]{1,0:T(8,128)(2,1)S(1)}, u32[]{:S(2)}, u32[]{:S(2)}) collective-permute-start(bf16[25,480]{1,0:T(8,128)(2,1)S(1)} %get-tuple-element.48), channel_id=1, source_target_pairs={{0,2},{1,3},{2,0},{3,1},{4,6},{5,7},{6,4},{7,5},{8,10},{9,11},{10,... | collective-permute-start | bytes 72008 | tf_op jit(solution)/shard_map/ppermute | solution.py:659
  118.4 1.1 collective-permute-start.39
  119.5 1.4 %collective-permute-start.40 = (bf16[25,480]{1,0:T(8,128)(2,1)S(1)}, bf16[25,480]{1,0:T(8,128)(2,1)S(1)}, u32[]{:S(2)}, u32[]{:S(2)}) collective-permute-start(bf16[25,480]{1,0:T(8,128)(2,1)S(1)} %get-tuple-element.50), channel_id=1, source_target_pairs={{0,6},{1,7},{2,4},{3,5},{4,2},{5,3},{6,0},{7,1},{8,14},{9,15},{10,... | collective-permute-start | bytes 72008 | tf_op jit(solution)/shard_map/ppermute | solution.py:659
  120.9 2.7 %collective-permute-done.39.refs_6_ = bf16[25,480]{1,0:T(8,128)(2,1)S(1)} collective-permute-done((bf16[25,480]{1,0:T(8,128)(2,1)S(1)}, bf16[25,480]{1,0:T(8,128)(2,1)S(1)}, u32[]{:S(2)}, u32[]{:S(2)}) %collective-permute-start.39) | collective-permute-done | bytes 24032 | tf_op jit(solution)/shard_map/ppermute | solution.py:659
  123.6 1.6 %collective-permute-done.40.refs_7_ = bf16[25,480]{1,0:T(8,128)(2,1)S(1)} collective-permute-done((bf16[25,480]{1,0:T(8,128)(2,1)S(1)}, bf16[25,480]{1,0:T(8,128)(2,1)S(1)}, u32[]{:S(2)}, u32[]{:S(2)}) %collective-permute-start.40) | collective-permute-done | bytes 24032 | tf_op jit(solution)/shard_map/ppermute | solution.py:659
  125.2 1.5 %shard_map.153 = bf16[25,2,1920]{2,1,0:T(2,128)(2,1)} custom-call(bf16[25,480]{1,0:T(8,128)(2,1)S(1)} %get-tuple-element.40.refs_0_, bf16[25,480]{1,0:T(8,128)(2,1)S(1)} %collective-permute-done.28.refs_1_, bf16[25,480]{1,0:T(8,128)(2,1)S(1)} %collective-permute-done.29.refs_2_, bf16[25,480]{1,0:T(8,128)(2,1)S(1)} %collective-permute-done.30.refs_3_, ...), custom_call_target="tpu_custom_call" | custom-call | tf_op jit(solution)/shard_map/pallas_call | solution.py:674
  (59 shorter events, 4.9 us)
Async XLA Ops:
  0.0 56.6 %collective-permute-start.20 = (bf16[3,240,1920]{2,1,0:T(8,128)(2,1)}, bf16[3,240,1920]{2,1,0:T(8,128)(2,1)S(1)}, u32[]{:S(2)}, u32[]{:S(2)}) collective-permute-start(bf16[3,240,1920]{2,1,0:T(8,128)(2,1)} %bitcast.23), channel_id=1, source_target_pairs={{0,1},{1,0},{2,3},{3,2},{4,5},{5,4},{6,7},{7,6},{8,9},{9,8},{10,11... | collective-permute-start | bytes 8294408 | tf_op jit(solution)/shard_map/ppermute | solution.py:662
  0.5 24.3 %copy-start.7 = (f32[1,3,240]{2,0,1:T(1,128)S(1)}, f32[1,3,240]{2,0,1:T(1,128)}, u32[]{:S(2)}) copy-start(f32[1,3,240]{2,0,1:T(1,128)} %param.23) | copy-start | bytes 8644
  3.8 52.7 %copy-start = (bf16[1,1920,3,240]{1,3,2,0:T(8,128)(2,1)S(1)}, bf16[1,1920,3,240]{1,3,2,0:T(8,128)(2,1)}, u32[]{:S(2)}) copy-start(bf16[1,1920,3,240]{1,3,2,0:T(8,128)(2,1)} %param.24) | copy-start | bytes 8294404
  3.8 1.7 %collective-permute-start.21 = (bf16[3,32,1920]{2,1,0:T(8,128)(2,1)S(1)}, bf16[3,32,1920]{2,1,0:T(8,128)(2,1)S(1)}, u32[]{:S(2)}, u32[]{:S(2)}) collective-permute-start(bf16[3,32,1920]{2,1,0:T(8,128)(2,1)S(1)} %get-tuple-element.36), channel_id=1, source_target_pairs={{2,1},{6,5},{10,9},{14,13},{18,17},{22,21},{26,25},{30,29}} | collective-permute-start | bytes 1105928 | tf_op jit(solution)/shard_map/ppermute | solution.py:736
  4.7 68.4 %collective-permute-start.26 = (bf16[240,1920]{1,0:T(8,128)(2,1)S(1)}, bf16[240,1920]{1,0:T(8,128)(2,1)S(1)}, u32[]{:S(2)}, u32[]{:S(2)}) collective-permute-start(bf16[240,1920]{1,0:T(8,128)(2,1)S(1)} %bitcast.27), channel_id=1, source_target_pairs={{0,1},{1,0},{2,3},{3,2},{4,5},{5,4},{6,7},{7,6},{8,9},{9,8},{10,11... | collective-permute-start | bytes 2764808 | tf_op jit(solution)/shard_map/ppermute | solution.py:662
  5.5 49.5 %collective-permute-start.22 = (bf16[3,32,1920]{2,1,0:T(8,128)(2,1)S(1)}, bf16[3,32,1920]{2,1,0:T(8,128)(2,1)S(1)}, u32[]{:S(2)}, u32[]{:S(2)}) collective-permute-start(bf16[3,32,1920]{2,1,0:T(8,128)(2,1)S(1)} %collective-permute-done.21.refs_14_.refs_18_), channel_id=1, source_target_pairs={{0,1},{1,0},{2,3},{3,2},{4,5},{5,4},{6,7},{7,6},{8,9},{9,8},{10,11... | collective-permute-start | bytes 1105928 | tf_op jit(solution)/shard_map/ppermute | solution.py:662
  13.3 3.8 %collective-permute-start.6 = (bf16[16,240]{1,0:T(8,128)(2,1)S(1)}, bf16[16,240]{1,0:T(8,128)(2,1)S(1)}, u32[]{:S(2)}, u32[]{:S(2)}) collective-permute-start(bf16[16,240]{1,0:T(8,128)(2,1)S(1)} %get-tuple-element.33.refs_0_), channel_id=1, source_target_pairs={{0,2},{1,3},{2,0},{3,1},{4,6},{5,7},{6,4},{7,5},{8,10},{9,11},{10,... | collective-permute-start | bytes 23048 | tf_op jit(solution)/shard_map/ppermute | solution.py:659
  13.3 6.8 %collective-permute-start.7 = (bf16[16,240]{1,0:T(8,128)(2,1)S(1)}, bf16[16,240]{1,0:T(8,128)(2,1)S(1)}, u32[]{:S(2)}, u32[]{:S(2)}) collective-permute-start(bf16[16,240]{1,0:T(8,128)(2,1)S(1)} %get-tuple-element.33.refs_0_), channel_id=1, source_target_pairs={{0,4},{1,5},{2,6},{3,7},{4,0},{5,1},{6,2},{7,3},{8,12},{9,13},{10,... | collective-permute-start | bytes 23048 | tf_op jit(solution)/shard_map/ppermute | solution.py:659
  17.0 5.4 %collective-permute-start.8 = (bf16[16,240]{1,0:T(8,128)(2,1)S(1)}, bf16[16,240]{1,0:T(8,128)(2,1)S(1)}, u32[]{:S(2)}, u32[]{:S(2)}) collective-permute-start(bf16[16,240]{1,0:T(8,128)(2,1)S(1)} %get-tuple-element.33.refs_0_), channel_id=1, source_target_pairs={{0,6},{1,7},{2,4},{3,5},{4,2},{5,3},{6,0},{7,1},{8,14},{9,15},{10,... | collective-permute-start | bytes 23048 | tf_op jit(solution)/shard_map/ppermute | solution.py:659
  20.1 2.4 %collective-permute-start.9 = (bf16[16,240]{1,0:T(8,128)(2,1)S(1)}, bf16[16,240]{1,0:T(8,128)(2,1)S(1)}, u32[]{:S(2)}, u32[]{:S(2)}) collective-permute-start(bf16[16,240]{1,0:T(8,128)(2,1)S(1)} %get-tuple-element.33.refs_0_), channel_id=1, source_target_pairs={{0,1},{1,0},{2,3},{3,2},{4,5},{5,4},{6,7},{7,6},{8,9},{9,8},{10,11... | collective-permute-start | bytes 23048 | tf_op jit(solution)/shard_map/ppermute | solution.py:662
  22.5 1.2 collective-permute-start.10
  22.5 1.3 %collective-permute-start.11 = (bf16[16,240]{1,0:T(8,128)(2,1)S(1)}, bf16[16,240]{1,0:T(8,128)(2,1)S(1)}, u32[]{:S(2)}, u32[]{:S(2)}) collective-permute-start(bf16[16,240]{1,0:T(8,128)(2,1)S(1)} %collective-permute-done.7.refs_2_), channel_id=1, source_target_pairs={{0,1},{1,0},{2,3},{3,2},{4,5},{5,4},{6,7},{7,6},{8,9},{9,8},{10,11... | collective-permute-start | bytes 23048 | tf_op jit(solution)/shard_map/ppermute | solution.py:662
  23.6 1.2 collective-permute-start.12
  26.0 3.9 %collective-permute-start.13 = (f32[2,16,240]{2,1,0:T(8,128)S(1)}, f32[2,16,240]{2,1,0:T(8,128)S(1)}, u32[]{:S(2)}, u32[]{:S(2)}) collective-permute-start(f32[2,16,240]{2,1,0:T(8,128)S(1)} %get-tuple-element.35.refs_4_), channel_id=1, source_target_pairs={{0,2},{1,3},{2,0},{3,1},{4,6},{5,7},{6,4},{7,5},{8,10},{9,11},{10,... | collective-permute-start | bytes 92168 | tf_op jit(solution)/shard_map/ppermute | solution.py:659
  26.4 7.0 %collective-permute-start.14 = (f32[2,16,240]{2,1,0:T(8,128)S(1)}, f32[2,16,240]{2,1,0:T(8,128)S(1)}, u32[]{:S(2)}, u32[]{:S(2)}) collective-permute-start(f32[2,16,240]{2,1,0:T(8,128)S(1)} %get-tuple-element.35.refs_4_), channel_id=1, source_target_pairs={{0,4},{1,5},{2,6},{3,7},{4,0},{5,1},{6,2},{7,3},{8,12},{9,13},{10,... | collective-permute-start | bytes 92168 | tf_op jit(solution)/shard_map/ppermute | solution.py:659
  29.9 5.7 %collective-permute-start.15 = (f32[2,16,240]{2,1,0:T(8,128)S(1)}, f32[2,16,240]{2,1,0:T(8,128)S(1)}, u32[]{:S(2)}, u32[]{:S(2)}) collective-permute-start(f32[2,16,240]{2,1,0:T(8,128)S(1)} %get-tuple-element.35.refs_4_), channel_id=1, source_target_pairs={{0,6},{1,7},{2,4},{3,5},{4,2},{5,3},{6,0},{7,1},{8,14},{9,15},{10,... | collective-permute-start | bytes 92168 | tf_op jit(solution)/shard_map/ppermute | solution.py:659
  33.4 2.3 %collective-permute-start.16 = (f32[2,16,240]{2,1,0:T(8,128)S(1)}, f32[2,16,240]{2,1,0:T(8,128)S(1)}, u32[]{:S(2)}, u32[]{:S(2)}) collective-permute-start(f32[2,16,240]{2,1,0:T(8,128)S(1)} %get-tuple-element.35.refs_4_), channel_id=1, source_target_pairs={{0,1},{1,0},{2,3},{3,2},{4,5},{5,4},{6,7},{7,6},{8,9},{9,8},{10,11... | collective-permute-start | bytes 92168 | tf_op jit(solution)/shard_map/ppermute | solution.py:662
  35.7 8.0 %collective-permute-start.3 = (bf16[104,512]{1,0:T(8,128)(2,1)S(1)}, bf16[104,512]{1,0:T(8,128)(2,1)S(1)}, u32[]{:S(2)}, u32[]{:S(2)}) collective-permute-start(bf16[104,512]{1,0:T(8,128)(2,1)S(1)} %get-tuple-element.32.refs_0_), channel_id=1, source_target_pairs={{0,2},{1,3},{2,0},{3,1},{4,6},{5,7},{6,4},{7,5},{8,10},{9,11},{10,... | collective-permute-start | bytes 319496 | tf_op jit(solution)/shard_map/ppermute | solution.py:659
  35.7 1.2 collective-permute-start.17
  36.9 1.2 collective-permute-start.18
  38.1 1.2 collective-permute-start.19
  39.3 12.0 %collective-permute-start.4 = (bf16[104,512]{1,0:T(8,128)(2,1)S(1)}, bf16[104,512]{1,0:T(8,128)(2,1)S(1)}, u32[]{:S(2)}, u32[]{:S(2)}) collective-permute-start(bf16[104,512]{1,0:T(8,128)(2,1)S(1)} %get-tuple-element.32.refs_0_), channel_id=1, source_target_pairs={{0,4},{1,5},{2,6},{3,7},{4,0},{5,1},{6,2},{7,3},{8,12},{9,13},{10,... | collective-permute-start | bytes 319496 | tf_op jit(solution)/shard_map/ppermute | solution.py:659
  43.6 7.9 %collective-permute-start.5 = (bf16[104,512]{1,0:T(8,128)(2,1)S(1)}, bf16[104,512]{1,0:T(8,128)(2,1)S(1)}, u32[]{:S(2)}, u32[]{:S(2)}) collective-permute-start(bf16[104,512]{1,0:T(8,128)(2,1)S(1)} %get-tuple-element.32.refs_0_), channel_id=1, source_target_pairs={{0,6},{1,7},{2,4},{3,5},{4,2},{5,3},{6,0},{7,1},{8,14},{9,15},{10,... | collective-permute-start | bytes 319496 | tf_op jit(solution)/shard_map/ppermute | solution.py:659
  51.3 9.2 %collective-permute-start = (bf16[4,32,512]{2,1,0:T(8,128)(2,1)S(1)}, bf16[4,32,512]{2,1,0:T(8,128)(2,1)S(1)}, u32[]{:S(2)}, u32[]{:S(2)}) collective-permute-start(bf16[4,32,512]{2,1,0:T(8,128)(2,1)S(1)} %get-tuple-element.29), channel_id=1, source_target_pairs={{0,2},{1,3},{2,0},{3,1},{4,6},{5,7},{6,4},{7,5},{8,10},{9,11},{10,... | collective-permute-start | bytes 393224 | tf_op jit(solution)/shard_map/ppermute | solution.py:659
  51.6 13.4 %collective-permute-start.1 = (bf16[4,32,512]{2,1,0:T(8,128)(2,1)S(1)}, bf16[4,32,512]{2,1,0:T(8,128)(2,1)S(1)}, u32[]{:S(2)}, u32[]{:S(2)}) collective-permute-start(bf16[4,32,512]{2,1,0:T(8,128)(2,1)S(1)} %get-tuple-element.30), channel_id=1, source_target_pairs={{0,4},{1,5},{2,6},{3,7},{4,0},{5,1},{6,2},{7,3},{8,12},{9,13},{10,... | collective-permute-start | bytes 393224 | tf_op jit(solution)/shard_map/ppermute | solution.py:659
  55.0 16.2 %copy-start.2 = (f32[4096,32]{0,1:T(8,128)S(1)}, f32[4096,32]{0,1:T(8,128)}, u32[]{:S(2)}) copy-start(f32[4096,32]{0,1:T(8,128)} %param.18) | copy-start | bytes 1572868
  55.0 16.2 %copy-start.3 = (bf16[32,1920]{1,0:T(8,128)(2,1)S(1)}, bf16[32,1920]{1,0:T(8,128)(2,1)}, u32[]{:S(2)}) copy-start(bf16[32,1920]{1,0:T(8,128)(2,1)} %refs_3_.1) | copy-start | bytes 368644
  55.0 16.2 %copy-start.4 = (bf16[25,1920]{1,0:T(8,128)(2,1)S(1)}, bf16[25,1920]{1,0:T(8,128)(2,1)}, u32[]{:S(2)}) copy-start(bf16[25,1920]{1,0:T(8,128)(2,1)} %refs_4_.1) | copy-start | bytes 288004
  55.0 16.2 %copy-start.5 = (f32[128,128]{1,0:T(8,128)S(1)}, f32[128,128]{1,0:T(8,128)}, u32[]{:S(2)}) copy-start(f32[128,128]{1,0:T(8,128)} %constant.2.clone.refs_2_) | copy-start | bytes 196612
  55.0 16.2 %copy-start.6 = (s32[1,8,30]{2,1,0:T(8,128)S(1)}, s32[1,8,30]{2,1,0:T(8,128)}, u32[]{:S(2)}) copy-start(s32[1,8,30]{2,1,0:T(8,128)} %param.17) | copy-start | bytes 2884
  55.0 9.9 %collective-permute-start.2 = (bf16[4,32,512]{2,1,0:T(8,128)(2,1)S(1)}, bf16[4,32,512]{2,1,0:T(8,128)(2,1)S(1)}, u32[]{:S(2)}, u32[]{:S(2)}) collective-permute-start(bf16[4,32,512]{2,1,0:T(8,128)(2,1)S(1)} %get-tuple-element.31), channel_id=1, source_target_pairs={{0,6},{1,7},{2,4},{3,5},{4,2},{5,3},{6,0},{7,1},{8,14},{9,15},{10,... | collective-permute-start | bytes 393224 | tf_op jit(solution)/shard_map/ppermute | solution.py:659
  66.7 6.4 %collective-permute-start.23 = (bf16[104,512]{1,0:T(8,128)(2,1)S(1)}, bf16[104,512]{1,0:T(8,128)(2,1)S(1)}, u32[]{:S(2)}, u32[]{:S(2)}) collective-permute-start(bf16[104,512]{1,0:T(8,128)(2,1)S(1)} %shard_map.148.refs_0_), channel_id=1, source_target_pairs={{0,2},{1,3},{2,0},{3,1},{4,6},{5,7},{6,4},{7,5},{8,10},{9,11},{10,... | collective-permute-start | bytes 319496 | tf_op jit(solution)/shard_map/ppermute | solution.py:659
  68.8 9.9 %collective-permute-start.24 = (bf16[104,512]{1,0:T(8,128)(2,1)S(1)}, bf16[104,512]{1,0:T(8,128)(2,1)S(1)}, u32[]{:S(2)}, u32[]{:S(2)}) collective-permute-start(bf16[104,512]{1,0:T(8,128)(2,1)S(1)} %shard_map.148.refs_0_), channel_id=1, source_target_pairs={{0,4},{1,5},{2,6},{3,7},{4,0},{5,1},{6,2},{7,3},{8,12},{9,13},{10,... | collective-permute-start | bytes 319496 | tf_op jit(solution)/shard_map/ppermute | solution.py:659
  69.6 9.1 %collective-permute-start.25 = (bf16[104,512]{1,0:T(8,128)(2,1)S(1)}, bf16[104,512]{1,0:T(8,128)(2,1)S(1)}, u32[]{:S(2)}, u32[]{:S(2)}) collective-permute-start(bf16[104,512]{1,0:T(8,128)(2,1)S(1)} %shard_map.148.refs_0_), channel_id=1, source_target_pairs={{0,6},{1,7},{2,4},{3,5},{4,2},{5,3},{6,0},{7,1},{8,14},{9,15},{10,... | collective-permute-start | bytes 319496 | tf_op jit(solution)/shard_map/ppermute | solution.py:659
  71.2 1.9 %collective-permute-start.27 = (f32[16,240]{1,0:T(8,128)S(1)}, f32[16,240]{1,0:T(8,128)S(1)}, u32[]{:S(2)}, u32[]{:S(2)}) collective-permute-start(f32[16,240]{1,0:T(8,128)S(1)} %get-tuple-element.39.refs_7_), channel_id=1, source_target_pairs={{0,1},{1,0},{2,3},{3,2},{4,5},{5,4},{6,7},{7,6},{8,9},{9,8},{10,11... | collective-permute-start | bytes 46088 | tf_op jit(solution)/shard_map/ppermute | solution.py:662
  79.9 5.8 %collective-permute-start.31 = (bf16[104,480]{1,0:T(8,128)(2,1)S(1)}, bf16[104,480]{1,0:T(8,128)(2,1)S(1)}, u32[]{:S(2)}, u32[]{:S(2)}) collective-permute-start(bf16[104,480]{1,0:T(8,128)(2,1)S(1)} %get-tuple-element.44), channel_id=1, source_target_pairs={{0,8},{8,16},{16,24},{24,0},{1,9},{9,17},{17,25},{25,1},{2,10},{10... | collective-permute-start | bytes 299528 | tf_op jit(solution)/shard_map/ppermute | solution.py:805
  85.8 5.0 %collective-permute-start.32 = (bf16[104,480]{1,0:T(8,128)(2,1)S(1)}, bf16[104,480]{1,0:T(8,128)(2,1)S(1)}, u32[]{:S(2)}, u32[]{:S(2)}) collective-permute-start(bf16[104,480]{1,0:T(8,128)(2,1)S(1)} %collective-permute-done.31.refs_0_), channel_id=1, source_target_pairs={{0,2},{1,3},{2,0},{3,1},{4,6},{5,7},{6,4},{7,5},{8,10},{9,11},{10,... | collective-permute-start | bytes 299528 | tf_op jit(solution)/shard_map/ppermute | solution.py:659
  87.6 9.1 %collective-permute-start.33 = (bf16[104,480]{1,0:T(8,128)(2,1)S(1)}, bf16[104,480]{1,0:T(8,128)(2,1)S(1)}, u32[]{:S(2)}, u32[]{:S(2)}) collective-permute-start(bf16[104,480]{1,0:T(8,128)(2,1)S(1)} %collective-permute-done.31.refs_0_), channel_id=1, source_target_pairs={{0,4},{1,5},{2,6},{3,7},{4,0},{5,1},{6,2},{7,3},{8,12},{9,13},{10,... | collective-permute-start | bytes 299528 | tf_op jit(solution)/shard_map/ppermute | solution.py:659
  88.3 8.4 %collective-permute-start.34 = (bf16[104,480]{1,0:T(8,128)(2,1)S(1)}, bf16[104,480]{1,0:T(8,128)(2,1)S(1)}, u32[]{:S(2)}, u32[]{:S(2)}) collective-permute-start(bf16[104,480]{1,0:T(8,128)(2,1)S(1)} %collective-permute-done.31.refs_0_), channel_id=1, source_target_pairs={{0,6},{1,7},{2,4},{3,5},{4,2},{5,3},{6,0},{7,1},{8,14},{9,15},{10,... | collective-permute-start | bytes 299528 | tf_op jit(solution)/shard_map/ppermute | solution.py:659
  101.3 7.1 %collective-permute-start.35 = (bf16[104,512]{1,0:T(8,128)(2,1)S(1)}, bf16[104,512]{1,0:T(8,128)(2,1)S(1)}, u32[]{:S(2)}, u32[]{:S(2)}) collective-permute-start(bf16[104,512]{1,0:T(8,128)(2,1)S(1)} %get-tuple-element.45.refs_0_), channel_id=1, source_target_pairs={{0,2},{1,3},{2,0},{3,1},{4,6},{5,7},{6,4},{7,5},{8,10},{9,11},{10,... | collective-permute-start | bytes 319496 | tf_op jit(solution)/shard_map/ppermute | solution.py:659
  103.1 11.8 %collective-permute-start.36 = (bf16[104,512]{1,0:T(8,128)(2,1)S(1)}, bf16[104,512]{1,0:T(8,128)(2,1)S(1)}, u32[]{:S(2)}, u32[]{:S(2)}) collective-permute-start(bf16[104,512]{1,0:T(8,128)(2,1)S(1)} %get-tuple-element.45.refs_0_), channel_id=1, source_target_pairs={{0,4},{1,5},{2,6},{3,7},{4,0},{5,1},{6,2},{7,3},{8,12},{9,13},{10,... | collective-permute-start | bytes 319496 | tf_op jit(solution)/shard_map/ppermute | solution.py:659
  104.1 10.9 %collective-permute-start.37 = (bf16[104,512]{1,0:T(8,128)(2,1)S(1)}, bf16[104,512]{1,0:T(8,128)(2,1)S(1)}, u32[]{:S(2)}, u32[]{:S(2)}) collective-permute-start(bf16[104,512]{1,0:T(8,128)(2,1)S(1)} %get-tuple-element.45.refs_0_), channel_id=1, source_target_pairs={{0,6},{1,7},{2,4},{3,5},{4,2},{5,3},{6,0},{7,1},{8,14},{9,15},{10,... | collective-permute-start | bytes 319496 | tf_op jit(solution)/shard_map/ppermute | solution.py:659
  105.8 13.7 %collective-permute-start.28 = (bf16[25,480]{1,0:T(8,128)(2,1)S(1)}, bf16[25,480]{1,0:T(8,128)(2,1)S(1)}, u32[]{:S(2)}, u32[]{:S(2)}) collective-permute-start(bf16[25,480]{1,0:T(8,128)(2,1)S(1)} %get-tuple-element.41), channel_id=1, source_target_pairs={{0,2},{1,3},{2,0},{3,1},{4,6},{5,7},{6,4},{7,5},{8,10},{9,11},{10,... | collective-permute-start | bytes 72008 | tf_op jit(solution)/shard_map/ppermute | solution.py:659
  106.6 14.3 %collective-permute-start.29 = (bf16[25,480]{1,0:T(8,128)(2,1)S(1)}, bf16[25,480]{1,0:T(8,128)(2,1)S(1)}, u32[]{:S(2)}, u32[]{:S(2)}) collective-permute-start(bf16[25,480]{1,0:T(8,128)(2,1)S(1)} %get-tuple-element.42), channel_id=1, source_target_pairs={{0,4},{1,5},{2,6},{3,7},{4,0},{5,1},{6,2},{7,3},{8,12},{9,13},{10,... | collective-permute-start | bytes 72008 | tf_op jit(solution)/shard_map/ppermute | solution.py:659
  108.5 12.4 %collective-permute-start.30 = (bf16[25,480]{1,0:T(8,128)(2,1)S(1)}, bf16[25,480]{1,0:T(8,128)(2,1)S(1)}, u32[]{:S(2)}, u32[]{:S(2)}) collective-permute-start(bf16[25,480]{1,0:T(8,128)(2,1)S(1)} %get-tuple-element.43), channel_id=1, source_target_pairs={{0,6},{1,7},{2,4},{3,5},{4,2},{5,3},{6,0},{7,1},{8,14},{9,15},{10,... | collective-permute-start | bytes 72008 | tf_op jit(solution)/shard_map/ppermute | solution.py:659
  116.2 4.7 %collective-permute-start.38 = (bf16[25,480]{1,0:T(8,128)(2,1)S(1)}, bf16[25,480]{1,0:T(8,128)(2,1)S(1)}, u32[]{:S(2)}, u32[]{:S(2)}) collective-permute-start(bf16[25,480]{1,0:T(8,128)(2,1)S(1)} %get-tuple-element.48), channel_id=1, source_target_pairs={{0,2},{1,3},{2,0},{3,1},{4,6},{5,7},{6,4},{7,5},{8,10},{9,11},{10,... | collective-permute-start | bytes 72008 | tf_op jit(solution)/shard_map/ppermute | solution.py:659
  118.4 5.2 %collective-permute-start.39 = (bf16[25,480]{1,0:T(8,128)(2,1)S(1)}, bf16[25,480]{1,0:T(8,128)(2,1)S(1)}, u32[]{:S(2)}, u32[]{:S(2)}) collective-permute-start(bf16[25,480]{1,0:T(8,128)(2,1)S(1)} %get-tuple-element.49), channel_id=1, source_target_pairs={{0,4},{1,5},{2,6},{3,7},{4,0},{5,1},{6,2},{7,3},{8,12},{9,13},{10,... | collective-permute-start | bytes 72008 | tf_op jit(solution)/shard_map/ppermute | solution.py:659
  119.5 5.7 %collective-permute-start.40 = (bf16[25,480]{1,0:T(8,128)(2,1)S(1)}, bf16[25,480]{1,0:T(8,128)(2,1)S(1)}, u32[]{:S(2)}, u32[]{:S(2)}) collective-permute-start(bf16[25,480]{1,0:T(8,128)(2,1)S(1)} %get-tuple-element.50), channel_id=1, source_target_pairs={{0,6},{1,7},{2,4},{3,5},{4,2},{5,3},{6,0},{7,1},{8,14},{9,15},{10,... | collective-permute-start | bytes 72008 | tf_op jit(solution)/shard_map/ppermute | solution.py:659
  (1 other events, 4.2 us)

commit v4 on v3

--- a/solution.py
+++ b/solution.py
@@ -402,10 +402,37 @@
             out[...] = full[:, at * plan.pair_cols : (at + 1) * plan.pair_cols]
 
 
+def fill_shifts(plan, tick, shifts, scale_at, offset_at):
+    place = lax.axis_index("tp")
+    core, pair = place % 2, place // 2
+    cols, half = plan.cols, plan.ticks * plan.pairs
+    own = pl.ds(pl.multiple_of(core * half, 8), half)
+    for k in range(plan.pairs):
+        for side in range(2):
+            start = pl.multiple_of(
+                (pair ^ k) * plan.pair_cols + (core if side == 0 else 1 - core) * cols, 16
+            )
+            scale_at[pl.ds(start, cols), :] = spread(shifts[side][k][0, own, :], tick, plan)
+            offset_at[pl.ds(start, cols), :] = spread(shifts[side][k][1, own, :], tick, plan)
+
+
+def expand_kernel(plan, *refs):
+    pairs = plan.pairs
+    shifts = (refs[:pairs], refs[pairs : 2 * pairs])
+    gate_mine, gate_other, scale_at, offset_at, *gates = refs[2 * pairs :]
+    core = lax.axis_index("tp") % 2
+    half = plan.ticks * pairs
+    fill_shifts(plan, plan.ticks - 1, shifts, scale_at, offset_at)
+    own = pl.ds(pl.multiple_of(core * half, 8), half)
+    for tick in range(plan.ticks):
+        for side, gate in enumerate((gate_mine, gate_other)):
+            start = pl.multiple_of((core if side == 0 else 1 - core) * plan.cols, 16)
+            gates[tick][pl.ds(start, plan.cols), :] = spread(gate[own, :], tick, plan)
+
+
 def project(plan, tick, pieces, shifts, weights, held, qkv, wide, scale_at, offset_at, turning):
     pairs = plan.pairs
     mine, other, near, far = weights
-    half = plan.ticks * plan.pairs
     place = lax.axis_index("tp")
     core, pair = place % 2, place // 2
     cols, pair_cols, lanes = plan.cols, plan.pair_cols, plan.lanes
@@ -434,15 +461,9 @@
                 def _(place_at=place_at, piece=piece):
                     turning[place_at * plan.tokens : (place_at + 1) * plan.tokens, :] = piece
 
-        for side in range(2):
-            start = pl.multiple_of(
-                at * pair_cols + (core if side == 0 else 1 - core) * cols, 16
-            )
-            own = pl.ds(pl.multiple_of(core * half, 8), half)
-            scale_at[pl.ds(start, cols), :] = spread(shifts[side][k][0, own, :], tick, plan)
-            offset_at[pl.ds(start, cols), :] = spread(shifts[side][k][1, own, :], tick, plan)
     if tick == 0:
         wide[...] = turning[...].T
+        fill_shifts(plan, tick, shifts, scale_at, offset_at)
     value = wide[...]
     average = jnp.sum(value, axis=0, keepdims=True) * (1.0 / plan.width)
     centred = value - average
@@ -536,34 +557,27 @@
 
 def layer_kernel(plan, tick, *refs):
     pairs = plan.pairs
-    attended, held, cached, mixed_at, qkv, *rest = refs[4 * pairs + 5 :]
-    project(
-        plan,
-        tick,
-        refs[:pairs],
-        (refs[pairs : 2 * pairs], refs[2 * pairs : 3 * pairs]),
-        refs[4 * pairs : 4 * pairs + 4],
-        held,
-        qkv,
-        *rest,
-    )
-    attend(plan, tick, refs[3 * pairs : 4 * pairs], qkv, refs[4 * pairs + 4], attended, cached, mixed_at)
+    pieces, (scale_at, offset_at) = refs[:pairs], refs[pairs : pairs + 2]
+    stores = refs[pairs + 2 : 2 * pairs + 2]
+    weights, refs = refs[2 * pairs + 2 : 2 * pairs + 6], refs[2 * pairs + 6 :]
+    sharp, attended, held, cached, mixed_at, qkv, wide = refs
+    project(plan, tick, pieces, None, weights, held, qkv, wide, scale_at, offset_at, None)
+    attend(plan, tick, stores, qkv, sharp, attended, cached, mixed_at)
 
 
 def return_kernel(plan, tick, *refs):
     pairs = plan.pairs
     pieces = refs[:pairs]
-    mine, other, held, gate_mine, gate_other = refs[pairs : pairs + 5]
-    rest = refs[pairs + 5 :]
+    mine, other, held, gate = refs[pairs : pairs + 4]
+    rest = refs[pairs + 4 :]
     if tick == 0:
-        entering, onward, *rows = rest[:-3]
+        entering, onward, *rows = rest[:-2]
     else:
-        rows = rest[:-3]
-    joined, projected, gate = rest[-3:]
+        rows = rest[:-2]
+    joined, projected = rest[-2:]
     place = lax.axis_index("tp")
     core, pair = place % 2, place // 2
     cols, dim = plan.cols, plan.head_dim
-    half = plan.ticks * pairs
     joined[plan.used :, :] = jnp.zeros((plan.lanes - plan.used, plan.width), BF16)
     for k in range(pairs):
         for at in range(pairs):
@@ -574,11 +588,9 @@
                 joined[: plan.dense, start : start + count] = pieces[k][:, :count]
 
     value = joined[...]
-    for side, (matrix, gates) in enumerate(((mine, gate_mine), (other, gate_other))):
+    for side, matrix in enumerate((mine, other)):
         start = pl.multiple_of((core if side == 0 else 1 - core) * cols, 16)
         projected[pl.ds(start, cols), :] = dot(matrix[...], value, ((1,), (1,))).astype(BF16).astype(F32)
-        gates = gates[pl.ds(pl.multiple_of(core * half, 8), half), :]
-        gate[pl.ds(start, cols), :] = spread(gates, tick, plan)
     result = held[...].astype(F32) + gate[...] * projected[...]
     turned = result.T
     for k in range(pairs):
@@ -750,6 +762,13 @@
         ],
     )
 
+    *later_shift, gate_0, gate_1 = call(
+        expand_kernel,
+        [((width, lanes), F32)] * 2 + [((pair_cols, lanes), F32)] * 2,
+        [],
+        [*shifts, gate, gate_back],
+    )
+    gates = (gate_0, gate_1)
     emitted = []
     for tick in range(ticks):
         wide = [pltpu.VMEM((width, lanes), F32)] * 3 + [pltpu.VMEM((lanes, width), F32)]
@@ -770,11 +789,11 @@
                 (pairs + 1,),
             )
         else:
-            values = [*pieces, *shifts, *stored, *weights, focus_sharpness_exponents]
+            values = [*pieces, *later_shift, *stored, *weights, focus_sharpness_exponents]
             attended, held = call(
                 lambda *refs, tick=tick: layer_kernel(refs[0], tick, *refs[1:]),
                 [((plan.dense, span), BF16), ((pair_cols, lanes), BF16)],
-                heads_of + [pltpu.VMEM((3, plan.rows, lanes), BF16)] + wide,
+                heads_of + [pltpu.VMEM((3, plan.rows, lanes), BF16), wide[0]],
                 values,
                 (len(values) - 1,),
             )
@@ -786,18 +805,13 @@
         results = call(
             lambda *refs, tick=tick: return_kernel(refs[0], tick, *refs[1:]),
             outs,
-            [
-                pltpu.VMEM((lanes, width), BF16),
-                pltpu.VMEM((pair_cols, lanes), F32),
-                pltpu.VMEM((pair_cols, lanes), F32),
-            ],
+            [pltpu.VMEM((lanes, width), BF16), pltpu.VMEM((pair_cols, lanes), F32)],
             [
                 *around(attended),
                 out_mine,
                 out_other,
                 held,
-                gate,
-                gate_back,
+                gates[tick],
                 *extra,
             ],
         )

time: 127 us -> 127 us (level)
    pallas_call x9 -> x10, Pallas kernels: 20.6 us -> 20.9 us  [call(): pl.pallas_call(lambda *refs: kernel(plan, *refs), out_shape=[space(shape,...]
  transfers between devices with their start and end apart: 41 -> 41, of which waited for: 17 -> 17; matrix products, arithmetic and copies ran while one was open for 0% -> 0% of each run, Pallas kernels for 10% -> 11%
where the time goes in v4:
time: 127 us; the launch traced here: 126 us
  starting transfers between devices  57.9 us (46%)
  waiting for transfers between devices  47.3 us (37%)
  Pallas kernels  20.9 us (16%)
    ppermute x27, starting transfers between devices, swap(): return lax.ppermute(value, 'tp', [(g, g ^ 2 * k) for g in range(tp)])  46.5 us
    ppermute x27, waiting for transfers between devices, swap(): return lax.ppermute(value, 'tp', [(g, g ^ 2 * k) for g in range(tp)])  37 us
    pallas_call x10, Pallas kernels, call(): pl.pallas_call(lambda *refs: kernel(plan, *refs), out_shape=[space(shape,...  20.9 us
    ppermute x12, starting transfers between devices, across(): return lax.ppermute(value, 'tp', [(g, g ^ 1) for g in range(tp)])  10.1 us
    ppermute x1, waiting for transfers between devices, paired(): lax.ppermute(results[0], 'section', [(s, (s + 1) % plan.section) for s in...  5.33 us
    ppermute x12, waiting for transfers between devices, across(): return lax.ppermute(value, 'tp', [(g, g ^ 1) for g in range(tp)])  4.97 us
  transfers between devices with their start and end apart: 41, of which 17 were waited for; matrix products, arithmetic and copies ran while one was open for 0% of the time, Pallas kernels for 11%

profile of v4, /device:TPU:0, one launch (start us, length us, event | category | flops | bytes accessed | tf_op | source)
XLA Modules:
  0.0 126.4 jit_solution(9686351246627652287)
XLA Ops:
  0.5 3.3 %shard_map.145 = (bf16[16,240]{1,0:T(8,128)(2,1)S(1)}, bf16[3,32,1920]{2,1,0:T(8,128)(2,1)S(1)}, bf16[3,240,1920]{2,1,0:T(8,128)(2,1)S(1)}, bf16[104,512]{1,0:T(...) custom-call(s32[5,8]{1,0:T(8,128)} %refs_0_.1, ...), custom_call_target="tpu_custom_call" | custom-call | tf_op jit(solution)/shard_map/pallas_call | solution.py:686
  3.8 0.8 collective-permute-start.21
  4.7 0.8 collective-permute-start.26
  5.5 7.8 %collective-permute-start.22 = (bf16[3,32,1920]{2,1,0:T(8,128)(2,1)S(1)}, bf16[3,32,1920]{2,1,0:T(8,128)(2,1)S(1)}, u32[]{:S(2)}, u32[]{:S(2)}) collective-permute-start(bf16[3,32,1920]{2,1,0:T(8,128)(2,1)S(1)} %collective-permute-done.21.refs_14_.refs_12_), channel_id=1, source_target_pairs={{0,1},{1,0},{2,3},{3,2},{4,5},{5,4},{6,7},{7,6},{8,9},{9,8},{10,11... | collective-permute-start | bytes 1105928 | tf_op jit(solution)/shard_map/ppermute | solution.py:674
  13.3 3.8 %collective-permute-start.7 = (bf16[16,240]{1,0:T(8,128)(2,1)S(1)}, bf16[16,240]{1,0:T(8,128)(2,1)S(1)}, u32[]{:S(2)}, u32[]{:S(2)}) collective-permute-start(bf16[16,240]{1,0:T(8,128)(2,1)S(1)} %get-tuple-element.37.refs_0_), channel_id=1, source_target_pairs={{0,4},{1,5},{2,6},{3,7},{4,0},{5,1},{6,2},{7,3},{8,12},{9,13},{10,... | collective-permute-start | bytes 23048 | tf_op jit(solution)/shard_map/ppermute | solution.py:671
  17.0 3.1 %collective-permute-start.8 = (bf16[16,240]{1,0:T(8,128)(2,1)S(1)}, bf16[16,240]{1,0:T(8,128)(2,1)S(1)}, u32[]{:S(2)}, u32[]{:S(2)}) collective-permute-start(bf16[16,240]{1,0:T(8,128)(2,1)S(1)} %get-tuple-element.37.refs_0_), channel_id=1, source_target_pairs={{0,6},{1,7},{2,4},{3,5},{4,2},{5,3},{6,0},{7,1},{8,14},{9,15},{10,... | collective-permute-start | bytes 23048 | tf_op jit(solution)/shard_map/ppermute | solution.py:671
  20.1 2.4 %collective-permute-done.8.refs_3_ = bf16[16,240]{1,0:T(8,128)(2,1)S(1)} collective-permute-done((bf16[16,240]{1,0:T(8,128)(2,1)S(1)}, bf16[16,240]{1,0:T(8,128)(2,1)S(1)}, u32[]{:S(2)}, u32[]{:S(2)}) %collective-permute-start.8) | collective-permute-done | bytes 7712 | tf_op jit(solution)/shard_map/ppermute | solution.py:671
  23.8 1.0 collective-permute-done.12.refs_7_
  24.8 1.2 shard_map.146
  26.4 3.3 %collective-permute-start.14 = (f32[2,16,240]{2,1,0:T(8,128)S(1)}, f32[2,16,240]{2,1,0:T(8,128)S(1)}, u32[]{:S(2)}, u32[]{:S(2)}) collective-permute-start(f32[2,16,240]{2,1,0:T(8,128)S(1)} %get-tuple-element.39.refs_4_.refs_0_), channel_id=1, source_target_pairs={{0,4},{1,5},{2,6},{3,7},{4,0},{5,1},{6,2},{7,3},{8,12},{9,13},{10,... | collective-permute-start | bytes 92168 | tf_op jit(solution)/shard_map/ppermute | solution.py:671
  30.0 3.4 %collective-permute-start.15 = (f32[2,16,240]{2,1,0:T(8,128)S(1)}, f32[2,16,240]{2,1,0:T(8,128)S(1)}, u32[]{:S(2)}, u32[]{:S(2)}) collective-permute-start(f32[2,16,240]{2,1,0:T(8,128)S(1)} %get-tuple-element.39.refs_4_.refs_0_), channel_id=1, source_target_pairs={{0,6},{1,7},{2,4},{3,5},{4,2},{5,3},{6,0},{7,1},{8,14},{9,15},{10,... | collective-permute-start | bytes 92168 | tf_op jit(solution)/shard_map/ppermute | solution.py:671
  33.4 2.3 %collective-permute-done.15.refs_7_.refs_3_ = f32[2,16,240]{2,1,0:T(8,128)S(1)} collective-permute-done((f32[2,16,240]{2,1,0:T(8,128)S(1)}, f32[2,16,240]{2,1,0:T(8,128)S(1)}, u32[]{:S(2)}, u32[]{:S(2)}) %collective-permute-start.15) | collective-permute-done | bytes 30752 | tf_op jit(solution)/shard_map/ppermute | solution.py:671
  35.7 1.2 collective-permute-done.17.refs_9_.refs_5_
  37.0 1.0 collective-permute-done.18.refs_10_.refs_6_
  38.3 1.0 collective-permute-done.19.refs_11_.refs_7_
  39.3 4.3 %collective-permute-start.4 = (bf16[104,512]{1,0:T(8,128)(2,1)S(1)}, bf16[104,512]{1,0:T(8,128)(2,1)S(1)}, u32[]{:S(2)}, u32[]{:S(2)}) collective-permute-start(bf16[104,512]{1,0:T(8,128)(2,1)S(1)} %get-tuple-element.36.refs_0_), channel_id=1, source_target_pairs={{0,4},{1,5},{2,6},{3,7},{4,0},{5,1},{6,2},{7,3},{8,12},{9,13},{10,... | collective-permute-start | bytes 319496 | tf_op jit(solution)/shard_map/ppermute | solution.py:671
  44.2 7.1 %collective-permute-done.4.refs_2_ = bf16[104,512]{1,0:T(8,128)(2,1)S(1)} collective-permute-done((bf16[104,512]{1,0:T(8,128)(2,1)S(1)}, bf16[104,512]{1,0:T(8,128)(2,1)S(1)}, u32[]{:S(2)}, u32[]{:S(2)}) %collective-permute-start.4) | collective-permute-done | bytes 106528 | tf_op jit(solution)/shard_map/ppermute | solution.py:671
  51.6 3.4 %collective-permute-start.1 = (bf16[4,32,512]{2,1,0:T(8,128)(2,1)S(1)}, bf16[4,32,512]{2,1,0:T(8,128)(2,1)S(1)}, u32[]{:S(2)}, u32[]{:S(2)}) collective-permute-start(bf16[4,32,512]{2,1,0:T(8,128)(2,1)S(1)} %get-tuple-element.34), channel_id=1, source_target_pairs={{0,4},{1,5},{2,6},{3,7},{4,0},{5,1},{6,2},{7,3},{8,12},{9,13},{10,... | collective-permute-start | bytes 393224 | tf_op jit(solution)/shard_map/ppermute | solution.py:671
  55.0 1.6 %collective-permute-start.2 = (bf16[4,32,512]{2,1,0:T(8,128)(2,1)S(1)}, bf16[4,32,512]{2,1,0:T(8,128)(2,1)S(1)}, u32[]{:S(2)}, u32[]{:S(2)}) collective-permute-start(bf16[4,32,512]{2,1,0:T(8,128)(2,1)S(1)} %get-tuple-element.35), channel_id=1, source_target_pairs={{0,6},{1,7},{2,4},{3,5},{4,2},{5,3},{6,0},{7,1},{8,14},{9,15},{10,... | collective-permute-start | bytes 393224 | tf_op jit(solution)/shard_map/ppermute | solution.py:671
  56.6 3.6 %shard_map.147 = (bf16[480,128]{1,0:T(8,128)(2,1)S(1)}, bf16[3,544,128]{2,1,0:T(8,128)(2,1)S(1)}) custom-call(bf16[104,512]{1,0:T(8,128)(2,1)S(1)} %get-tuple-element.36.refs_0_, bf16[104,512]{1,0:T(8,128)(2,1)S(1)} %collective-permute-done.3.refs_1_, bf16[104,512]{1,0:T(8,128)(2,1)S(1)} %collective-permute-done.4.refs_2_, ...), custom_call_target="tpu_custom_call" | custom-call | tf_op jit(solution)/shard_map/pallas_call | solution.py:686
  60.2 4.7 %collective-permute-done.1.refs_2_.refs_8_ = bf16[4,32,512]{2,1,0:T(8,128)(2,1)S(1)} collective-permute-done((bf16[4,32,512]{2,1,0:T(8,128)(2,1)S(1)}, bf16[4,32,512]{2,1,0:T(8,128)(2,1)S(1)}, u32[]{:S(2)}, u32[]{:S(2)}) %collective-permute-start.1) | collective-permute-done | bytes 131104 | tf_op jit(solution)/shard_map/ppermute | solution.py:671
  64.9 1.7 %shard_map.148.refs_0_ = bf16[104,512]{1,0:T(8,128)(2,1)S(1)} custom-call(bf16[4,32,512]{2,1,0:T(8,128)(2,1)S(1)} %get-tuple-element.32.refs_0_.refs_6_, bf16[4,32,512]{2,1,0:T(8,128)(2,1)S(1)} %collective-permute-done.refs_1_.refs_7_, bf16[4,32,512]{2,1,0:T(8,128)(2,1)S(1)} %collective-permute-done.1.refs_2_.refs_8_, ...), custom_call_target="tpu_custom_call" | custom-call | tf_op jit(solution)/shard_map/pallas_call | solution.py:686
  66.7 2.1 %collective-permute-start.23 = (bf16[104,512]{1,0:T(8,128)(2,1)S(1)}, bf16[104,512]{1,0:T(8,128)(2,1)S(1)}, u32[]{:S(2)}, u32[]{:S(2)}) collective-permute-start(bf16[104,512]{1,0:T(8,128)(2,1)S(1)} %shard_map.148.refs_0_), channel_id=1, source_target_pairs={{0,2},{1,3},{2,0},{3,1},{4,6},{5,7},{6,4},{7,5},{8,10},{9,11},{10,... | collective-permute-start | bytes 319496 | tf_op jit(solution)/shard_map/ppermute | solution.py:671
  68.8 0.8 collective-permute-start.24
  69.6 1.6 %collective-permute-start.25 = (bf16[104,512]{1,0:T(8,128)(2,1)S(1)}, bf16[104,512]{1,0:T(8,128)(2,1)S(1)}, u32[]{:S(2)}, u32[]{:S(2)}) collective-permute-start(bf16[104,512]{1,0:T(8,128)(2,1)S(1)} %shard_map.148.refs_0_), channel_id=1, source_target_pairs={{0,6},{1,7},{2,4},{3,5},{4,2},{5,3},{6,0},{7,1},{8,14},{9,15},{10,... | collective-permute-start | bytes 319496 | tf_op jit(solution)/shard_map/ppermute | solution.py:671
  71.3 1.8 %shard_map.150.refs_8_ = bf16[104,480]{1,0:T(8,128)(2,1)S(1)} custom-call(s32[8,30]{1,0:T(8,128)S(1)} %bitcast.31, f32[32,4096]{1,0:T(8,128)S(1)} %bitcast.30, f32[128,128]{1,0:T(8,128)S(1)} %copy-done.5, bf16[32,1920]{1,0:T(8,128)(2,1)S(1)} %copy-done.3, bf16[25,1920]{1,0:T(8,128)(2,1)S(1)} %copy-done.4), custom_call_target="tpu_custom_call" | custom-call | tf_op jit(solution)/shard_map/pallas_call | solution.py:686
  73.1 0.8 shard_map.149
  74.0 4.7 %collective-permute-done.24.refs_2_ = bf16[104,512]{1,0:T(8,128)(2,1)S(1)} collective-permute-done((bf16[104,512]{1,0:T(8,128)(2,1)S(1)}, bf16[104,512]{1,0:T(8,128)(2,1)S(1)}, u32[]{:S(2)}, u32[]{:S(2)}) %collective-permute-start.24) | collective-permute-done | bytes 106528 | tf_op jit(solution)/shard_map/ppermute | solution.py:671
  78.7 1.2 shard_map.151
  80.4 5.3 %collective-permute-done.31.refs_0_ = bf16[104,480]{1,0:T(8,128)(2,1)S(1)} collective-permute-done((bf16[104,480]{1,0:T(8,128)(2,1)S(1)}, bf16[104,480]{1,0:T(8,128)(2,1)S(1)}, u32[]{:S(2)}, u32[]{:S(2)}) %collective-permute-start.31) | collective-permute-done | bytes 99872 | tf_op jit(solution)/shard_map/ppermute | solution.py:819
  85.7 1.8 %collective-permute-start.32 = (bf16[104,480]{1,0:T(8,128)(2,1)S(1)}, bf16[104,480]{1,0:T(8,128)(2,1)S(1)}, u32[]{:S(2)}, u32[]{:S(2)}) collective-permute-start(bf16[104,480]{1,0:T(8,128)(2,1)S(1)} %collective-permute-done.31.refs_0_), channel_id=1, source_target_pairs={{0,2},{1,3},{2,0},{3,1},{4,6},{5,7},{6,4},{7,5},{8,10},{9,11},{10,... | collective-permute-start | bytes 299528 | tf_op jit(solution)/shard_map/ppermute | solution.py:671
  88.2 1.9 %collective-permute-start.34 = (bf16[104,480]{1,0:T(8,128)(2,1)S(1)}, bf16[104,480]{1,0:T(8,128)(2,1)S(1)}, u32[]{:S(2)}, u32[]{:S(2)}) collective-permute-start(bf16[104,480]{1,0:T(8,128)(2,1)S(1)} %collective-permute-done.31.refs_0_), channel_id=1, source_target_pairs={{0,6},{1,7},{2,4},{3,5},{4,2},{5,3},{6,0},{7,1},{8,14},{9,15},{10,... | collective-permute-start | bytes 299528 | tf_op jit(solution)/shard_map/ppermute | solution.py:671
  90.7 5.9 %collective-permute-done.33.refs_2_ = bf16[104,480]{1,0:T(8,128)(2,1)S(1)} collective-permute-done((bf16[104,480]{1,0:T(8,128)(2,1)S(1)}, bf16[104,480]{1,0:T(8,128)(2,1)S(1)}, u32[]{:S(2)}, u32[]{:S(2)}) %collective-permute-start.33) | collective-permute-done | bytes 99872 | tf_op jit(solution)/shard_map/ppermute | solution.py:671
  96.6 4.5 %shard_map.152 = (bf16[104,512]{1,0:T(8,128)(2,1)S(1)}, bf16[480,128]{1,0:T(8,128)(2,1)S(1)}) custom-call(bf16[104,480]{1,0:T(8,128)(2,1)S(1)} %collective-permute-done.31.refs_0_, bf16[104,480]{1,0:T(8,128)(2,1)S(1)} %collective-permute-done.32.refs_1_, bf16[104,480]{1,0:T(8,128)(2,1)S(1)} %collective-permute-done.33.refs_2_, ...), custom_call_target="tpu_custom_call" | custom-call | tf_op jit(solution)/shard_map/pallas_call | solution.py:686
  101.1 1.8 %collective-permute-start.35 = (bf16[104,512]{1,0:T(8,128)(2,1)S(1)}, bf16[104,512]{1,0:T(8,128)(2,1)S(1)}, u32[]{:S(2)}, u32[]{:S(2)}) collective-permute-start(bf16[104,512]{1,0:T(8,128)(2,1)S(1)} %get-tuple-element.52.refs_0_), channel_id=1, source_target_pairs={{0,2},{1,3},{2,0},{3,1},{4,6},{5,7},{6,4},{7,5},{8,10},{9,11},{10,... | collective-permute-start | bytes 319496 | tf_op jit(solution)/shard_map/ppermute | solution.py:671
  102.9 1.0 collective-permute-start.36
  103.9 1.7 %collective-permute-start.37 = (bf16[104,512]{1,0:T(8,128)(2,1)S(1)}, bf16[104,512]{1,0:T(8,128)(2,1)S(1)}, u32[]{:S(2)}, u32[]{:S(2)}) collective-permute-start(bf16[104,512]{1,0:T(8,128)(2,1)S(1)} %get-tuple-element.52.refs_0_), channel_id=1, source_target_pairs={{0,6},{1,7},{2,4},{3,5},{4,2},{5,3},{6,0},{7,1},{8,14},{9,15},{10,... | collective-permute-start | bytes 319496 | tf_op jit(solution)/shard_map/ppermute | solution.py:671
  105.6 0.8 collective-permute-start.28
  106.4 1.9 %collective-permute-start.29 = (bf16[25,480]{1,0:T(8,128)(2,1)S(1)}, bf16[25,480]{1,0:T(8,128)(2,1)S(1)}, u32[]{:S(2)}, u32[]{:S(2)}) collective-permute-start(bf16[25,480]{1,0:T(8,128)(2,1)S(1)} %get-tuple-element.47), channel_id=1, source_target_pairs={{0,4},{1,5},{2,6},{3,7},{4,0},{5,1},{6,2},{7,3},{8,12},{9,13},{10,... | collective-permute-start | bytes 72008 | tf_op jit(solution)/shard_map/ppermute | solution.py:671
  108.3 1.7 %collective-permute-start.30 = (bf16[25,480]{1,0:T(8,128)(2,1)S(1)}, bf16[25,480]{1,0:T(8,128)(2,1)S(1)}, u32[]{:S(2)}, u32[]{:S(2)}) collective-permute-start(bf16[25,480]{1,0:T(8,128)(2,1)S(1)} %get-tuple-element.48), channel_id=1, source_target_pairs={{0,6},{1,7},{2,4},{3,5},{4,2},{5,3},{6,0},{7,1},{8,14},{9,15},{10,... | collective-permute-start | bytes 72008 | tf_op jit(solution)/shard_map/ppermute | solution.py:671
  110.0 4.8 %collective-permute-done.36.refs_2_ = bf16[104,512]{1,0:T(8,128)(2,1)S(1)} collective-permute-done((bf16[104,512]{1,0:T(8,128)(2,1)S(1)}, bf16[104,512]{1,0:T(8,128)(2,1)S(1)}, u32[]{:S(2)}, u32[]{:S(2)}) %collective-permute-start.36) | collective-permute-done | bytes 106528 | tf_op jit(solution)/shard_map/ppermute | solution.py:671
  114.7 1.2 shard_map.153
  115.9 2.2 %collective-permute-start.38 = (bf16[25,480]{1,0:T(8,128)(2,1)S(1)}, bf16[25,480]{1,0:T(8,128)(2,1)S(1)}, u32[]{:S(2)}, u32[]{:S(2)}) collective-permute-start(bf16[25,480]{1,0:T(8,128)(2,1)S(1)} %get-tuple-element.56), channel_id=1, source_target_pairs={{0,2},{1,3},{2,0},{3,1},{4,6},{5,7},{6,4},{7,5},{8,10},{9,11},{10,... | collective-permute-start | bytes 72008 | tf_op jit(solution)/shard_map/ppermute | solution.py:671
  118.1 1.1 collective-permute-start.39
  119.2 1.4 %collective-permute-start.40 = (bf16[25,480]{1,0:T(8,128)(2,1)S(1)}, bf16[25,480]{1,0:T(8,128)(2,1)S(1)}, u32[]{:S(2)}, u32[]{:S(2)}) collective-permute-start(bf16[25,480]{1,0:T(8,128)(2,1)S(1)} %get-tuple-element.58), channel_id=1, source_target_pairs={{0,6},{1,7},{2,4},{3,5},{4,2},{5,3},{6,0},{7,1},{8,14},{9,15},{10,... | collective-permute-start | bytes 72008 | tf_op jit(solution)/shard_map/ppermute | solution.py:671
  120.6 2.7 %collective-permute-done.39.refs_6_ = bf16[25,480]{1,0:T(8,128)(2,1)S(1)} collective-permute-done((bf16[25,480]{1,0:T(8,128)(2,1)S(1)}, bf16[25,480]{1,0:T(8,128)(2,1)S(1)}, u32[]{:S(2)}, u32[]{:S(2)}) %collective-permute-start.39) | collective-permute-done | bytes 24032 | tf_op jit(solution)/shard_map/ppermute | solution.py:671
  123.3 1.6 %collective-permute-done.40.refs_7_ = bf16[25,480]{1,0:T(8,128)(2,1)S(1)} collective-permute-done((bf16[25,480]{1,0:T(8,128)(2,1)S(1)}, bf16[25,480]{1,0:T(8,128)(2,1)S(1)}, u32[]{:S(2)}, u32[]{:S(2)}) %collective-permute-start.40) | collective-permute-done | bytes 24032 | tf_op jit(solution)/shard_map/ppermute | solution.py:671
  124.9 1.5 %shard_map.154 = bf16[25,2,1920]{2,1,0:T(2,128)(2,1)} custom-call(bf16[25,480]{1,0:T(8,128)(2,1)S(1)} %get-tuple-element.45.refs_0_, bf16[25,480]{1,0:T(8,128)(2,1)S(1)} %collective-permute-done.28.refs_1_, bf16[25,480]{1,0:T(8,128)(2,1)S(1)} %collective-permute-done.29.refs_2_, bf16[25,480]{1,0:T(8,128)(2,1)S(1)} %collective-permute-done.30.refs_3_, ...), custom_call_target="tpu_custom_call" | custom-call | tf_op jit(solution)/shard_map/pallas_call | solution.py:686
  (60 shorter events, 5.6 us)
Async XLA Ops:
  0.0 56.6 %collective-permute-start.20 = (bf16[3,240,1920]{2,1,0:T(8,128)(2,1)}, bf16[3,240,1920]{2,1,0:T(8,128)(2,1)S(1)}, u32[]{:S(2)}, u32[]{:S(2)}) collective-permute-start(bf16[3,240,1920]{2,1,0:T(8,128)(2,1)} %bitcast.23), channel_id=1, source_target_pairs={{0,1},{1,0},{2,3},{3,2},{4,5},{5,4},{6,7},{7,6},{8,9},{9,8},{10,11... | collective-permute-start | bytes 8294408 | tf_op jit(solution)/shard_map/ppermute | solution.py:674
  0.5 24.3 %copy-start.7 = (f32[1,3,240]{2,0,1:T(1,128)S(1)}, f32[1,3,240]{2,0,1:T(1,128)}, u32[]{:S(2)}) copy-start(f32[1,3,240]{2,0,1:T(1,128)} %param.23) | copy-start | bytes 8644
  3.8 52.8 %copy-start = (bf16[1,1920,3,240]{1,3,2,0:T(8,128)(2,1)S(1)}, bf16[1,1920,3,240]{1,3,2,0:T(8,128)(2,1)}, u32[]{:S(2)}) copy-start(bf16[1,1920,3,240]{1,3,2,0:T(8,128)(2,1)} %param.24) | copy-start | bytes 8294404
  3.8 1.7 %collective-permute-start.21 = (bf16[3,32,1920]{2,1,0:T(8,128)(2,1)S(1)}, bf16[3,32,1920]{2,1,0:T(8,128)(2,1)S(1)}, u32[]{:S(2)}, u32[]{:S(2)}) collective-permute-start(bf16[3,32,1920]{2,1,0:T(8,128)(2,1)S(1)} %get-tuple-element.40), channel_id=1, source_target_pairs={{2,1},{6,5},{10,9},{14,13},{18,17},{22,21},{26,25},{30,29}} | collective-permute-start | bytes 1105928 | tf_op jit(solution)/shard_map/ppermute | solution.py:748
  4.7 69.3 %collective-permute-start.26 = (bf16[240,1920]{1,0:T(8,128)(2,1)S(1)}, bf16[240,1920]{1,0:T(8,128)(2,1)S(1)}, u32[]{:S(2)}, u32[]{:S(2)}) collective-permute-start(bf16[240,1920]{1,0:T(8,128)(2,1)S(1)} %bitcast.27), channel_id=1, source_target_pairs={{0,1},{1,0},{2,3},{3,2},{4,5},{5,4},{6,7},{7,6},{8,9},{9,8},{10,11... | collective-permute-start | bytes 2764808 | tf_op jit(solution)/shard_map/ppermute | solution.py:674
  5.5 49.5 %collective-permute-start.22 = (bf16[3,32,1920]{2,1,0:T(8,128)(2,1)S(1)}, bf16[3,32,1920]{2,1,0:T(8,128)(2,1)S(1)}, u32[]{:S(2)}, u32[]{:S(2)}) collective-permute-start(bf16[3,32,1920]{2,1,0:T(8,128)(2,1)S(1)} %collective-permute-done.21.refs_14_.refs_12_), channel_id=1, source_target_pairs={{0,1},{1,0},{2,3},{3,2},{4,5},{5,4},{6,7},{7,6},{8,9},{9,8},{10,11... | collective-permute-start | bytes 1105928 | tf_op jit(solution)/shard_map/ppermute | solution.py:674
  13.3 3.8 %collective-permute-start.6 = (bf16[16,240]{1,0:T(8,128)(2,1)S(1)}, bf16[16,240]{1,0:T(8,128)(2,1)S(1)}, u32[]{:S(2)}, u32[]{:S(2)}) collective-permute-start(bf16[16,240]{1,0:T(8,128)(2,1)S(1)} %get-tuple-element.37.refs_0_), channel_id=1, source_target_pairs={{0,2},{1,3},{2,0},{3,1},{4,6},{5,7},{6,4},{7,5},{8,10},{9,11},{10,... | collective-permute-start | bytes 23048 | tf_op jit(solution)/shard_map/ppermute | solution.py:671
  13.3 6.8 %collective-permute-start.7 = (bf16[16,240]{1,0:T(8,128)(2,1)S(1)}, bf16[16,240]{1,0:T(8,128)(2,1)S(1)}, u32[]{:S(2)}, u32[]{:S(2)}) collective-permute-start(bf16[16,240]{1,0:T(8,128)(2,1)S(1)} %get-tuple-element.37.refs_0_), channel_id=1, source_target_pairs={{0,4},{1,5},{2,6},{3,7},{4,0},{5,1},{6,2},{7,3},{8,12},{9,13},{10,... | collective-permute-start | bytes 23048 | tf_op jit(solution)/shard_map/ppermute | solution.py:671
  17.0 5.4 %collective-permute-start.8 = (bf16[16,240]{1,0:T(8,128)(2,1)S(1)}, bf16[16,240]{1,0:T(8,128)(2,1)S(1)}, u32[]{:S(2)}, u32[]{:S(2)}) collective-permute-start(bf16[16,240]{1,0:T(8,128)(2,1)S(1)} %get-tuple-element.37.refs_0_), channel_id=1, source_target_pairs={{0,6},{1,7},{2,4},{3,5},{4,2},{5,3},{6,0},{7,1},{8,14},{9,15},{10,... | collective-permute-start | bytes 23048 | tf_op jit(solution)/shard_map/ppermute | solution.py:671
  20.1 2.4 %collective-permute-start.9 = (bf16[16,240]{1,0:T(8,128)(2,1)S(1)}, bf16[16,240]{1,0:T(8,128)(2,1)S(1)}, u32[]{:S(2)}, u32[]{:S(2)}) collective-permute-start(bf16[16,240]{1,0:T(8,128)(2,1)S(1)} %get-tuple-element.37.refs_0_), channel_id=1, source_target_pairs={{0,1},{1,0},{2,3},{3,2},{4,5},{5,4},{6,7},{7,6},{8,9},{9,8},{10,11... | collective-permute-start | bytes 23048 | tf_op jit(solution)/shard_map/ppermute | solution.py:674
  22.5 1.2 collective-permute-start.10
  22.5 1.3 %collective-permute-start.11 = (bf16[16,240]{1,0:T(8,128)(2,1)S(1)}, bf16[16,240]{1,0:T(8,128)(2,1)S(1)}, u32[]{:S(2)}, u32[]{:S(2)}) collective-permute-start(bf16[16,240]{1,0:T(8,128)(2,1)S(1)} %collective-permute-done.7.refs_2_), channel_id=1, source_target_pairs={{0,1},{1,0},{2,3},{3,2},{4,5},{5,4},{6,7},{7,6},{8,9},{9,8},{10,11... | collective-permute-start | bytes 23048 | tf_op jit(solution)/shard_map/ppermute | solution.py:674
  23.6 1.2 collective-permute-start.12
  26.0 3.9 %collective-permute-start.13 = (f32[2,16,240]{2,1,0:T(8,128)S(1)}, f32[2,16,240]{2,1,0:T(8,128)S(1)}, u32[]{:S(2)}, u32[]{:S(2)}) collective-permute-start(f32[2,16,240]{2,1,0:T(8,128)S(1)} %get-tuple-element.39.refs_4_.refs_0_), channel_id=1, source_target_pairs={{0,2},{1,3},{2,0},{3,1},{4,6},{5,7},{6,4},{7,5},{8,10},{9,11},{10,... | collective-permute-start | bytes 92168 | tf_op jit(solution)/shard_map/ppermute | solution.py:671
  26.4 7.0 %collective-permute-start.14 = (f32[2,16,240]{2,1,0:T(8,128)S(1)}, f32[2,16,240]{2,1,0:T(8,128)S(1)}, u32[]{:S(2)}, u32[]{:S(2)}) collective-permute-start(f32[2,16,240]{2,1,0:T(8,128)S(1)} %get-tuple-element.39.refs_4_.refs_0_), channel_id=1, source_target_pairs={{0,4},{1,5},{2,6},{3,7},{4,0},{5,1},{6,2},{7,3},{8,12},{9,13},{10,... | collective-permute-start | bytes 92168 | tf_op jit(solution)/shard_map/ppermute | solution.py:671
  30.0 5.7 %collective-permute-start.15 = (f32[2,16,240]{2,1,0:T(8,128)S(1)}, f32[2,16,240]{2,1,0:T(8,128)S(1)}, u32[]{:S(2)}, u32[]{:S(2)}) collective-permute-start(f32[2,16,240]{2,1,0:T(8,128)S(1)} %get-tuple-element.39.refs_4_.refs_0_), channel_id=1, source_target_pairs={{0,6},{1,7},{2,4},{3,5},{4,2},{5,3},{6,0},{7,1},{8,14},{9,15},{10,... | collective-permute-start | bytes 92168 | tf_op jit(solution)/shard_map/ppermute | solution.py:671
  33.4 2.3 %collective-permute-start.16 = (f32[2,16,240]{2,1,0:T(8,128)S(1)}, f32[2,16,240]{2,1,0:T(8,128)S(1)}, u32[]{:S(2)}, u32[]{:S(2)}) collective-permute-start(f32[2,16,240]{2,1,0:T(8,128)S(1)} %get-tuple-element.39.refs_4_.refs_0_), channel_id=1, source_target_pairs={{0,1},{1,0},{2,3},{3,2},{4,5},{5,4},{6,7},{7,6},{8,9},{9,8},{10,11... | collective-permute-start | bytes 92168 | tf_op jit(solution)/shard_map/ppermute | solution.py:674
  35.7 8.0 %collective-permute-start.3 = (bf16[104,512]{1,0:T(8,128)(2,1)S(1)}, bf16[104,512]{1,0:T(8,128)(2,1)S(1)}, u32[]{:S(2)}, u32[]{:S(2)}) collective-permute-start(bf16[104,512]{1,0:T(8,128)(2,1)S(1)} %get-tuple-element.36.refs_0_), channel_id=1, source_target_pairs={{0,2},{1,3},{2,0},{3,1},{4,6},{5,7},{6,4},{7,5},{8,10},{9,11},{10,... | collective-permute-start | bytes 319496 | tf_op jit(solution)/shard_map/ppermute | solution.py:671
  35.7 1.2 collective-permute-start.17
  36.9 1.2 collective-permute-start.18
  38.1 1.2 collective-permute-start.19
  39.3 12.0 %collective-permute-start.4 = (bf16[104,512]{1,0:T(8,128)(2,1)S(1)}, bf16[104,512]{1,0:T(8,128)(2,1)S(1)}, u32[]{:S(2)}, u32[]{:S(2)}) collective-permute-start(bf16[104,512]{1,0:T(8,128)(2,1)S(1)} %get-tuple-element.36.refs_0_), channel_id=1, source_target_pairs={{0,4},{1,5},{2,6},{3,7},{4,0},{5,1},{6,2},{7,3},{8,12},{9,13},{10,... | collective-permute-start | bytes 319496 | tf_op jit(solution)/shard_map/ppermute | solution.py:671
  43.7 7.9 %collective-permute-start.5 = (bf16[104,512]{1,0:T(8,128)(2,1)S(1)}, bf16[104,512]{1,0:T(8,128)(2,1)S(1)}, u32[]{:S(2)}, u32[]{:S(2)}) collective-permute-start(bf16[104,512]{1,0:T(8,128)(2,1)S(1)} %get-tuple-element.36.refs_0_), channel_id=1, source_target_pairs={{0,6},{1,7},{2,4},{3,5},{4,2},{5,3},{6,0},{7,1},{8,14},{9,15},{10,... | collective-permute-start | bytes 319496 | tf_op jit(solution)/shard_map/ppermute | solution.py:671
  51.3 8.9 %collective-permute-start = (bf16[4,32,512]{2,1,0:T(8,128)(2,1)S(1)}, bf16[4,32,512]{2,1,0:T(8,128)(2,1)S(1)}, u32[]{:S(2)}, u32[]{:S(2)}) collective-permute-start(bf16[4,32,512]{2,1,0:T(8,128)(2,1)S(1)} %get-tuple-element.33), channel_id=1, source_target_pairs={{0,2},{1,3},{2,0},{3,1},{4,6},{5,7},{6,4},{7,5},{8,10},{9,11},{10,... | collective-permute-start | bytes 393224 | tf_op jit(solution)/shard_map/ppermute | solution.py:671
  51.6 13.4 %collective-permute-start.1 = (bf16[4,32,512]{2,1,0:T(8,128)(2,1)S(1)}, bf16[4,32,512]{2,1,0:T(8,128)(2,1)S(1)}, u32[]{:S(2)}, u32[]{:S(2)}) collective-permute-start(bf16[4,32,512]{2,1,0:T(8,128)(2,1)S(1)} %get-tuple-element.34), channel_id=1, source_target_pairs={{0,4},{1,5},{2,6},{3,7},{4,0},{5,1},{6,2},{7,3},{8,12},{9,13},{10,... | collective-permute-start | bytes 393224 | tf_op jit(solution)/shard_map/ppermute | solution.py:671
  55.0 16.2 %copy-start.2 = (f32[4096,32]{0,1:T(8,128)S(1)}, f32[4096,32]{0,1:T(8,128)}, u32[]{:S(2)}) copy-start(f32[4096,32]{0,1:T(8,128)} %param.18) | copy-start | bytes 1572868
  55.0 16.2 %copy-start.3 = (bf16[32,1920]{1,0:T(8,128)(2,1)S(1)}, bf16[32,1920]{1,0:T(8,128)(2,1)}, u32[]{:S(2)}) copy-start(bf16[32,1920]{1,0:T(8,128)(2,1)} %refs_3_.1) | copy-start | bytes 368644
  55.0 16.2 %copy-start.4 = (bf16[25,1920]{1,0:T(8,128)(2,1)S(1)}, bf16[25,1920]{1,0:T(8,128)(2,1)}, u32[]{:S(2)}) copy-start(bf16[25,1920]{1,0:T(8,128)(2,1)} %refs_4_.1) | copy-start | bytes 288004
  55.0 16.2 %copy-start.5 = (f32[128,128]{1,0:T(8,128)S(1)}, f32[128,128]{1,0:T(8,128)}, u32[]{:S(2)}) copy-start(f32[128,128]{1,0:T(8,128)} %constant.2.clone.refs_2_) | copy-start | bytes 196612
  55.0 16.2 %copy-start.6 = (s32[1,8,30]{2,1,0:T(8,128)S(1)}, s32[1,8,30]{2,1,0:T(8,128)}, u32[]{:S(2)}) copy-start(s32[1,8,30]{2,1,0:T(8,128)} %param.17) | copy-start | bytes 2884
  55.0 9.9 %collective-permute-start.2 = (bf16[4,32,512]{2,1,0:T(8,128)(2,1)S(1)}, bf16[4,32,512]{2,1,0:T(8,128)(2,1)S(1)}, u32[]{:S(2)}, u32[]{:S(2)}) collective-permute-start(bf16[4,32,512]{2,1,0:T(8,128)(2,1)S(1)} %get-tuple-element.35), channel_id=1, source_target_pairs={{0,6},{1,7},{2,4},{3,5},{4,2},{5,3},{6,0},{7,1},{8,14},{9,15},{10,... | collective-permute-start | bytes 393224 | tf_op jit(solution)/shard_map/ppermute | solution.py:671
  66.7 7.3 %collective-permute-start.23 = (bf16[104,512]{1,0:T(8,128)(2,1)S(1)}, bf16[104,512]{1,0:T(8,128)(2,1)S(1)}, u32[]{:S(2)}, u32[]{:S(2)}) collective-permute-start(bf16[104,512]{1,0:T(8,128)(2,1)S(1)} %shard_map.148.refs_0_), channel_id=1, source_target_pairs={{0,2},{1,3},{2,0},{3,1},{4,6},{5,7},{6,4},{7,5},{8,10},{9,11},{10,... | collective-permute-start | bytes 319496 | tf_op jit(solution)/shard_map/ppermute | solution.py:671
  68.8 9.9 %collective-permute-start.24 = (bf16[104,512]{1,0:T(8,128)(2,1)S(1)}, bf16[104,512]{1,0:T(8,128)(2,1)S(1)}, u32[]{:S(2)}, u32[]{:S(2)}) collective-permute-start(bf16[104,512]{1,0:T(8,128)(2,1)S(1)} %shard_map.148.refs_0_), channel_id=1, source_target_pairs={{0,4},{1,5},{2,6},{3,7},{4,0},{5,1},{6,2},{7,3},{8,12},{9,13},{10,... | collective-permute-start | bytes 319496 | tf_op jit(solution)/shard_map/ppermute | solution.py:671
  69.6 9.1 %collective-permute-start.25 = (bf16[104,512]{1,0:T(8,128)(2,1)S(1)}, bf16[104,512]{1,0:T(8,128)(2,1)S(1)}, u32[]{:S(2)}, u32[]{:S(2)}) collective-permute-start(bf16[104,512]{1,0:T(8,128)(2,1)S(1)} %shard_map.148.refs_0_), channel_id=1, source_target_pairs={{0,6},{1,7},{2,4},{3,5},{4,2},{5,3},{6,0},{7,1},{8,14},{9,15},{10,... | collective-permute-start | bytes 319496 | tf_op jit(solution)/shard_map/ppermute | solution.py:671
  71.2 1.9 %collective-permute-start.27 = (f32[16,240]{1,0:T(8,128)S(1)}, f32[16,240]{1,0:T(8,128)S(1)}, u32[]{:S(2)}, u32[]{:S(2)}) collective-permute-start(f32[16,240]{1,0:T(8,128)S(1)} %get-tuple-element.43.refs_8_), channel_id=1, source_target_pairs={{0,1},{1,0},{2,3},{3,2},{4,5},{5,4},{6,7},{7,6},{8,9},{9,8},{10,11... | collective-permute-start | bytes 46088 | tf_op jit(solution)/shard_map/ppermute | solution.py:674
  79.9 5.8 %collective-permute-start.31 = (bf16[104,480]{1,0:T(8,128)(2,1)S(1)}, bf16[104,480]{1,0:T(8,128)(2,1)S(1)}, u32[]{:S(2)}, u32[]{:S(2)}) collective-permute-start(bf16[104,480]{1,0:T(8,128)(2,1)S(1)} %get-tuple-element.49), channel_id=1, source_target_pairs={{0,8},{8,16},{16,24},{24,0},{1,9},{9,17},{17,25},{25,1},{2,10},{10... | collective-permute-start | bytes 299528 | tf_op jit(solution)/shard_map/ppermute | solution.py:819
  85.7 5.0 %collective-permute-start.32 = (bf16[104,480]{1,0:T(8,128)(2,1)S(1)}, bf16[104,480]{1,0:T(8,128)(2,1)S(1)}, u32[]{:S(2)}, u32[]{:S(2)}) collective-permute-start(bf16[104,480]{1,0:T(8,128)(2,1)S(1)} %collective-permute-done.31.refs_0_), channel_id=1, source_target_pairs={{0,2},{1,3},{2,0},{3,1},{4,6},{5,7},{6,4},{7,5},{8,10},{9,11},{10,... | collective-permute-start | bytes 299528 | tf_op jit(solution)/shard_map/ppermute | solution.py:671
  87.5 9.1 %collective-permute-start.33 = (bf16[104,480]{1,0:T(8,128)(2,1)S(1)}, bf16[104,480]{1,0:T(8,128)(2,1)S(1)}, u32[]{:S(2)}, u32[]{:S(2)}) collective-permute-start(bf16[104,480]{1,0:T(8,128)(2,1)S(1)} %collective-permute-done.31.refs_0_), channel_id=1, source_target_pairs={{0,4},{1,5},{2,6},{3,7},{4,0},{5,1},{6,2},{7,3},{8,12},{9,13},{10,... | collective-permute-start | bytes 299528 | tf_op jit(solution)/shard_map/ppermute | solution.py:671
  88.2 8.4 %collective-permute-start.34 = (bf16[104,480]{1,0:T(8,128)(2,1)S(1)}, bf16[104,480]{1,0:T(8,128)(2,1)S(1)}, u32[]{:S(2)}, u32[]{:S(2)}) collective-permute-start(bf16[104,480]{1,0:T(8,128)(2,1)S(1)} %collective-permute-done.31.refs_0_), channel_id=1, source_target_pairs={{0,6},{1,7},{2,4},{3,5},{4,2},{5,3},{6,0},{7,1},{8,14},{9,15},{10,... | collective-permute-start | bytes 299528 | tf_op jit(solution)/shard_map/ppermute | solution.py:671
  101.1 7.1 %collective-permute-start.35 = (bf16[104,512]{1,0:T(8,128)(2,1)S(1)}, bf16[104,512]{1,0:T(8,128)(2,1)S(1)}, u32[]{:S(2)}, u32[]{:S(2)}) collective-permute-start(bf16[104,512]{1,0:T(8,128)(2,1)S(1)} %get-tuple-element.52.refs_0_), channel_id=1, source_target_pairs={{0,2},{1,3},{2,0},{3,1},{4,6},{5,7},{6,4},{7,5},{8,10},{9,11},{10,... | collective-permute-start | bytes 319496 | tf_op jit(solution)/shard_map/ppermute | solution.py:671
  102.9 11.8 %collective-permute-start.36 = (bf16[104,512]{1,0:T(8,128)(2,1)S(1)}, bf16[104,512]{1,0:T(8,128)(2,1)S(1)}, u32[]{:S(2)}, u32[]{:S(2)}) collective-permute-start(bf16[104,512]{1,0:T(8,128)(2,1)S(1)} %get-tuple-element.52.refs_0_), channel_id=1, source_target_pairs={{0,4},{1,5},{2,6},{3,7},{4,0},{5,1},{6,2},{7,3},{8,12},{9,13},{10,... | collective-permute-start | bytes 319496 | tf_op jit(solution)/shard_map/ppermute | solution.py:671
  103.9 10.9 %collective-permute-start.37 = (bf16[104,512]{1,0:T(8,128)(2,1)S(1)}, bf16[104,512]{1,0:T(8,128)(2,1)S(1)}, u32[]{:S(2)}, u32[]{:S(2)}) collective-permute-start(bf16[104,512]{1,0:T(8,128)(2,1)S(1)} %get-tuple-element.52.refs_0_), channel_id=1, source_target_pairs={{0,6},{1,7},{2,4},{3,5},{4,2},{5,3},{6,0},{7,1},{8,14},{9,15},{10,... | collective-permute-start | bytes 319496 | tf_op jit(solution)/shard_map/ppermute | solution.py:671
  105.6 13.6 %collective-permute-start.28 = (bf16[25,480]{1,0:T(8,128)(2,1)S(1)}, bf16[25,480]{1,0:T(8,128)(2,1)S(1)}, u32[]{:S(2)}, u32[]{:S(2)}) collective-permute-start(bf16[25,480]{1,0:T(8,128)(2,1)S(1)} %get-tuple-element.46), channel_id=1, source_target_pairs={{0,2},{1,3},{2,0},{3,1},{4,6},{5,7},{6,4},{7,5},{8,10},{9,11},{10,... | collective-permute-start | bytes 72008 | tf_op jit(solution)/shard_map/ppermute | solution.py:671
  106.4 14.2 %collective-permute-start.29 = (bf16[25,480]{1,0:T(8,128)(2,1)S(1)}, bf16[25,480]{1,0:T(8,128)(2,1)S(1)}, u32[]{:S(2)}, u32[]{:S(2)}) collective-permute-start(bf16[25,480]{1,0:T(8,128)(2,1)S(1)} %get-tuple-element.47), channel_id=1, source_target_pairs={{0,4},{1,5},{2,6},{3,7},{4,0},{5,1},{6,2},{7,3},{8,12},{9,13},{10,... | collective-permute-start | bytes 72008 | tf_op jit(solution)/shard_map/ppermute | solution.py:671
  108.3 12.3 %collective-permute-start.30 = (bf16[25,480]{1,0:T(8,128)(2,1)S(1)}, bf16[25,480]{1,0:T(8,128)(2,1)S(1)}, u32[]{:S(2)}, u32[]{:S(2)}) collective-permute-start(bf16[25,480]{1,0:T(8,128)(2,1)S(1)} %get-tuple-element.48), channel_id=1, source_target_pairs={{0,6},{1,7},{2,4},{3,5},{4,2},{5,3},{6,0},{7,1},{8,14},{9,15},{10,... | collective-permute-start | bytes 72008 | tf_op jit(solution)/shard_map/ppermute | solution.py:671
  115.9 4.7 %collective-permute-start.38 = (bf16[25,480]{1,0:T(8,128)(2,1)S(1)}, bf16[25,480]{1,0:T(8,128)(2,1)S(1)}, u32[]{:S(2)}, u32[]{:S(2)}) collective-permute-start(bf16[25,480]{1,0:T(8,128)(2,1)S(1)} %get-tuple-element.56), channel_id=1, source_target_pairs={{0,2},{1,3},{2,0},{3,1},{4,6},{5,7},{6,4},{7,5},{8,10},{9,11},{10,... | collective-permute-start | bytes 72008 | tf_op jit(solution)/shard_map/ppermute | solution.py:671
  118.1 5.2 %collective-permute-start.39 = (bf16[25,480]{1,0:T(8,128)(2,1)S(1)}, bf16[25,480]{1,0:T(8,128)(2,1)S(1)}, u32[]{:S(2)}, u32[]{:S(2)}) collective-permute-start(bf16[25,480]{1,0:T(8,128)(2,1)S(1)} %get-tuple-element.57), channel_id=1, source_target_pairs={{0,4},{1,5},{2,6},{3,7},{4,0},{5,1},{6,2},{7,3},{8,12},{9,13},{10,... | collective-permute-start | bytes 72008 | tf_op jit(solution)/shard_map/ppermute | solution.py:671
  119.2 5.7 %collective-permute-start.40 = (bf16[25,480]{1,0:T(8,128)(2,1)S(1)}, bf16[25,480]{1,0:T(8,128)(2,1)S(1)}, u32[]{:S(2)}, u32[]{:S(2)}) collective-permute-start(bf16[25,480]{1,0:T(8,128)(2,1)S(1)} %get-tuple-element.58), channel_id=1, source_target_pairs={{0,6},{1,7},{2,4},{3,5},{4,2},{5,3},{6,0},{7,1},{8,14},{9,15},{10,... | collective-permute-start | bytes 72008 | tf_op jit(solution)/shard_map/ppermute | solution.py:671
  (1 other events, 4.2 us)
